TPU v7x, 512 devices: a whole 4x4x16 slice. The times are simulated.
512 devices in a mesh: exp: 64 (over y, z), ctx: 8 (over x, core).
Axes of the slice: x: 4, y: 4, z: 16, core: 2. Of those that a mesh axis runs over, the one named last changes fastest.
Arguments:
- inputs: bfloat16 [65536, 1024], P(('exp', 'ctx')), may hold values from -30 to 30
- selected: int32 [128, 128], P(None, 'ctx'), may hold values from 0 to 65535, as said below
- selection_gate: float32 [128, 128], P('exp', 'ctx'), may hold values from 0.1 to 1
- gate_weight: bfloat16 [128, 1024, 2048], P('exp', None, 'ctx'), may hold values from -0.1875 to 0.1875
- up_weight: bfloat16 [128, 1024, 2048], P('exp', None, 'ctx'), may hold values from -0.1875 to 0.1875
- down_weight: bfloat16 [128, 2048, 1024], P('exp', 'ctx'), may hold values from -0.125 to 0.125
- norm_gain: float32 [1024], replicated, may hold values from 0.5 to 1.5
- query_weight: bfloat16 [1024, 1024], P('exp'), may hold values from -1 to 1
- key_weight: bfloat16 [1024, 1024], P('exp'), may hold values from -1 to 1
- value_weight: bfloat16 [1024, 1024], P('exp'), may hold values from -0.1875 to 0.1875
- train_count: int32 [64], P('exp'), may hold values from 256 to 1023
Outputs:
- layer_out: bfloat16 [65536, 1024], P(('exp', 'ctx'))
- context: bfloat16 [65536, 1024], P(('exp', 'ctx'))
Inputs may be any that keep to these rules, and one draw needn't show every extreme that they name: `selected`: each expert's 128 entries are distinct rows. Entries c * 16 to (c + 1) * 16 - 1 of every expert name rows at positions c * 128 to (c + 1) * 128 - 1 of their tables. At most 2 entries of one expert name rows of one block of 128 rows, and in each group of 16 entries of each expert some block gives exactly 2.
All inputs are finite; a program needn't handle non-finite values.
Results may differ from a plain program's by a relative error of at most 0.017.
Values may be sent and summed in bfloat16 or wider, within the bound.
No kernel may reach another device: no remote copies, remote signals or barrier semaphores. Data moves between devices by JAX's collectives and lax.ppermute only.
A program may use at most 64 MiB of HBM per device.

v0:
```python
import jax
import jax.numpy as jnp
from jax import lax
from jax.sharding import PartitionSpec as P

HEADS = 16
HEAD_DIM = 64


EPSILON = 1e-06
MASKED = -1e30


def copy_for_each(shard, axis):
    copies = jnp.broadcast_to(shard, (lax.axis_size(axis), *shard.shape))
    return lax.all_to_all(copies, axis, split_axis=0, concat_axis=0, tiled=True)


def in_order(blocks, dim):
    shape = list(blocks.shape[1:])
    shape[dim] *= blocks.shape[0]
    return jnp.moveaxis(blocks, 0, dim).reshape(shape)


def collect(shard, axis, dim):
    blocks = copy_for_each(shard, axis)
    return in_order(blocks, dim)


def cut_along(shard, dim, count):
    shape = shard.shape
    blocks = shard.reshape(*shape[:dim], count, shape[dim] // count, *shape[dim + 1 :])
    return jnp.moveaxis(blocks, dim, 0)


def sent_and_summed(shard, axis, dim):
    blocks = cut_along(shard, dim, lax.axis_size(axis))
    arrived = lax.all_to_all(blocks, axis, split_axis=0, concat_axis=0, tiled=True)
    return arrived.astype(jnp.float32).sum(axis=0)


def side_by_side(arrays, axis, dim, along):
    ends, at = ([], 0)
    for a in arrays[:-1]:
        at += a.shape[along]
        ends.append(at)
    both = jnp.concatenate(arrays, axis=along)
    return tuple(jnp.split(lax.all_gather(both, axis, axis=dim, tiled=True), ends, axis=along))


def block_rank(block_ids):
    slot_count = block_ids.shape[1]
    earlier = jnp.arange(slot_count)[:, None] > jnp.arange(slot_count)[None, :]
    same_block = block_ids[:, :, None] == block_ids[:, None, :]
    return jnp.sum(jnp.where(same_block & earlier[None], 1, 0), axis=2).astype(jnp.int32)


def local(
    inputs,
    selected,
    selection_gate,
    gate_weight,
    up_weight,
    down_weight,
    norm_gain,
    query_weight,
    key_weight,
    value_weight,
    train_count,
):
    exp_count = lax.axis_size("exp")
    ctx_count = lax.axis_size("ctx")
    exp_index = lax.axis_index("exp")
    ctx_index = lax.axis_index("ctx")
    row_count, model_width = inputs.shape
    expert_local = gate_weight.shape[0]
    group_take = selected.shape[1]
    most_rows = max(2, (2 * group_take + exp_count - 1) // exp_count)
    block_ids = selected // row_count
    slot_rank = block_rank(block_ids)
    own_block = exp_index * ctx_count + ctx_index
    is_mine = block_ids == own_block
    local_row = selected - own_block * row_count
    rank_slots = jnp.arange(most_rows, dtype=jnp.int32)
    slot_hit = is_mine[:, None, :] & (slot_rank[:, None, :] == rank_slots[None, :, None])
    pick_row = jnp.sum(jnp.where(slot_hit, local_row[:, None, :], 0), axis=2)
    filled = jnp.any(slot_hit, axis=2).reshape(-1)
    picked = jnp.take(inputs, pick_row.reshape(-1), axis=0)
    outgoing = jnp.where(filled[:, None], picked, jnp.zeros_like(picked)).reshape(
        exp_count, -1, model_width
    )
    incoming = lax.all_to_all(outgoing, "exp", split_axis=0, concat_axis=0, tiled=True)
    my_blocks = lax.dynamic_slice_in_dim(block_ids, exp_index * expert_local, expert_local, 0)
    my_rank = lax.dynamic_slice_in_dim(slot_rank, exp_index * expert_local, expert_local, 0)
    my_source = my_blocks // ctx_count
    expert_slot = jnp.arange(expert_local, dtype=jnp.int32)[:, None]
    flat_index = (my_source * expert_local + expert_slot) * most_rows + my_rank
    compact = jnp.take(incoming.reshape(-1, model_width), flat_index.T.reshape(-1), axis=0)
    compact = compact.reshape(group_take, expert_local, model_width)
    block_rows = collect(compact, "ctx", 0)
    gate_part = jnp.einsum(
        "nxd,xdf->nxf", block_rows, gate_weight, preferred_element_type=jnp.float32
    )
    up_part = jnp.einsum("nxd,xdf->nxf", block_rows, up_weight, preferred_element_type=jnp.float32)
    hidden = (jax.nn.silu(gate_part) * up_part).astype(jnp.bfloat16)
    summed = sent_and_summed(
        jnp.einsum("nxf,xfd->nxd", hidden, down_weight, preferred_element_type=jnp.float32).astype(
            jnp.bfloat16
        ),
        "ctx",
        0,
    )
    weighted = (summed * selection_gate.T[:, :, None]).astype(jnp.bfloat16)
    source_ids = jnp.arange(exp_count, dtype=jnp.int32)
    expert_ids = jnp.arange(expert_local, dtype=jnp.int32)[None, :, None, None]
    slot_index = jnp.arange(group_take, dtype=jnp.int32)[None, None, None, :]
    reply_hit = (my_source[None, :, None, :] == source_ids[:, None, None, None]) & (
        my_rank[None, :, None, :] == rank_slots[None, None, :, None]
    )
    reply_pick = jnp.sum(jnp.where(reply_hit, slot_index * expert_local + expert_ids, 0), axis=3)
    reply_filled = jnp.any(reply_hit, axis=3).reshape(-1)
    reply_rows = jnp.take(weighted.reshape(-1, model_width), reply_pick.reshape(-1), axis=0)
    reply_rows = jnp.where(reply_filled[:, None], reply_rows, jnp.zeros_like(reply_rows)).reshape(
        exp_count, -1, model_width
    )
    returned = lax.all_to_all(reply_rows, "exp", split_axis=0, concat_axis=0, tiled=True)
    owner_hit = (
        pick_row.reshape(-1)[None, :] == jnp.arange(row_count, dtype=jnp.int32)[:, None]
    ) & filled[None, :]
    moe_sum = jnp.dot(
        owner_hit.astype(jnp.bfloat16),
        returned.reshape(-1, model_width),
        preferred_element_type=jnp.float32,
    )
    layer_out = (inputs.astype(jnp.float32) + moe_sum).astype(jnp.bfloat16)
    widened = layer_out.astype(jnp.float32)
    scale_row = lax.rsqrt(jnp.mean(widened * widened, axis=1, keepdims=True) + EPSILON)
    normed = (widened * scale_row * norm_gain).astype(jnp.bfloat16)
    score_scale = HEAD_DIM ** (-0.5)
    train_rows = train_count[0]
    pieces = side_by_side((query_weight, key_weight, value_weight), "exp", 0, 1)
    projected = tuple(
        (jnp.dot(normed, piece_rows, preferred_element_type=jnp.float32) for piece_rows in pieces)
    )
    query_rows = projected[0].astype(jnp.bfloat16)
    key_rows = projected[1].astype(jnp.bfloat16)
    value_rows = projected[2].astype(jnp.bfloat16)
    query_heads = query_rows.reshape(row_count, HEADS, HEAD_DIM)
    top_score = jnp.full((HEADS, row_count), MASKED, jnp.float32)
    key_piece, value_piece = side_by_side((key_rows, value_rows), "ctx", 0, 1)
    piece_count = key_piece.shape[0]
    key_heads = key_piece.reshape(piece_count, HEADS, HEAD_DIM)
    value_heads = value_piece.reshape(piece_count, HEADS, HEAD_DIM)
    scores = (
        jnp.einsum("qhd,khd->hqk", query_heads, key_heads, preferred_element_type=jnp.float32)
        * score_scale
    )
    allowed = jnp.arange(piece_count, dtype=jnp.int32) < train_rows
    scores = jnp.where(allowed, scores, MASKED)
    new_top = jnp.maximum(top_score, jnp.max(scores, axis=2))
    weights = jnp.where(allowed, jnp.exp(scores - new_top[:, :, None]), 0.0)
    denominator = jnp.sum(weights, axis=2)
    accumulated = jnp.einsum(
        "hqk,khd->hqd",
        weights.astype(jnp.bfloat16),
        value_heads,
        preferred_element_type=jnp.float32,
    )
    blended = accumulated / denominator[:, :, None]
    context = jnp.transpose(blended, (1, 0, 2)).reshape(row_count, model_width).astype(jnp.bfloat16)
    return (layer_out, context)


def solution(mesh):
    placed = (
        P(("exp", "ctx"), None),
        P(None, "ctx"),
        P("exp", "ctx"),
        P("exp", None, "ctx"),
        P("exp", None, "ctx"),
        P("exp", "ctx", None),
        P(),
        P("exp", None),
        P("exp", None),
        P("exp", None),
        P("exp"),
    )
    return jax.shard_map(
        local,
        mesh=mesh,
        in_specs=placed,
        out_specs=(P(("exp", "ctx"), None), P(("exp", "ctx"), None)),
        check_vma=False,
    )
```

profile of v0, /device:TPU:1, one launch (start us, length us, event | category | flops | bytes accessed | tf_op | source)
XLA Modules:
  0.0 251.1 jit_solution(3562985261268316742)
XLA Ops:
  7.2 1.5 pad_maximum_fusion.1
  8.8 0.7 broadcast_compare_fusion
  9.5 0.1 select_reduce_fusion
  9.6 0.7 broadcast_subtract_fusion
  10.4 0.1 copy.70
  10.5 0.1 reshape.256
  10.7 0.1 copy.71
  10.9 0.1 broadcast_in_dim.127
  11.0 0.1 copy.81
  11.2 2.6 %gather_fusion = bf16[256,1024]{1,0:T(8,128)(2,1)S(1)} fusion(bf16[128,1024]{1,0:T(8,128)(2,1)} %param.11, s32[1024]{0:T(1024)S(1)} %pad_clamp_fusion.2), kind=kCustom, calls=%fused_computation | custom fusion | bytes 1049600 | tf_op jit(solution)/shard_map/jit(_take)/gather | solution.py:88
  13.8 0.2 gather.19
  14.0 1.3 select_select_fusion.1
  15.3 19.3 %all-to-all-start = ((bf16[64,4,1024]{2,1,0:T(4,128)(2,1)}), bf16[64,4,1024]{2,1,0:T(4,128)(2,1)S(1)}, u32[]{:S(2)}, u32[]{:S(2)}) async-start(bf16[64,4,1024]{2,1,0:T(4,128)(2,1)} %select_select_fusion.1), calls=%async_computation | async-start | bytes 1048576 | tf_op jit(solution)/shard_map/all_to_all | solution.py:92
  34.6 0.1 compare_and_fusion
  34.7 0.1 reshape.258
  35.0 33.9 %all-to-all-done = bf16[64,4,1024]{2,1,0:T(4,128)(2,1)S(1)} async-done(((bf16[64,4,1024]{2,1,0:T(4,128)(2,1)}), bf16[64,4,1024]{2,1,0:T(4,128)(2,1)S(1)}, u32[]{:S(2)}, u32[]{:S(2)}) %all-to-all-start) | async-done | bytes 524320 | tf_op jit(solution)/shard_map/all_to_all | solution.py:92
  68.9 0.1 reshape.257
  69.1 0.6 gather_fusion.1
  69.7 0.1 broadcast_select_fusion
  69.9 0.9 broadcast_in_dim.132
  70.7 7.0 %all-to-all-start.1 = ((bf16[8,16,2,1024]{3,1,2,0:T(8,128)(2,1)}), bf16[8,16,2,1024]{3,1,2,0:T(8,128)(2,1)S(1)}, u32[]{:S(2)}, u32[]{:S(2)}) async-start(bf16[8,16,2,1024]{3,1,2,0:T(8,128)(2,1)} %broadcast_in_dim.132), calls=%async_computation.1 | async-start | bytes 1048576 | tf_op jit(solution)/shard_map/all_to_all | solution.py:16
  77.7 0.1 and_reduce_fusion
  77.8 0.1 copy.88
  77.9 0.7 mul.75
  78.5 0.5 broadcast_in_dim.121
  79.1 0.1 fusion.46
  79.2 0.1 copy.89
  79.3 0.5 copy-done.5
  79.8 7.3 %all-to-all-done.1 = bf16[8,16,2,1024]{3,1,2,0:T(8,128)(2,1)S(1)} async-done(((bf16[8,16,2,1024]{3,1,2,0:T(8,128)(2,1)}), bf16[8,16,2,1024]{3,1,2,0:T(8,128)(2,1)S(1)}, u32[]{:S(2)}, u32[]{:S(2)}) %all-to-all-start.1) | async-done | bytes 524320 | tf_op jit(solution)/shard_map/all_to_all | solution.py:16
  87.1 0.3 convolution_bitcast_fusion.1
  87.4 1.8 convolution_convert_fusion
  89.2 0.8 copy.85
  90.1 4.5 %all-to-all-start.2 = ((bf16[8,16,2,1024]{3,1,2,0:T(8,128)(2,1)}), bf16[8,16,2,1024]{3,1,2,0:T(8,128)(2,1)S(1)}, u32[]{:S(2)}, u32[]{:S(2)}) async-start(bf16[8,16,2,1024]{3,1,2,0:T(8,128)(2,1)} %copy.85), calls=%async_computation.2 | async-start | bytes 1048576 | tf_op jit(solution)/shard_map/all_to_all | solution.py:38
  94.6 0.7 compare_and_fusion.2
  95.3 0.1 copy.75
  95.4 0.7 copy.74
  96.1 0.1 reshape.261
  96.3 7.7 %all-to-all-done.2 = bf16[8,16,2,1024]{3,1,2,0:T(8,128)(2,1)S(1)} async-done(((bf16[8,16,2,1024]{3,1,2,0:T(8,128)(2,1)}), bf16[8,16,2,1024]{3,1,2,0:T(8,128)(2,1)S(1)}, u32[]{:S(2)}, u32[]{:S(2)}) %all-to-all-start.2) | async-done | bytes 524320 | tf_op jit(solution)/shard_map/all_to_all | solution.py:38
  104.1 0.1 copy.87
  104.2 0.1 reduce_sum.60
  104.4 1.2 gather_fusion.2
  105.5 0.2 gather.23
  105.7 1.3 select_select_fusion
  107.0 5.6 %all-to-all-start.3 = ((bf16[64,4,1024]{2,1,0:T(4,128)(2,1)}), bf16[64,4,1024]{2,1,0:T(4,128)(2,1)S(1)}, u32[]{:S(2)}, u32[]{:S(2)}) async-start(bf16[64,4,1024]{2,1,0:T(4,128)(2,1)} %select_select_fusion), calls=%async_computation.3 | async-start | bytes 1048576 | tf_op jit(solution)/shard_map/all_to_all | solution.py:126
  112.6 0.2 all-gather.5.cloned.1.call-start
  112.9 0.1 and.80
  113.0 0.1 eq.93
  113.2 34.6 %all-to-all-done.3 = bf16[64,4,1024]{2,1,0:T(4,128)(2,1)S(1)} async-done(((bf16[64,4,1024]{2,1,0:T(4,128)(2,1)}), bf16[64,4,1024]{2,1,0:T(4,128)(2,1)S(1)}, u32[]{:S(2)}, u32[]{:S(2)}) %all-to-all-start.3) | async-done | bytes 524320 | tf_op jit(solution)/shard_map/all_to_all | solution.py:126
  147.8 0.1 reshape.262
  147.9 0.3 fusion.33
  148.2 30.5 %all-gather.3.cloned.1.call-done = bf16[1024,3072]{1,0:T(8,128)(2,1)} async-done(((bf16[16,3072]{1,0:T(8,128)(2,1)}), bf16[1024,3072]{1,0:T(8,128)(2,1)}) %all-gather.3.cloned.1.call-update) | async-done | bytes 6291472 | tf_op jit(solution)/shard_map/all_gather | solution.py:48
  178.8 2.1 fusion.18
  180.9 2.1 fusion.21
  182.9 0.9 pad_maximum_fusion
  184.5 2.1 fusion.15
  186.6 0.2 copy.90
  186.7 39.3 %all-gather.5.cloned.1.call-done = bf16[1024,2048]{1,0:T(8,128)(2,1)} async-done(((bf16[128,2048]{1,0:T(8,128)(2,1)}), bf16[1024,2048]{1,0:T(8,128)(2,1)}) %all-gather.5.cloned.1.call-update) | async-done | bytes 4194320 | tf_op jit(solution)/shard_map/all_gather | solution.py:48
  226.0 4.6 %fusion.61 = (bf16[1024,1024]{1,0:T(8,128)(2,1)}, bf16[1024,1024]{1,0:T(8,128)(2,1)}) fusion(bf16[1024,2048]{1,0:T(8,128)(2,1)} %all-gather.5.cloned.1.call-done), kind=kLoop, calls=%fused_computation.102 | loop fusion | bytes 8388608 | tf_op jit(solution)/shard_map/split | solution.py:48
  230.7 2.9 %copy.91 = bf16[1024,1024]{0,1:T(8,128)(2,1)S(1)} copy(bf16[1024,1024]{1,0:T(8,128)(2,1)} %get-tuple-element.16) | data formatting | bytes 4194304 | tf_op jit(solution)/shard_map/split | solution.py:48
  233.5 3.9 %copy.92 = bf16[1024,1024]{0,1:T(8,128)(2,1)} copy(bf16[1024,1024]{1,0:T(8,128)(2,1)} %get-tuple-element.17) | data formatting | bytes 4194304 | tf_op jit(solution)/shard_map/split | solution.py:48
  237.5 1.4 fusion
  238.9 2.2 fusion.1
  241.1 2.3 fusion.30
  243.4 0.9 copy.93
  (46 shorter events, 0.9 us)
Async XLA Ops:
  7.2 80.3 %copy-start = (bf16[2,256,1024]{2,1,0:T(8,128)(2,1)S(1)}, bf16[2,256,1024]{2,1,0:T(8,128)(2,1)}, u32[]{:S(2)}) copy-start(bf16[2,256,1024]{2,1,0:T(8,128)(2,1)} %param.16) | copy-start | bytes 3145732
  7.2 70.6 %copy-start.7 = (f32[2,16]{1,0:T(2,128)S(1)}, f32[2,16]{1,0:T(2,128)}, u32[]{:S(2)}) copy-start(f32[2,16]{1,0:T(2,128)} %param.13) | copy-start | bytes 388
  7.2 171.6 %all-gather.3.cloned.1.call-start = ((), (), s32[]{:S(2)}) async-start(), calls=%async_computation.4 | async-start | bytes 6389760 | tf_op jit(solution)/shard_map/all_gather | solution.py:48
  11.2 75.9 %copy-start.3 = (bf16[2,1024,256]{2,1,0:T(8,128)(2,1)S(1)}, bf16[2,1024,256]{2,1,0:T(8,128)(2,1)}, u32[]{:S(2)}) copy-start(bf16[2,1024,256]{2,1,0:T(8,128)(2,1)} %param.14) | copy-start | bytes 3145732
  15.3 53.6 %all-to-all-start = ((bf16[64,4,1024]{2,1,0:T(4,128)(2,1)}), bf16[64,4,1024]{2,1,0:T(4,128)(2,1)S(1)}, u32[]{:S(2)}, u32[]{:S(2)}) async-start(bf16[64,4,1024]{2,1,0:T(4,128)(2,1)} %select_select_fusion.1), calls=%async_computation | async-start | bytes 1048576 | tf_op jit(solution)/shard_map/all_to_all | solution.py:92
  70.7 16.3 %all-to-all-start.1 = ((bf16[8,16,2,1024]{3,1,2,0:T(8,128)(2,1)}), bf16[8,16,2,1024]{3,1,2,0:T(8,128)(2,1)S(1)}, u32[]{:S(2)}, u32[]{:S(2)}) async-start(bf16[8,16,2,1024]{3,1,2,0:T(8,128)(2,1)} %broadcast_in_dim.132), calls=%async_computation.1 | async-start | bytes 1048576 | tf_op jit(solution)/shard_map/all_to_all | solution.py:16
  79.2 0.6 copy-start.5
  87.4 16.8 %copy-start.6 = (f32[32]{0:T(128)S(1)}, f32[32]{0:T(128)}, u32[]{:S(2)}) copy-start(f32[32]{0:T(128)} %mul.75) | copy-start | bytes 388
  89.2 58.7 %copy-start.1 = (bf16[128,1024]{1,0:T(8,128)(2,1)S(1)}, bf16[128,1024]{1,0:T(8,128)(2,1)}, u32[]{:S(2)}) copy-start(bf16[128,1024]{1,0:T(8,128)(2,1)} %param.11) | copy-start | bytes 786436
  90.1 88.7 %copy-start.8 = (f32[1024]{0:T(1024)S(1)}, f32[1024]{0:T(1024)}, u32[]{:S(2)}) copy-start(f32[1024]{0:T(1024)} %param.17) | copy-start | bytes 12292
  90.1 13.9 %all-to-all-start.2 = ((bf16[8,16,2,1024]{3,1,2,0:T(8,128)(2,1)}), bf16[8,16,2,1024]{3,1,2,0:T(8,128)(2,1)S(1)}, u32[]{:S(2)}, u32[]{:S(2)}) async-start(bf16[8,16,2,1024]{3,1,2,0:T(8,128)(2,1)} %copy.85), calls=%async_computation.2 | async-start | bytes 1048576 | tf_op jit(solution)/shard_map/all_to_all | solution.py:38
  107.0 40.8 %all-to-all-start.3 = ((bf16[64,4,1024]{2,1,0:T(4,128)(2,1)}), bf16[64,4,1024]{2,1,0:T(4,128)(2,1)S(1)}, u32[]{:S(2)}, u32[]{:S(2)}) async-start(bf16[64,4,1024]{2,1,0:T(4,128)(2,1)} %select_select_fusion), calls=%async_computation.3 | async-start | bytes 1048576 | tf_op jit(solution)/shard_map/all_to_all | solution.py:126
  112.6 113.4 %all-gather.5.cloned.1.call-start = ((), (), s32[]{:S(2)}) async-start(), calls=%async_computation.5 | async-start | bytes 4718592 | tf_op jit(solution)/shard_map/all_gather | solution.py:48
  148.2 82.4 %copy-start.4 = (bf16[128,1024]{1,0:T(8,128)(2,1)}, bf16[128,1024]{1,0:T(8,128)(2,1)S(1)}, u32[]{:S(2)}) copy-start(bf16[128,1024]{1,0:T(8,128)(2,1)S(1)} %get-tuple-element.19) | copy-start | bytes 786436
  238.9 2.2 copy-start.2
Sparse Core Ops, SparseCore 0:
  11.5 167.1 all-gather.2
  183.9 42.0 all-gather.4
where the time goes:
time: 252 us; the launch traced here: 251 us
  waiting for transfers between devices  153 us (61%)
  starting transfers between devices  36.6 us (15%)
  local copies, waits for them, and re-layouts  23.7 us (9%)
  between operations  15.1 us (6%)
  matrix products  12.3 us (5%)
  other arithmetic  10.1 us (4%)
    all_gather x2, waiting for transfers between devices, side_by_side(): lax.all_gather(both, axis, axis=dim, tiled=True)  69.8 us
    all_to_all x1, waiting for transfers between devices, local(): lax.all_to_all(reply_rows, 'exp', split_axis=0, concat_axis=0, tiled=True)  34.6 us
    all_to_all x1, waiting for transfers between devices, local(): lax.all_to_all(outgoing, 'exp', split_axis=0, concat_axis=0, tiled=True)  33.9 us
    all_to_all x1, starting transfers between devices, local(): lax.all_to_all(outgoing, 'exp', split_axis=0, concat_axis=0, tiled=True)  19.3 us
    split x3, local copies, waits for them, and re-layouts, side_by_side(): jnp.split(lax.all_gather(both, axis, axis=dim, tiled=True), ends, axis=al...  11.4 us
    all_to_all x1, waiting for transfers between devices, sent_and_summed(): lax.all_to_all(blocks, axis, split_axis=0, concat_axis=0, tiled=True)  7.68 us
    all_to_all x1, waiting for transfers between devices, copy_for_each(): return lax.all_to_all(copies, axis, split_axis=0, concat_axis=0, tiled=True)  7.27 us
    all_to_all x1, starting transfers between devices, copy_for_each(): return lax.all_to_all(copies, axis, split_axis=0, concat_axis=0, tiled=True)  6.95 us
  transfers between devices with their start and end apart: 6, of which 6 were waited for; matrix products, arithmetic and copies ran while one was open for 8% of the time, Pallas kernels for 0%

commit v1 on v0

v1 whole, which is shorter than its diff:
```python
import jax
import jax.numpy as jnp
from jax import lax
from jax.experimental import pallas as pl
from jax.experimental.pallas import tpu as pltpu
from jax.sharding import PartitionSpec as P

HEADS = 16
HEAD_DIM = 64
EPSILON = 1e-06
MASKED = -1e30
LOG2_E = 1.4426950408889634
MOST = 2

N_Z = 16
N_X, N_CORE = 4, 2

def exchange(blocks, axis):
    return lax.all_to_all(blocks, axis, split_axis=0, concat_axis=0, tiled=True)


def copies(shard, count):
    return jnp.broadcast_to(shard, (count, *shard.shape))


def shift(v, axis, move):
    count = lax.axis_size(axis)
    return lax.ppermute(v, axis, [(i, move(i)) for i in range(count)])


def shift_chip(v, step):
    return shift(v, "ctx", lambda i: (i // N_CORE + step) % N_X * N_CORE + i % N_CORE)


def swap_core(v):
    return shift(v, "ctx", lambda i: i ^ 1)


def gather_four(v, digit, stride):
    def move(step):
        return lambda i: i + ((i // stride + step) % 4 - i // stride % 4) * stride

    one, two, three = (shift(v, "exp", move(step)) for step in (1, 2, 3))
    turned = jnp.stack([three, two, one, v, three, two, one])
    return lax.dynamic_slice_in_dim(turned, 3 - digit, 4, 0)


def attention_kernel(ids, train, near, far, out, queries, keys, values, bias):
    chunks, rows = near.shape[0] // 128 * 2, 128
    half = chunks // 2
    width = 2 * HEAD_DIM
    lane = lax.broadcasted_iota(jnp.int32, (rows, width), 1)
    first = lane < HEAD_DIM
    for j in range(chunks):
        source = near if j < half else far
        at = (j % half) * rows
        queries[j] = source[pl.ds(at, rows), 0:width]
        keys[pl.ds(j * rows, rows), :] = source[pl.ds(at, rows), width : 2 * width]
        values[pl.ds(j * rows, rows), :] = source[pl.ds(at, rows), 2 * width : 3 * width]
        position = ids[j] * rows + lax.broadcasted_iota(jnp.int32, (1, rows), 1)
        bias[:, j * rows : (j + 1) * rows] = jnp.where(position < train[0], 0.0, MASKED)

    def one_chunk(j, carry):
        q = queries[j]
        zero = jnp.zeros_like(q)
        parts = []
        for h in range(2):
            q_h = jnp.where(first, q, zero) if h == 0 else jnp.where(first, zero, q)
            scores = lax.dot_general(
                q_h, keys[...], (((1,), (1,)), ((), ())), preferred_element_type=jnp.float32
            )
            scores = scores * (LOG2_E * HEAD_DIM**-0.5) + bias[...]
            top = jnp.max(scores, axis=1, keepdims=True)
            weights = jnp.exp2(scores - top)
            total = jnp.sum(weights, axis=1, keepdims=True)
            mixed = jnp.dot(
                weights.astype(jnp.bfloat16), values[...], preferred_element_type=jnp.float32
            )
            parts.append(mixed / total)
        out[ids[j]] = jnp.where(first, parts[0], parts[1]).astype(jnp.bfloat16)
        return carry

    lax.fori_loop(0, chunks, one_chunk, 0)


def attention(ids, train, near, far):
    chunks = ids.shape[0]
    rows, width = 128, 2 * HEAD_DIM
    vmem = pl.BlockSpec(memory_space=pltpu.VMEM)
    smem = pl.BlockSpec(memory_space=pltpu.SMEM)
    return pl.pallas_call(
        attention_kernel,
        out_shape=jax.ShapeDtypeStruct((chunks, rows, width), jnp.bfloat16),
        in_specs=[smem, smem, vmem, vmem],
        out_specs=vmem,
        scratch_shapes=[
            pltpu.VMEM((chunks, rows, width), jnp.bfloat16),
            pltpu.VMEM((chunks * rows, width), jnp.bfloat16),
            pltpu.VMEM((chunks * rows, width), jnp.bfloat16),
            pltpu.VMEM((1, chunks * rows), jnp.float32),
        ],
        name="attention",
    )(ids, train, near, far)


def local(
    inputs,
    selected,
    selection_gate,
    gate_weight,
    up_weight,
    down_weight,
    norm_gain,
    query_weight,
    key_weight,
    value_weight,
    train_count,
):
    exp_count = lax.axis_size("exp")
    ctx_count = lax.axis_size("ctx")
    exp_index = lax.axis_index("exp")
    ctx_index = lax.axis_index("ctx")
    row_count, model_width = inputs.shape
    experts = gate_weight.shape[0]
    group_take = selected.shape[1]
    table_rows = row_count * ctx_count
    head_width = model_width // ctx_count

    piece = jnp.concatenate(
        [
            lax.dynamic_slice_in_dim(w, ctx_index * head_width, head_width, 1)
            for w in (query_weight, key_weight, value_weight)
        ],
        axis=1,
    )
    own_block = exp_index * ctx_count + ctx_index
    taken = selected.reshape(exp_count, experts, group_take) - own_block * row_count
    mine = (taken >= 0) & (taken < row_count)
    lower = jnp.min(jnp.where(mine, taken, row_count), axis=2)
    upper = jnp.max(jnp.where(mine, taken, -1), axis=2)
    upper = jnp.where(upper > lower, upper, -1)
    picks = jnp.stack([lower, upper], axis=2)
    row_ids = jnp.arange(row_count, dtype=jnp.int32)
    owner_hit = (picks.reshape(-1, 1) == row_ids).astype(jnp.bfloat16)
    outgoing = jnp.dot(owner_hit, inputs, preferred_element_type=jnp.float32)
    outgoing = outgoing.astype(jnp.bfloat16).reshape(exp_count, -1, model_width)

    outgoing, piece = lax.optimization_barrier((outgoing, piece))
    quarter = gather_four(piece, exp_index // 4 % 4, 4)
    arrived = exchange(outgoing, "exp").reshape(-1, model_width)

    my_rows = lax.dynamic_slice_in_dim(selected, exp_index * experts, experts, 0)
    my_table = my_rows // table_rows
    lower_rows = (my_table[:, :, None] == my_table[:, None, :]) & (
        my_rows[:, None, :] < my_rows[:, :, None]
    )
    my_rank = jnp.sum(lower_rows.astype(jnp.int32), axis=2)
    expert_ids = jnp.arange(experts, dtype=jnp.int32)[:, None]
    my_place = ((my_table * experts + expert_ids) * MOST + my_rank).reshape(-1, 1)
    places = jnp.arange(exp_count * experts * MOST, dtype=jnp.int32)
    slot_hit = (my_place == places).astype(jnp.bfloat16)

    compact = jnp.dot(slot_hit, arrived, preferred_element_type=jnp.float32).astype(jnp.bfloat16)
    compact, quarter = lax.optimization_barrier((compact, quarter))
    layer = gather_four(quarter, exp_index % 4, 1)
    layer = jnp.moveaxis(layer, 0, 1)
    chosen = exchange(copies(compact, ctx_count), "ctx")
    chosen = chosen.reshape(ctx_count, experts, group_take, model_width)
    partials = []
    for x in range(experts):
        rows = chosen[:, x].reshape(-1, model_width)
        gate_part = jnp.dot(rows, gate_weight[x], preferred_element_type=jnp.float32)
        up_part = jnp.dot(rows, up_weight[x], preferred_element_type=jnp.float32)
        hidden = (jax.nn.silu(gate_part) * up_part).astype(jnp.bfloat16)
        partial = jnp.dot(hidden, down_weight[x], preferred_element_type=jnp.float32)
        partials.append(
            partial.astype(jnp.bfloat16).reshape(ctx_count, group_take, model_width)
        )
    parts = exchange(jnp.concatenate(partials, axis=1), "ctx")
    expert_out = jnp.sum(parts.astype(jnp.float32), axis=0)
    weighted = (expert_out * selection_gate.reshape(-1, 1)).astype(jnp.bfloat16)
    reply = lax.dot_general(
        slot_hit, weighted, (((0,), (0,)), ((), ())), preferred_element_type=jnp.float32
    )
    reply = reply.astype(jnp.bfloat16).reshape(exp_count, -1, model_width)
    reply, layer = lax.optimization_barrier((reply, layer))
    weight_rows = gather_four(layer, exp_index // N_Z, N_Z).reshape(model_width, -1)
    returned = exchange(reply, "exp").reshape(-1, model_width)
    moe_sum = lax.dot_general(
        owner_hit, returned, (((0,), (0,)), ((), ())), preferred_element_type=jnp.float32
    )

    layer_out = (inputs.astype(jnp.float32) + moe_sum).astype(jnp.bfloat16)
    widened = layer_out.astype(jnp.float32)
    scale_row = lax.rsqrt(jnp.mean(widened * widened, axis=1, keepdims=True) + EPSILON)
    normed = (widened * scale_row * norm_gain).astype(jnp.bfloat16)

    near = jnp.concatenate(
        [normed, shift_chip(normed, 1), shift_chip(normed, -1), shift_chip(normed, 2)], axis=0
    )
    far = swap_core(near)
    chip, core = ctx_index // N_CORE, ctx_index % N_CORE
    steps = jnp.array([0, N_X - 1, 1, 2], jnp.int32)
    chips = (chip + steps) % N_X
    ids = jnp.concatenate([chips * N_CORE + core, chips * N_CORE + 1 - core])
    near_rows = jnp.dot(near, weight_rows, preferred_element_type=jnp.float32)
    far_rows = jnp.dot(far, weight_rows, preferred_element_type=jnp.float32)
    mixed = attention(
        ids, train_count, near_rows.astype(jnp.bfloat16), far_rows.astype(jnp.bfloat16)
    )
    by_heads = exchange(mixed, "ctx")
    context = jnp.moveaxis(by_heads, 0, 1).reshape(row_count, model_width)
    return (layer_out, context)


def solution(mesh):
    placed = (
        P(("exp", "ctx"), None),
        P(None, "ctx"),
        P("exp", "ctx"),
        P("exp", None, "ctx"),
        P("exp", None, "ctx"),
        P("exp", "ctx", None),
        P(),
        P("exp", None),
        P("exp", None),
        P("exp", None),
        P("exp"),
    )
    return jax.shard_map(
        local,
        mesh=mesh,
        in_specs=placed,
        out_specs=(P(("exp", "ctx"), None), P(("exp", "ctx"), None)),
        check_vma=False,
    )
```

time: 252 us -> 202 us (0.80)
  waiting for transfers between devices: 153 us -> 72.9 us
  starting transfers between devices: 36.6 us -> 88.1 us
  local copies, waits for them, and re-layouts: 23.7 us -> 6.65 us
  between operations: 15.1 us -> 1.9 us
  blocking collectives: 0 us -> 10.2 us
  Pallas kernels: 0 us -> 8.94 us
  other arithmetic: 10.1 us -> 2.65 us
  matrix products: 12.3 us -> 9.15 us
    all_gather x2 -> x0, waiting for transfers between devices: 69.8 us -> none  [side_by_side(): lax.all_gather(both, axis, axis=dim, tiled=True)]
    ppermute x0 -> x13, starting transfers between devices: none -> 59.2 us  [shift(): return lax.ppermute(v, axis, [(i, move(i)) for i in range(count)])]
    all_to_all x4, waiting for transfers between devices: 83.4 us -> 60.4 us  [exchange(): return lax.all_to_all(blocks, axis, split_axis=0, concat_axis=0, tiled=True)]
    ppermute x0 -> x13, waiting for transfers between devices: none -> 12.5 us  [shift(): return lax.ppermute(v, axis, [(i, move(i)) for i in range(count)])]
    split x3 -> x0, local copies, waits for them, and re-layouts: 11.4 us -> none  [side_by_side(): jnp.split(lax.all_gather(both, axis, axis=dim, tiled=True), ends, axis=al...]
    all_to_all x0 -> x1, blocking collectives: none -> 10.2 us  [exchange(): return lax.all_to_all(blocks, axis, split_axis=0, concat_axis=0, tiled=True)]
    pallas_call x0 -> x1, Pallas kernels: none -> 8.94 us  [attention(): pl.pallas_call(attention_kernel, out_shape=jax.ShapeDtypeStruct((chunks,...]
    all_to_all x4, starting transfers between devices: 36.4 us -> 28.9 us  [exchange(): return lax.all_to_all(blocks, axis, split_axis=0, concat_axis=0, tiled=True)]
  transfers between devices with their start and end apart: 6 -> 17, of which waited for: 6 -> 9; matrix products, arithmetic and copies ran while one was open for 8% -> 2% of each run, Pallas kernels for 0% -> 0%
where the time goes in v1:
time: 202 us; the launch traced here: 200 us
  starting transfers between devices  88.1 us (44%)
  waiting for transfers between devices  72.9 us (36%)
  blocking collectives  10.2 us (5%)
  matrix products  9.15 us (5%)
  Pallas kernels  8.94 us (4%)
  local copies, waits for them, and re-layouts  6.65 us (3%)
  other arithmetic  2.65 us (1%)
    all_to_all x4, waiting for transfers between devices, exchange(): return lax.all_to_all(blocks, axis, split_axis=0, concat_axis=0, tiled=True)  60.4 us
    ppermute x13, starting transfers between devices, shift(): return lax.ppermute(v, axis, [(i, move(i)) for i in range(count)])  59.2 us
    all_to_all x4, starting transfers between devices, exchange(): return lax.all_to_all(blocks, axis, split_axis=0, concat_axis=0, tiled=True)  28.9 us
    ppermute x13, waiting for transfers between devices, shift(): return lax.ppermute(v, axis, [(i, move(i)) for i in range(count)])  12.5 us
    all_to_all x1, blocking collectives, exchange(): return lax.all_to_all(blocks, axis, split_axis=0, concat_axis=0, tiled=True)  10.2 us
    pallas_call x1, Pallas kernels, attention(): pl.pallas_call(attention_kernel, out_shape=jax.ShapeDtypeStruct((chunks,...  8.94 us
  transfers between devices with their start and end apart: 17, of which 9 were waited for; matrix products, arithmetic and copies ran while one was open for 2% of the time, Pallas kernels for 0%

profile of v1, /device:TPU:1, one launch (start us, length us, event | category | flops | bytes accessed | tf_op | source)
XLA Modules:
  0.0 200.4 jit_solution(10887705953000014407)
XLA Ops:
  0.6 0.0 copy-start
  0.7 0.7 select_reduce_fusion.1
  1.4 0.1 reduce_max.12
  1.5 0.1 stack.61
  1.7 0.5 copy.47
  2.2 0.1 eq.49
  2.4 1.3 convolution_convert_fusion.1
  3.6 1.0 reshape.82
  4.6 0.7 constant_dynamic-slice_fusion.2
  5.4 13.4 %collective-permute-start = (bf16[16,384]{1,0:T(8,128)(2,1)S(1)}, bf16[16,384]{1,0:T(8,128)(2,1)S(1)}, u32[]{:S(2)}, u32[]{:S(2)}) collective-permute-start(bf16[16,384]{1,0:T(8,128)(2,1)S(1)} %pad_maximum_fusion.2), channel_id=1, source_target_pairs={{0,96},{8,104},{16,112},{24,120},{32,0},{40,8},{48,16},{56,24},{64... | collective-permute-start | bytes 36872 | tf_op jit(solution)/shard_map/ppermute | solution.py:28
  18.8 4.9 %collective-permute-start.1 = (bf16[16,384]{1,0:T(8,128)(2,1)S(1)}, bf16[16,384]{1,0:T(8,128)(2,1)S(1)}, u32[]{:S(2)}, u32[]{:S(2)}) collective-permute-start(bf16[16,384]{1,0:T(8,128)(2,1)S(1)} %pad_maximum_fusion.2), channel_id=1, source_target_pairs={{0,64},{8,72},{16,80},{24,88},{32,96},{40,104},{48,112},{56,120},{... | collective-permute-start | bytes 36872 | tf_op jit(solution)/shard_map/ppermute | solution.py:28
  23.7 7.3 %collective-permute-start.2 = (bf16[16,384]{1,0:T(8,128)(2,1)S(1)}, bf16[16,384]{1,0:T(8,128)(2,1)S(1)}, u32[]{:S(2)}, u32[]{:S(2)}) collective-permute-start(bf16[16,384]{1,0:T(8,128)(2,1)S(1)} %pad_maximum_fusion.2), channel_id=1, source_target_pairs={{0,32},{8,40},{16,48},{24,56},{32,64},{40,72},{48,80},{56,88},{64,... | collective-permute-start | bytes 36872 | tf_op jit(solution)/shard_map/ppermute | solution.py:28
  31.0 8.4 %all-to-all-start = ((bf16[64,4,1024]{2,1,0:T(4,128)(2,1)}), bf16[64,4,1024]{2,1,0:T(4,128)(2,1)S(1)}, u32[]{:S(2)}, u32[]{:S(2)}) async-start(bf16[64,4,1024]{2,1,0:T(4,128)(2,1)} %reshape.82), calls=%async_computation | async-start | bytes 1048576 | tf_op jit(solution)/shard_map/all_to_all | solution.py:19
  39.4 0.1 constant_dynamic-slice_fusion.5
  39.4 0.1 copy.56
  39.5 0.2 convert_reduce_fusion.1
  39.8 0.1 eq.56
  40.0 28.0 %all-to-all-done = bf16[64,4,1024]{2,1,0:T(4,128)(2,1)S(1)} async-done(((bf16[64,4,1024]{2,1,0:T(4,128)(2,1)}), bf16[64,4,1024]{2,1,0:T(4,128)(2,1)S(1)}, u32[]{:S(2)}, u32[]{:S(2)}) %all-to-all-start) | async-done | bytes 524320 | tf_op jit(solution)/shard_map/all_to_all | solution.py:19
  68.0 0.1 reshape.83
  68.1 0.2 convolution_convert_fusion.6
  68.3 4.1 %collective-permute-start.3 = (bf16[4,16,384]{2,1,0:T(8,128)(2,1)S(1)}, bf16[4,16,384]{2,1,0:T(8,128)(2,1)S(1)}, u32[]{:S(2)}, u32[]{:S(2)}) collective-permute-start(bf16[4,16,384]{2,1,0:T(8,128)(2,1)S(1)} %constant_dynamic-slice_fusion.1), channel_id=1, source_target_pairs={{0,24},{8,0},{16,8},{24,16},{32,56},{40,32},{48,40},{56,48},{64,88... | collective-permute-start | bytes 147464 | tf_op jit(solution)/shard_map/ppermute | solution.py:28
  72.5 0.1 mul.76
  72.6 3.7 %collective-permute-start.4 = (bf16[4,16,384]{2,1,0:T(8,128)(2,1)S(1)}, bf16[4,16,384]{2,1,0:T(8,128)(2,1)S(1)}, u32[]{:S(2)}, u32[]{:S(2)}) collective-permute-start(bf16[4,16,384]{2,1,0:T(8,128)(2,1)S(1)} %constant_dynamic-slice_fusion.1), channel_id=1, source_target_pairs={{0,16},{8,24},{16,0},{24,8},{32,48},{40,56},{48,32},{56,40},{64,80... | collective-permute-start | bytes 147464 | tf_op jit(solution)/shard_map/ppermute | solution.py:28
  76.3 1.9 collective-permute-start.5
  78.2 0.9 broadcast_in_dim.13
  79.1 7.9 %all-to-all-start.1 = ((bf16[8,32,1024]{2,1,0:T(8,128)(2,1)}), bf16[8,32,1024]{2,1,0:T(8,128)(2,1)S(1)}, u32[]{:S(2)}, u32[]{:S(2)}) async-start(bf16[8,32,1024]{2,1,0:T(8,128)(2,1)} %broadcast_in_dim.13), calls=%async_computation.1 | async-start | bytes 1048576 | tf_op jit(solution)/shard_map/all_to_all | solution.py:19
  87.1 9.2 %all-to-all-done.1 = bf16[8,32,1024]{2,1,0:T(8,128)(2,1)S(1)} async-done(((bf16[8,32,1024]{2,1,0:T(8,128)(2,1)}), bf16[8,32,1024]{2,1,0:T(8,128)(2,1)S(1)}, u32[]{:S(2)}, u32[]{:S(2)}) %all-to-all-start.1) | async-done | bytes 524320 | tf_op jit(solution)/shard_map/all_to_all | solution.py:19
  96.4 0.2 fusion.9
  96.7 0.2 fusion.14
  96.9 1.7 convolution_convert_fusion.4
  98.6 1.7 convolution_convert_fusion.5
  100.3 0.8 pad_maximum_fusion.1
  101.2 4.4 %all-to-all-start.2 = ((bf16[8,32,1024]{2,1,0:T(8,128)(2,1)}), bf16[8,32,1024]{2,1,0:T(8,128)(2,1)S(1)}, u32[]{:S(2)}, u32[]{:S(2)}) async-start(bf16[8,32,1024]{2,1,0:T(8,128)(2,1)} %pad_maximum_fusion.1), calls=%async_computation.2 | async-start | bytes 1048576 | tf_op jit(solution)/shard_map/all_to_all | solution.py:19
  105.6 9.3 %all-to-all-done.2 = bf16[8,32,1024]{2,1,0:T(8,128)(2,1)S(1)} async-done(((bf16[8,32,1024]{2,1,0:T(8,128)(2,1)}), bf16[8,32,1024]{2,1,0:T(8,128)(2,1)S(1)}, u32[]{:S(2)}, u32[]{:S(2)}) %all-to-all-start.2) | async-done | bytes 524320 | tf_op jit(solution)/shard_map/all_to_all | solution.py:19
  114.9 0.1 convert_reduce_fusion
  115.0 0.0 copy-start.6
  115.0 0.4 convolution_convert_fusion
  115.4 1.0 reshape.87
  116.4 8.2 %all-to-all-start.3 = ((bf16[64,4,1024]{2,1,0:T(4,128)(2,1)}), bf16[64,4,1024]{2,1,0:T(4,128)(2,1)S(1)}, u32[]{:S(2)}, u32[]{:S(2)}) async-start(bf16[64,4,1024]{2,1,0:T(4,128)(2,1)} %reshape.87), calls=%async_computation.3 | async-start | bytes 1048576 | tf_op jit(solution)/shard_map/all_to_all | solution.py:19
  124.7 4.3 %collective-permute-start.9 = (bf16[4,4,16,384]{3,2,1,0:T(8,128)(2,1)S(1)}, bf16[4,4,16,384]{3,2,1,0:T(8,128)(2,1)S(1)}, u32[]{:S(2)}, u32[]{:S(2)}) collective-permute-start(bf16[4,4,16,384]{3,2,1,0:T(8,128)(2,1)S(1)} %dynamic-slice_bitcast_fusion), channel_id=1, source_target_pairs={{0,384},{8,392},{16,400},{24,408},{32,416},{40,424},{48,432},{56,4... | collective-permute-start | bytes 589832 | tf_op jit(solution)/shard_map/ppermute | solution.py:28
  129.7 0.6 pad_add_fusion.1.ids
  130.2 2.4 %collective-permute-start.10 = (bf16[4,4,16,384]{3,2,1,0:T(8,128)(2,1)S(1)}, bf16[4,4,16,384]{3,2,1,0:T(8,128)(2,1)S(1)}, u32[]{:S(2)}, u32[]{:S(2)}) collective-permute-start(bf16[4,4,16,384]{3,2,1,0:T(8,128)(2,1)S(1)} %dynamic-slice_bitcast_fusion), channel_id=1, source_target_pairs={{0,256},{8,264},{16,272},{24,280},{32,288},{40,296},{48,304},{56,3... | collective-permute-start | bytes 589832 | tf_op jit(solution)/shard_map/ppermute | solution.py:28
  132.7 2.6 %collective-permute-start.11 = (bf16[4,4,16,384]{3,2,1,0:T(8,128)(2,1)S(1)}, bf16[4,4,16,384]{3,2,1,0:T(8,128)(2,1)S(1)}, u32[]{:S(2)}, u32[]{:S(2)}) collective-permute-start(bf16[4,4,16,384]{3,2,1,0:T(8,128)(2,1)S(1)} %dynamic-slice_bitcast_fusion), channel_id=1, source_target_pairs={{0,128},{8,136},{16,144},{24,152},{32,160},{40,168},{48,176},{56,1... | collective-permute-start | bytes 589832 | tf_op jit(solution)/shard_map/ppermute | solution.py:28
  135.3 4.8 %collective-permute-done.10 = bf16[4,4,16,384]{3,2,1,0:T(8,128)(2,1)S(1)} collective-permute-done((bf16[4,4,16,384]{3,2,1,0:T(8,128)(2,1)S(1)}, bf16[4,4,16,384]{3,2,1,0:T(8,128)(2,1)S(1)}, u32[]{:S(2)}, u32[]{:S(2)}) %collective-permute-start.10) | collective-permute-done | bytes 196640 | tf_op jit(solution)/shard_map/ppermute | solution.py:28
  140.1 13.9 %all-to-all-done.3 = bf16[64,4,1024]{2,1,0:T(4,128)(2,1)S(1)} async-done(((bf16[64,4,1024]{2,1,0:T(4,128)(2,1)}), bf16[64,4,1024]{2,1,0:T(4,128)(2,1)S(1)}, u32[]{:S(2)}, u32[]{:S(2)}) %all-to-all-start.3) | async-done | bytes 524320 | tf_op jit(solution)/shard_map/all_to_all | solution.py:19
  154.0 0.1 reshape.88
  154.1 0.4 fusion.3
  154.6 0.1 fusion.5
  154.7 2.5 %collective-permute-start.8 = (bf16[128,1024]{1,0:T(8,128)(2,1)S(1)}, bf16[128,1024]{1,0:T(8,128)(2,1)S(1)}, u32[]{:S(2)}, u32[]{:S(2)}) collective-permute-start(bf16[128,1024]{1,0:T(8,128)(2,1)S(1)} %fusion.5), channel_id=1, source_target_pairs={{0,4},{1,5},{2,6},{3,7},{4,0},{5,1},{6,2},{7,3},{8,12},{9,13},{10,... | collective-permute-start | bytes 786440 | tf_op jit(solution)/shard_map/ppermute | solution.py:28
  157.2 4.0 %collective-permute-start.7 = (bf16[128,1024]{1,0:T(8,128)(2,1)S(1)}, bf16[128,1024]{1,0:T(8,128)(2,1)S(1)}, u32[]{:S(2)}, u32[]{:S(2)}) collective-permute-start(bf16[128,1024]{1,0:T(8,128)(2,1)S(1)} %fusion.5), channel_id=1, source_target_pairs={{0,6},{1,7},{2,0},{3,1},{4,2},{5,3},{6,4},{7,5},{8,14},{9,15},{10,... | collective-permute-start | bytes 786440 | tf_op jit(solution)/shard_map/ppermute | solution.py:28
  161.2 1.9 collective-permute-start.6
  163.2 0.1 collective-permute-done.8
  163.3 4.5 %collective-permute-done.7 = bf16[128,1024]{1,0:T(8,128)(2,1)S(1)} collective-permute-done((bf16[128,1024]{1,0:T(8,128)(2,1)S(1)}, bf16[128,1024]{1,0:T(8,128)(2,1)S(1)}, u32[]{:S(2)}, u32[]{:S(2)}) %collective-permute-start.7) | collective-permute-done | bytes 262176 | tf_op jit(solution)/shard_map/ppermute | solution.py:28
  167.8 2.6 %collective-permute-done.6 = bf16[128,1024]{1,0:T(8,128)(2,1)S(1)} collective-permute-done((bf16[128,1024]{1,0:T(8,128)(2,1)S(1)}, bf16[128,1024]{1,0:T(8,128)(2,1)S(1)}, u32[]{:S(2)}, u32[]{:S(2)}) %collective-permute-start.6) | collective-permute-done | bytes 262176 | tf_op jit(solution)/shard_map/ppermute | solution.py:28
  170.4 0.1 pad_maximum_fusion
  170.4 6.1 %collective-permute-start.12 = (bf16[512,1024]{1,0:T(8,128)(2,1)S(1)}, bf16[512,1024]{1,0:T(8,128)(2,1)S(1)}, u32[]{:S(2)}, u32[]{:S(2)}) collective-permute-start(bf16[512,1024]{1,0:T(8,128)(2,1)S(1)} %pad_maximum_fusion), channel_id=1, source_target_pairs={{0,1},{1,0},{2,3},{3,2},{4,5},{5,4},{6,7},{7,6},{8,9},{9,8},{10,11... | collective-permute-start | bytes 3145736 | tf_op jit(solution)/shard_map/ppermute | solution.py:28
  176.7 0.1 constant_dynamic-slice_fusion
  176.8 1.5 convolution_convert_fusion.3.near
  178.2 0.6 collective-permute-done.12
  178.8 1.5 convolution_convert_fusion.2.far
  180.3 8.9 %attention.1 = bf16[8,128,128]{2,1,0:T(8,128)(2,1)} custom-call(s32[8]{0:T(128)} %pad_add_fusion.1.ids, s32[1]{0:T(128)S(6)} %copy.75.train, bf16[512,384]{1,0:T(8,128)(2,1)} %convolution_convert_fusion.3.near, bf16[512,384]{1,0:T(8,128)(2,1)} %convolution_convert_fusion.2.far), custom_call_target="tpu_custom_call" | custom-call | tf_op jit(solution)/shard_map/attention/pallas_call | solution.py:91
  189.2 10.2 %all_to_all.25 = bf16[8,128,128]{2,1,0:T(8,128)(2,1)S(1)} all-to-all(bf16[8,128,128]{2,1,0:T(8,128)(2,1)} %attention.1), channel_id=1, replica_groups=mesh['exp'=64,'ctx'=8] {'ctx'}, dimensions={0} | all-to-all | bytes 524288 | tf_op jit(solution)/shard_map/all_to_all | solution.py:19
  199.4 0.2 copy.54
  199.6 0.9 copy.55
  (55 shorter events, 0.6 us)
Async XLA Ops:
  0.6 4.0 %copy-start = (bf16[16,1024]{1,0:T(8,128)(2,1)S(1)}, bf16[16,1024]{1,0:T(8,128)(2,1)}, u32[]{:S(2)}) copy-start(bf16[16,1024]{1,0:T(8,128)(2,1)} %param.19) | copy-start | bytes 98308
  2.3 37.0 %copy-start.4 = (s32[128,16]{0,1:T(8,128)S(1)}, s32[128,16]{0,1:T(8,128)}, u32[]{:S(2)}) copy-start(s32[128,16]{0,1:T(8,128)} %param.13) | copy-start | bytes 24580
  5.4 67.1 %copy-start.7 = (f32[2,16]{1,0:T(2,128)S(1)}, f32[2,16]{1,0:T(2,128)}, u32[]{:S(2)}) copy-start(f32[2,16]{1,0:T(2,128)} %param.14) | copy-start | bytes 388
  5.4 34.5 %collective-permute-start = (bf16[16,384]{1,0:T(8,128)(2,1)S(1)}, bf16[16,384]{1,0:T(8,128)(2,1)S(1)}, u32[]{:S(2)}, u32[]{:S(2)}) collective-permute-start(bf16[16,384]{1,0:T(8,128)(2,1)S(1)} %pad_maximum_fusion.2), channel_id=1, source_target_pairs={{0,96},{8,104},{16,112},{24,120},{32,0},{40,8},{48,16},{56,24},{64... | collective-permute-start | bytes 36872 | tf_op jit(solution)/shard_map/ppermute | solution.py:28
  18.8 21.1 %collective-permute-start.1 = (bf16[16,384]{1,0:T(8,128)(2,1)S(1)}, bf16[16,384]{1,0:T(8,128)(2,1)S(1)}, u32[]{:S(2)}, u32[]{:S(2)}) collective-permute-start(bf16[16,384]{1,0:T(8,128)(2,1)S(1)} %pad_maximum_fusion.2), channel_id=1, source_target_pairs={{0,64},{8,72},{16,80},{24,88},{32,96},{40,104},{48,112},{56,120},{... | collective-permute-start | bytes 36872 | tf_op jit(solution)/shard_map/ppermute | solution.py:28
  23.7 16.2 %collective-permute-start.2 = (bf16[16,384]{1,0:T(8,128)(2,1)S(1)}, bf16[16,384]{1,0:T(8,128)(2,1)S(1)}, u32[]{:S(2)}, u32[]{:S(2)}) collective-permute-start(bf16[16,384]{1,0:T(8,128)(2,1)S(1)} %pad_maximum_fusion.2), channel_id=1, source_target_pairs={{0,32},{8,40},{16,48},{24,56},{32,64},{40,72},{48,80},{56,88},{64,... | collective-permute-start | bytes 36872 | tf_op jit(solution)/shard_map/ppermute | solution.py:28
  31.0 37.0 %all-to-all-start = ((bf16[64,4,1024]{2,1,0:T(4,128)(2,1)}), bf16[64,4,1024]{2,1,0:T(4,128)(2,1)S(1)}, u32[]{:S(2)}, u32[]{:S(2)}) async-start(bf16[64,4,1024]{2,1,0:T(4,128)(2,1)} %reshape.82), calls=%async_computation | async-start | bytes 1048576 | tf_op jit(solution)/shard_map/all_to_all | solution.py:19
  68.3 18.7 %collective-permute-start.3 = (bf16[4,16,384]{2,1,0:T(8,128)(2,1)S(1)}, bf16[4,16,384]{2,1,0:T(8,128)(2,1)S(1)}, u32[]{:S(2)}, u32[]{:S(2)}) collective-permute-start(bf16[4,16,384]{2,1,0:T(8,128)(2,1)S(1)} %constant_dynamic-slice_fusion.1), channel_id=1, source_target_pairs={{0,24},{8,0},{16,8},{24,16},{32,56},{40,32},{48,40},{56,48},{64,88... | collective-permute-start | bytes 147464 | tf_op jit(solution)/shard_map/ppermute | solution.py:28
  72.6 14.4 %collective-permute-start.4 = (bf16[4,16,384]{2,1,0:T(8,128)(2,1)S(1)}, bf16[4,16,384]{2,1,0:T(8,128)(2,1)S(1)}, u32[]{:S(2)}, u32[]{:S(2)}) collective-permute-start(bf16[4,16,384]{2,1,0:T(8,128)(2,1)S(1)} %constant_dynamic-slice_fusion.1), channel_id=1, source_target_pairs={{0,16},{8,24},{16,0},{24,8},{32,48},{40,56},{48,32},{56,40},{64,80... | collective-permute-start | bytes 147464 | tf_op jit(solution)/shard_map/ppermute | solution.py:28
  76.3 10.8 %collective-permute-start.5 = (bf16[4,16,384]{2,1,0:T(8,128)(2,1)S(1)}, bf16[4,16,384]{2,1,0:T(8,128)(2,1)S(1)}, u32[]{:S(2)}, u32[]{:S(2)}) collective-permute-start(bf16[4,16,384]{2,1,0:T(8,128)(2,1)S(1)} %constant_dynamic-slice_fusion.1), channel_id=1, source_target_pairs={{0,8},{8,16},{16,24},{24,0},{32,40},{40,48},{48,56},{56,32},{64,72... | collective-permute-start | bytes 147464 | tf_op jit(solution)/shard_map/ppermute | solution.py:28
  79.1 17.3 %copy-start.2 = (bf16[2,1024,256]{2,1,0:T(8,128)(2,1)S(1)}, bf16[2,1024,256]{2,1,0:T(8,128)(2,1)}, u32[]{:S(2)}) copy-start(bf16[2,1024,256]{2,1,0:T(8,128)(2,1)} %param.15) | copy-start | bytes 3145732
  79.1 17.3 %all-to-all-start.1 = ((bf16[8,32,1024]{2,1,0:T(8,128)(2,1)}), bf16[8,32,1024]{2,1,0:T(8,128)(2,1)S(1)}, u32[]{:S(2)}, u32[]{:S(2)}) async-start(bf16[8,32,1024]{2,1,0:T(8,128)(2,1)} %broadcast_in_dim.13), calls=%async_computation.1 | async-start | bytes 1048576 | tf_op jit(solution)/shard_map/all_to_all | solution.py:19
  101.2 13.7 %all-to-all-start.2 = ((bf16[8,32,1024]{2,1,0:T(8,128)(2,1)}), bf16[8,32,1024]{2,1,0:T(8,128)(2,1)S(1)}, u32[]{:S(2)}, u32[]{:S(2)}) async-start(bf16[8,32,1024]{2,1,0:T(8,128)(2,1)} %pad_maximum_fusion.1), calls=%async_computation.2 | async-start | bytes 1048576 | tf_op jit(solution)/shard_map/all_to_all | solution.py:19
  115.0 9.6 %copy-start.6 = (s32[4]{0:T(128)S(1)}, s32[4]{0:T(128)}, u32[]{:S(2)}) copy-start(s32[4]{0:T(128)} %constant.120.clone) | copy-start | bytes 52
  116.4 37.6 %copy-start.3 = (bf16[128,1024]{1,0:T(8,128)(2,1)S(1)}, bf16[128,1024]{1,0:T(8,128)(2,1)}, u32[]{:S(2)}) copy-start(bf16[128,1024]{1,0:T(8,128)(2,1)} %param.12) | copy-start | bytes 786436
  116.4 37.5 %all-to-all-start.3 = ((bf16[64,4,1024]{2,1,0:T(4,128)(2,1)}), bf16[64,4,1024]{2,1,0:T(4,128)(2,1)S(1)}, u32[]{:S(2)}, u32[]{:S(2)}) async-start(bf16[64,4,1024]{2,1,0:T(4,128)(2,1)} %reshape.87), calls=%async_computation.3 | async-start | bytes 1048576 | tf_op jit(solution)/shard_map/all_to_all | solution.py:19
  124.7 10.6 %collective-permute-start.9 = (bf16[4,4,16,384]{3,2,1,0:T(8,128)(2,1)S(1)}, bf16[4,4,16,384]{3,2,1,0:T(8,128)(2,1)S(1)}, u32[]{:S(2)}, u32[]{:S(2)}) collective-permute-start(bf16[4,4,16,384]{3,2,1,0:T(8,128)(2,1)S(1)} %dynamic-slice_bitcast_fusion), channel_id=1, source_target_pairs={{0,384},{8,392},{16,400},{24,408},{32,416},{40,424},{48,432},{56,4... | collective-permute-start | bytes 589832 | tf_op jit(solution)/shard_map/ppermute | solution.py:28
  130.2 24.3 %copy-start.5 = (f32[1024]{0:T(1024)S(1)}, f32[1024]{0:T(1024)}, u32[]{:S(2)}) copy-start(f32[1024]{0:T(1024)} %param.18) | copy-start | bytes 12292
  130.2 9.8 %collective-permute-start.10 = (bf16[4,4,16,384]{3,2,1,0:T(8,128)(2,1)S(1)}, bf16[4,4,16,384]{3,2,1,0:T(8,128)(2,1)S(1)}, u32[]{:S(2)}, u32[]{:S(2)}) collective-permute-start(bf16[4,4,16,384]{3,2,1,0:T(8,128)(2,1)S(1)} %dynamic-slice_bitcast_fusion), channel_id=1, source_target_pairs={{0,256},{8,264},{16,272},{24,280},{32,288},{40,296},{48,304},{56,3... | collective-permute-start | bytes 589832 | tf_op jit(solution)/shard_map/ppermute | solution.py:28
  132.7 30.5 %collective-permute-start.11 = (bf16[4,4,16,384]{3,2,1,0:T(8,128)(2,1)S(1)}, bf16[4,4,16,384]{3,2,1,0:T(8,128)(2,1)S(1)}, u32[]{:S(2)}, u32[]{:S(2)}) collective-permute-start(bf16[4,4,16,384]{3,2,1,0:T(8,128)(2,1)S(1)} %dynamic-slice_bitcast_fusion), channel_id=1, source_target_pairs={{0,128},{8,136},{16,144},{24,152},{32,160},{40,168},{48,176},{56,1... | collective-permute-start | bytes 589832 | tf_op jit(solution)/shard_map/ppermute | solution.py:28
  154.5 15.9 %copy-start.1 = (bf16[128,1024]{1,0:T(8,128)(2,1)}, bf16[128,1024]{1,0:T(8,128)(2,1)S(1)}, u32[]{:S(2)}) copy-start(bf16[128,1024]{1,0:T(8,128)(2,1)S(1)} %get-tuple-element.27) | copy-start | bytes 786436
  154.7 8.6 %collective-permute-start.8 = (bf16[128,1024]{1,0:T(8,128)(2,1)S(1)}, bf16[128,1024]{1,0:T(8,128)(2,1)S(1)}, u32[]{:S(2)}, u32[]{:S(2)}) collective-permute-start(bf16[128,1024]{1,0:T(8,128)(2,1)S(1)} %fusion.5), channel_id=1, source_target_pairs={{0,4},{1,5},{2,6},{3,7},{4,0},{5,1},{6,2},{7,3},{8,12},{9,13},{10,... | collective-permute-start | bytes 786440 | tf_op jit(solution)/shard_map/ppermute | solution.py:28
  157.2 10.6 %collective-permute-start.7 = (bf16[128,1024]{1,0:T(8,128)(2,1)S(1)}, bf16[128,1024]{1,0:T(8,128)(2,1)S(1)}, u32[]{:S(2)}, u32[]{:S(2)}) collective-permute-start(bf16[128,1024]{1,0:T(8,128)(2,1)S(1)} %fusion.5), channel_id=1, source_target_pairs={{0,6},{1,7},{2,0},{3,1},{4,2},{5,3},{6,4},{7,5},{8,14},{9,15},{10,... | collective-permute-start | bytes 786440 | tf_op jit(solution)/shard_map/ppermute | solution.py:28
  161.2 9.2 %collective-permute-start.6 = (bf16[128,1024]{1,0:T(8,128)(2,1)S(1)}, bf16[128,1024]{1,0:T(8,128)(2,1)S(1)}, u32[]{:S(2)}, u32[]{:S(2)}) collective-permute-start(bf16[128,1024]{1,0:T(8,128)(2,1)S(1)} %fusion.5), channel_id=1, source_target_pairs={{0,2},{1,3},{2,4},{3,5},{4,6},{5,7},{6,0},{7,1},{8,10},{9,11},{10,... | collective-permute-start | bytes 786440 | tf_op jit(solution)/shard_map/ppermute | solution.py:28
  170.4 8.4 %collective-permute-start.12 = (bf16[512,1024]{1,0:T(8,128)(2,1)S(1)}, bf16[512,1024]{1,0:T(8,128)(2,1)S(1)}, u32[]{:S(2)}, u32[]{:S(2)}) collective-permute-start(bf16[512,1024]{1,0:T(8,128)(2,1)S(1)} %pad_maximum_fusion), channel_id=1, source_target_pairs={{0,1},{1,0},{2,3},{3,2},{4,5},{5,4},{6,7},{7,6},{8,9},{9,8},{10,11... | collective-permute-start | bytes 3145736 | tf_op jit(solution)/shard_map/ppermute | solution.py:28

commit v2 on v1

--- a/solution.py
+++ b/solution.py
@@ -5,7 +5,7 @@
 from jax.experimental.pallas import tpu as pltpu
 from jax.sharding import PartitionSpec as P
 
-HEADS = 16
+
 HEAD_DIM = 64
 EPSILON = 1e-06
 MASKED = -1e30
@@ -15,6 +15,7 @@
 N_Z = 16
 N_X, N_CORE = 4, 2
 
+
 def exchange(blocks, axis):
     return lax.all_to_all(blocks, axis, split_axis=0, concat_axis=0, tiled=True)
 
@@ -40,47 +41,75 @@
     def move(step):
         return lambda i: i + ((i // stride + step) % 4 - i // stride % 4) * stride
 
-    one, two, three = (shift(v, "exp", move(step)) for step in (1, 2, 3))
+    others = []
+    for step in (1, 2, 3):
+        others.append(shift(v, "exp", move(step)))
+    one, two, three = others
     turned = jnp.stack([three, two, one, v, three, two, one])
     return lax.dynamic_slice_in_dim(turned, 3 - digit, 4, 0)
 
 
-def attention_kernel(ids, train, near, far, out, queries, keys, values, bias):
-    chunks, rows = near.shape[0] // 128 * 2, 128
-    half = chunks // 2
-    width = 2 * HEAD_DIM
+def expert_kernel(chosen, gate, up, down, out):
+    senders, _, width = chosen.shape
+    experts = gate.shape[0]
+    take = chosen.shape[1] // experts
+    for x in range(experts):
+        slots = slice(x * take, (x + 1) * take)
+        rows = chosen[:, slots, :].reshape(senders * take, width)
+        gate_part = jnp.dot(rows, gate[x], preferred_element_type=jnp.float32)
+        up_part = jnp.dot(rows, up[x], preferred_element_type=jnp.float32)
+        hidden = (gate_part / (1.0 + jnp.exp(-gate_part)) * up_part).astype(jnp.bfloat16)
+        partial = jnp.dot(hidden, down[x], preferred_element_type=jnp.float32)
+        out[:, slots, :] = partial.astype(jnp.bfloat16).reshape(senders, take, width)
+
+
+def expert_parts(chosen, gate, up, down):
+    vmem = pl.BlockSpec(memory_space=pltpu.VMEM)
+    return pl.pallas_call(
+        expert_kernel,
+        out_shape=jax.ShapeDtypeStruct(chosen.shape, chosen.dtype),
+        in_specs=[vmem] * 4,
+        out_specs=vmem,
+        compiler_params=pltpu.CompilerParams(vmem_limit_bytes=12 * 2**20),
+        name="experts",
+    )(chosen, gate, up, down)
+
+
+def attention_kernel(ids, train, near, far, out, queries, keys, values):
+    rows, width = 128, 2 * HEAD_DIM
+    half = near.shape[0] // rows
+    chunks = 2 * half
     lane = lax.broadcasted_iota(jnp.int32, (rows, width), 1)
     first = lane < HEAD_DIM
+    one_lane = jnp.where(lane == 0, 1.0, 0.0).astype(jnp.bfloat16)
     for j in range(chunks):
         source = near if j < half else far
         at = (j % half) * rows
-        queries[j] = source[pl.ds(at, rows), 0:width]
-        keys[pl.ds(j * rows, rows), :] = source[pl.ds(at, rows), width : 2 * width]
-        values[pl.ds(j * rows, rows), :] = source[pl.ds(at, rows), 2 * width : 3 * width]
-        position = ids[j] * rows + lax.broadcasted_iota(jnp.int32, (1, rows), 1)
-        bias[:, j * rows : (j + 1) * rows] = jnp.where(position < train[0], 0.0, MASKED)
-
-    def one_chunk(j, carry):
-        q = queries[j]
+        here = slice(j * rows, (j + 1) * rows)
+        low, high = slice(2 * j * rows, (2 * j + 1) * rows), slice((2 * j + 1) * rows, (2 * j + 2) * rows)
+        q = source[at : at + rows, 0:width]
         zero = jnp.zeros_like(q)
-        parts = []
-        for h in range(2):
-            q_h = jnp.where(first, q, zero) if h == 0 else jnp.where(first, zero, q)
-            scores = lax.dot_general(
-                q_h, keys[...], (((1,), (1,)), ((), ())), preferred_element_type=jnp.float32
-            )
-            scores = scores * (LOG2_E * HEAD_DIM**-0.5) + bias[...]
-            top = jnp.max(scores, axis=1, keepdims=True)
-            weights = jnp.exp2(scores - top)
-            total = jnp.sum(weights, axis=1, keepdims=True)
-            mixed = jnp.dot(
-                weights.astype(jnp.bfloat16), values[...], preferred_element_type=jnp.float32
-            )
-            parts.append(mixed / total)
-        out[ids[j]] = jnp.where(first, parts[0], parts[1]).astype(jnp.bfloat16)
-        return carry
-
-    lax.fori_loop(0, chunks, one_chunk, 0)
+        queries[low, 0:width] = jnp.where(first, q, zero)
+        queries[high, 0:width] = jnp.where(first, zero, q)
+        queries[low, width:] = one_lane
+        queries[high, width:] = one_lane
+        position = ids[j] * rows + lax.broadcasted_iota(jnp.int32, (rows, width), 0)
+        masked = (position >= train[0]) & (lane == 0)
+        keys[here, 0:width] = source[at : at + rows, width : 2 * width]
+        keys[here, width:] = jnp.where(masked, MASKED, 0.0).astype(jnp.bfloat16)
+        values[here, 0:width] = source[at : at + rows, 2 * width : 3 * width]
+        values[here, width:] = jnp.ones((rows, width), jnp.bfloat16)
+
+    for j in range(chunks):
+        q = queries[2 * j * rows : (2 * j + 2) * rows, :]
+        scores = lax.dot_general(
+            q, keys[...], (((1,), (1,)), ((), ())), preferred_element_type=jnp.float32
+        )
+        top = jnp.max(scores, axis=1, keepdims=True)
+        weights = jnp.exp2((scores - top) * (LOG2_E * HEAD_DIM**-0.5)).astype(jnp.bfloat16)
+        mixed = jnp.dot(weights, values[...], preferred_element_type=jnp.float32)
+        blended = mixed[:, :width] / mixed[:, width:]
+        out[ids[j]] = jnp.where(first, blended[:rows], blended[rows:]).astype(jnp.bfloat16)
 
 
 def attention(ids, train, near, far):
@@ -94,11 +123,11 @@
         in_specs=[smem, smem, vmem, vmem],
         out_specs=vmem,
         scratch_shapes=[
-            pltpu.VMEM((chunks, rows, width), jnp.bfloat16),
-            pltpu.VMEM((chunks * rows, width), jnp.bfloat16),
-            pltpu.VMEM((chunks * rows, width), jnp.bfloat16),
-            pltpu.VMEM((1, chunks * rows), jnp.float32),
+            pltpu.VMEM((2 * chunks * rows, 2 * width), jnp.bfloat16),
+            pltpu.VMEM((chunks * rows, 2 * width), jnp.bfloat16),
+            pltpu.VMEM((chunks * rows, 2 * width), jnp.bfloat16),
         ],
+        compiler_params=pltpu.CompilerParams(vmem_limit_bytes=20 * 2**20),
         name="attention",
     )(ids, train, near, far)
 
@@ -145,8 +174,6 @@
     outgoing = jnp.dot(owner_hit, inputs, preferred_element_type=jnp.float32)
     outgoing = outgoing.astype(jnp.bfloat16).reshape(exp_count, -1, model_width)
 
-    outgoing, piece = lax.optimization_barrier((outgoing, piece))
-    quarter = gather_four(piece, exp_index // 4 % 4, 4)
     arrived = exchange(outgoing, "exp").reshape(-1, model_width)
 
     my_rows = lax.dynamic_slice_in_dim(selected, exp_index * experts, experts, 0)
@@ -161,22 +188,13 @@
     slot_hit = (my_place == places).astype(jnp.bfloat16)
 
     compact = jnp.dot(slot_hit, arrived, preferred_element_type=jnp.float32).astype(jnp.bfloat16)
-    compact, quarter = lax.optimization_barrier((compact, quarter))
-    layer = gather_four(quarter, exp_index % 4, 1)
-    layer = jnp.moveaxis(layer, 0, 1)
+    compact, piece = lax.optimization_barrier((compact, piece))
+    quarter = gather_four(piece, exp_index // 4 % 4, 4)
     chosen = exchange(copies(compact, ctx_count), "ctx")
-    chosen = chosen.reshape(ctx_count, experts, group_take, model_width)
-    partials = []
-    for x in range(experts):
-        rows = chosen[:, x].reshape(-1, model_width)
-        gate_part = jnp.dot(rows, gate_weight[x], preferred_element_type=jnp.float32)
-        up_part = jnp.dot(rows, up_weight[x], preferred_element_type=jnp.float32)
-        hidden = (jax.nn.silu(gate_part) * up_part).astype(jnp.bfloat16)
-        partial = jnp.dot(hidden, down_weight[x], preferred_element_type=jnp.float32)
-        partials.append(
-            partial.astype(jnp.bfloat16).reshape(ctx_count, group_take, model_width)
-        )
-    parts = exchange(jnp.concatenate(partials, axis=1), "ctx")
+    partials = expert_parts(chosen, gate_weight, up_weight, down_weight)
+    partials, quarter = lax.optimization_barrier((partials, quarter))
+    layer = jnp.moveaxis(gather_four(quarter, exp_index % 4, 1), 0, 1)
+    parts = exchange(partials, "ctx")
     expert_out = jnp.sum(parts.astype(jnp.float32), axis=0)
     weighted = (expert_out * selection_gate.reshape(-1, 1)).astype(jnp.bfloat16)
     reply = lax.dot_general(
@@ -185,7 +203,8 @@
     reply = reply.astype(jnp.bfloat16).reshape(exp_count, -1, model_width)
     reply, layer = lax.optimization_barrier((reply, layer))
     weight_rows = gather_four(layer, exp_index // N_Z, N_Z).reshape(model_width, -1)
-    returned = exchange(reply, "exp").reshape(-1, model_width)
+    returned = exchange(reply, "exp")
+    returned = returned.reshape(-1, model_width)
     moe_sum = lax.dot_general(
         owner_hit, returned, (((0,), (0,)), ((), ())), preferred_element_type=jnp.float32
     )

time: 202 us -> 196 us (0.970)
  matrix products: 9.15 us -> 3.76 us
  Pallas kernels: 8.94 us -> 5.36 us
  starting transfers between devices: 88.1 us -> 91.4 us
    all_to_all x4, starting transfers between devices: 28.9 us -> 41.7 us  [exchange(): return lax.all_to_all(blocks, axis, split_axis=0, concat_axis=0, tiled=True)]
    ppermute x13, starting transfers between devices: 59.2 us -> 49.7 us  [shift(): return lax.ppermute(v, axis, [(i, move(i)) for i in range(count)])]
    pallas_call x1, Pallas kernels: 8.94 us -> 3.73 us  [attention(): pl.pallas_call(attention_kernel, out_shape=jax.ShapeDtypeStruct((chunks,...]
    dot_general x4 -> x0, matrix products: 3.89 us -> none  [the longest x2 3.42 us: local(): jnp.dot(hidden, down_weight[x], preferred_element_type=jnp.float32)]
where the time goes in v2:
time: 196 us; the launch traced here: 195 us
  starting transfers between devices  91.4 us (47%)
  waiting for transfers between devices  74.3 us (38%)
  blocking collectives  9.25 us (5%)
  local copies, waits for them, and re-layouts  7.82 us (4%)
  Pallas kernels  5.36 us (3%)
  matrix products  3.76 us (2%)
    all_to_all x4, waiting for transfers between devices, exchange(): return lax.all_to_all(blocks, axis, split_axis=0, concat_axis=0, tiled=True)  61.1 us
    ppermute x13, starting transfers between devices, shift(): return lax.ppermute(v, axis, [(i, move(i)) for i in range(count)])  49.7 us
    all_to_all x4, starting transfers between devices, exchange(): return lax.all_to_all(blocks, axis, split_axis=0, concat_axis=0, tiled=True)  41.7 us
    ppermute x13, waiting for transfers between devices, shift(): return lax.ppermute(v, axis, [(i, move(i)) for i in range(count)])  13.3 us
    all_to_all x1, blocking collectives, exchange(): return lax.all_to_all(blocks, axis, split_axis=0, concat_axis=0, tiled=True)  9.25 us
  transfers between devices with their start and end apart: 17, of which 9 were waited for; matrix products, arithmetic and copies ran while one was open for 2% of the time, Pallas kernels for 0%

profile of v2, /device:TPU:1, one launch (start us, length us, event | category | flops | bytes accessed | tf_op | source)
XLA Modules:
  0.0 195.1 jit_solution(1835535444153817464)
XLA Ops:
  0.6 0.0 copy-start
  0.7 0.7 select_reduce_fusion.1
  1.4 0.1 reduce_max.12
  1.5 0.1 stack.61
  1.7 0.5 copy.47
  2.2 0.1 eq.49
  2.3 0.0 copy-start.6
  2.3 1.3 convolution_convert_fusion.1
  3.6 1.0 reshape.73
  4.6 19.3 %all-to-all-start = ((bf16[64,4,1024]{2,1,0:T(4,128)(2,1)}), bf16[64,4,1024]{2,1,0:T(4,128)(2,1)S(1)}, u32[]{:S(2)}, u32[]{:S(2)}) async-start(bf16[64,4,1024]{2,1,0:T(4,128)(2,1)} %reshape.73), calls=%async_computation | async-start | bytes 1048576 | tf_op jit(solution)/shard_map/all_to_all | solution.py:20
  23.9 0.1 constant_dynamic-slice_fusion.5
  24.0 0.1 copy.56
  24.1 0.2 convert_reduce_fusion.1
  24.3 0.1 eq.56
  24.4 0.7 constant_dynamic-slice_fusion.2
  25.1 28.3 %all-to-all-done = bf16[64,4,1024]{2,1,0:T(4,128)(2,1)S(1)} async-done(((bf16[64,4,1024]{2,1,0:T(4,128)(2,1)}), bf16[64,4,1024]{2,1,0:T(4,128)(2,1)S(1)}, u32[]{:S(2)}, u32[]{:S(2)}) %all-to-all-start) | async-done | bytes 524320 | tf_op jit(solution)/shard_map/all_to_all | solution.py:20
  53.4 0.1 reshape.74
  53.6 0.0 copy-start.1
  53.6 0.0 copy-start.2
  53.6 0.2 convolution_convert_fusion.4
  53.8 4.9 %collective-permute-start = (bf16[16,384]{1,0:T(8,128)(2,1)S(1)}, bf16[16,384]{1,0:T(8,128)(2,1)S(1)}, u32[]{:S(2)}, u32[]{:S(2)}) collective-permute-start(bf16[16,384]{1,0:T(8,128)(2,1)S(1)} %pad_maximum_fusion.1), channel_id=1, source_target_pairs={{0,96},{8,104},{16,112},{24,120},{32,0},{40,8},{48,16},{56,24},{64... | collective-permute-start | bytes 36872 | tf_op jit(solution)/shard_map/ppermute | solution.py:29
  58.7 7.0 %collective-permute-start.1 = (bf16[16,384]{1,0:T(8,128)(2,1)S(1)}, bf16[16,384]{1,0:T(8,128)(2,1)S(1)}, u32[]{:S(2)}, u32[]{:S(2)}) collective-permute-start(bf16[16,384]{1,0:T(8,128)(2,1)S(1)} %pad_maximum_fusion.1), channel_id=1, source_target_pairs={{0,64},{8,72},{16,80},{24,88},{32,96},{40,104},{48,112},{56,120},{... | collective-permute-start | bytes 36872 | tf_op jit(solution)/shard_map/ppermute | solution.py:29
  65.8 4.6 %collective-permute-start.2 = (bf16[16,384]{1,0:T(8,128)(2,1)S(1)}, bf16[16,384]{1,0:T(8,128)(2,1)S(1)}, u32[]{:S(2)}, u32[]{:S(2)}) collective-permute-start(bf16[16,384]{1,0:T(8,128)(2,1)S(1)} %pad_maximum_fusion.1), channel_id=1, source_target_pairs={{0,32},{8,40},{16,48},{24,56},{32,64},{40,72},{48,80},{56,88},{64,... | collective-permute-start | bytes 36872 | tf_op jit(solution)/shard_map/ppermute | solution.py:29
  70.3 0.9 broadcast_in_dim.13
  71.2 6.6 %all-to-all-start.1 = ((bf16[8,32,1024]{2,1,0:T(8,128)(2,1)}), bf16[8,32,1024]{2,1,0:T(8,128)(2,1)S(1)}, u32[]{:S(2)}, u32[]{:S(2)}) async-start(bf16[8,32,1024]{2,1,0:T(8,128)(2,1)} %broadcast_in_dim.13), calls=%async_computation.1 | async-start | bytes 1048576 | tf_op jit(solution)/shard_map/all_to_all | solution.py:20
  77.9 9.2 %all-to-all-done.1.chosen = bf16[8,32,1024]{2,1,0:T(8,128)(2,1)S(1)} async-done(((bf16[8,32,1024]{2,1,0:T(8,128)(2,1)}), bf16[8,32,1024]{2,1,0:T(8,128)(2,1)S(1)}, u32[]{:S(2)}, u32[]{:S(2)}) %all-to-all-start.1) | async-done | bytes 524320 | tf_op jit(solution)/shard_map/all_to_all | solution.py:20
  87.1 1.2 copy-done.3
  88.3 1.6 experts.1
  90.0 4.9 %collective-permute-start.3 = (bf16[4,16,384]{2,1,0:T(8,128)(2,1)S(1)}, bf16[4,16,384]{2,1,0:T(8,128)(2,1)S(1)}, u32[]{:S(2)}, u32[]{:S(2)}) collective-permute-start(bf16[4,16,384]{2,1,0:T(8,128)(2,1)S(1)} %constant_dynamic-slice_fusion.1), channel_id=1, source_target_pairs={{0,24},{8,0},{16,8},{24,16},{32,56},{40,32},{48,40},{56,48},{64,88... | collective-permute-start | bytes 147464 | tf_op jit(solution)/shard_map/ppermute | solution.py:29
  94.9 0.1 mul.59
  95.0 1.9 collective-permute-start.4
  96.9 2.6 %collective-permute-start.5 = (bf16[4,16,384]{2,1,0:T(8,128)(2,1)S(1)}, bf16[4,16,384]{2,1,0:T(8,128)(2,1)S(1)}, u32[]{:S(2)}, u32[]{:S(2)}) collective-permute-start(bf16[4,16,384]{2,1,0:T(8,128)(2,1)S(1)} %constant_dynamic-slice_fusion.1), channel_id=1, source_target_pairs={{0,8},{8,16},{16,24},{24,0},{32,40},{40,48},{48,56},{56,32},{64,72... | collective-permute-start | bytes 147464 | tf_op jit(solution)/shard_map/ppermute | solution.py:29
  99.5 5.2 %all-to-all-start.2 = ((bf16[8,32,1024]{2,1,0:T(8,128)(2,1)}), bf16[8,32,1024]{2,1,0:T(8,128)(2,1)S(1)}, u32[]{:S(2)}, u32[]{:S(2)}) async-start(bf16[8,32,1024]{2,1,0:T(8,128)(2,1)} %experts.1), calls=%async_computation.2 | async-start | bytes 1048576 | tf_op jit(solution)/shard_map/all_to_all | solution.py:20
  104.9 9.2 %all-to-all-done.2 = bf16[8,32,1024]{2,1,0:T(8,128)(2,1)S(1)} async-done(((bf16[8,32,1024]{2,1,0:T(8,128)(2,1)}), bf16[8,32,1024]{2,1,0:T(8,128)(2,1)S(1)}, u32[]{:S(2)}, u32[]{:S(2)}) %all-to-all-start.2) | async-done | bytes 524320 | tf_op jit(solution)/shard_map/all_to_all | solution.py:20
  114.1 0.1 convert_reduce_fusion
  114.2 0.0 copy-start.8
  114.2 0.4 convolution_convert_fusion
  114.6 1.0 reshape.75
  115.6 10.6 %all-to-all-start.3 = ((bf16[64,4,1024]{2,1,0:T(4,128)(2,1)}), bf16[64,4,1024]{2,1,0:T(4,128)(2,1)S(1)}, u32[]{:S(2)}, u32[]{:S(2)}) async-start(bf16[64,4,1024]{2,1,0:T(4,128)(2,1)} %reshape.75), calls=%async_computation.3 | async-start | bytes 1048576 | tf_op jit(solution)/shard_map/all_to_all | solution.py:20
  126.2 4.3 %collective-permute-start.9 = (bf16[4,4,16,384]{3,2,1,0:T(8,128)(2,1)S(1)}, bf16[4,4,16,384]{3,2,1,0:T(8,128)(2,1)S(1)}, u32[]{:S(2)}, u32[]{:S(2)}) collective-permute-start(bf16[4,4,16,384]{3,2,1,0:T(8,128)(2,1)S(1)} %dynamic-slice_bitcast_fusion), channel_id=1, source_target_pairs={{0,384},{8,392},{16,400},{24,408},{32,416},{40,424},{48,432},{56,4... | collective-permute-start | bytes 589832 | tf_op jit(solution)/shard_map/ppermute | solution.py:29
  131.3 0.1 pad_add_fusion.1.ids
  131.3 2.4 %collective-permute-start.10 = (bf16[4,4,16,384]{3,2,1,0:T(8,128)(2,1)S(1)}, bf16[4,4,16,384]{3,2,1,0:T(8,128)(2,1)S(1)}, u32[]{:S(2)}, u32[]{:S(2)}) collective-permute-start(bf16[4,4,16,384]{3,2,1,0:T(8,128)(2,1)S(1)} %dynamic-slice_bitcast_fusion), channel_id=1, source_target_pairs={{0,256},{8,264},{16,272},{24,280},{32,288},{40,296},{48,304},{56,3... | collective-permute-start | bytes 589832 | tf_op jit(solution)/shard_map/ppermute | solution.py:29
  133.7 2.6 %collective-permute-start.11 = (bf16[4,4,16,384]{3,2,1,0:T(8,128)(2,1)S(1)}, bf16[4,4,16,384]{3,2,1,0:T(8,128)(2,1)S(1)}, u32[]{:S(2)}, u32[]{:S(2)}) collective-permute-start(bf16[4,4,16,384]{3,2,1,0:T(8,128)(2,1)S(1)} %dynamic-slice_bitcast_fusion), channel_id=1, source_target_pairs={{0,128},{8,136},{16,144},{24,152},{32,160},{40,168},{48,176},{56,1... | collective-permute-start | bytes 589832 | tf_op jit(solution)/shard_map/ppermute | solution.py:29
  136.4 4.8 %collective-permute-done.10 = bf16[4,4,16,384]{3,2,1,0:T(8,128)(2,1)S(1)} collective-permute-done((bf16[4,4,16,384]{3,2,1,0:T(8,128)(2,1)S(1)}, bf16[4,4,16,384]{3,2,1,0:T(8,128)(2,1)S(1)}, u32[]{:S(2)}, u32[]{:S(2)}) %collective-permute-start.10) | collective-permute-done | bytes 196640 | tf_op jit(solution)/shard_map/ppermute | solution.py:29
  141.2 14.3 %all-to-all-done.3 = bf16[64,4,1024]{2,1,0:T(4,128)(2,1)S(1)} async-done(((bf16[64,4,1024]{2,1,0:T(4,128)(2,1)}), bf16[64,4,1024]{2,1,0:T(4,128)(2,1)S(1)}, u32[]{:S(2)}, u32[]{:S(2)}) %all-to-all-start.3) | async-done | bytes 524320 | tf_op jit(solution)/shard_map/all_to_all | solution.py:20
  155.5 0.1 reshape.76
  155.6 0.4 fusion.1
  156.1 0.1 fusion.3
  156.2 2.5 %collective-permute-start.8 = (bf16[128,1024]{1,0:T(8,128)(2,1)S(1)}, bf16[128,1024]{1,0:T(8,128)(2,1)S(1)}, u32[]{:S(2)}, u32[]{:S(2)}) collective-permute-start(bf16[128,1024]{1,0:T(8,128)(2,1)S(1)} %fusion.3), channel_id=1, source_target_pairs={{0,4},{1,5},{2,6},{3,7},{4,0},{5,1},{6,2},{7,3},{8,12},{9,13},{10,... | collective-permute-start | bytes 786440 | tf_op jit(solution)/shard_map/ppermute | solution.py:29
  158.8 4.0 %collective-permute-start.7 = (bf16[128,1024]{1,0:T(8,128)(2,1)S(1)}, bf16[128,1024]{1,0:T(8,128)(2,1)S(1)}, u32[]{:S(2)}, u32[]{:S(2)}) collective-permute-start(bf16[128,1024]{1,0:T(8,128)(2,1)S(1)} %fusion.3), channel_id=1, source_target_pairs={{0,6},{1,7},{2,0},{3,1},{4,2},{5,3},{6,4},{7,5},{8,14},{9,15},{10,... | collective-permute-start | bytes 786440 | tf_op jit(solution)/shard_map/ppermute | solution.py:29
  162.8 1.9 collective-permute-start.6
  164.8 0.1 collective-permute-done.8
  164.9 4.5 %collective-permute-done.7 = bf16[128,1024]{1,0:T(8,128)(2,1)S(1)} collective-permute-done((bf16[128,1024]{1,0:T(8,128)(2,1)S(1)}, bf16[128,1024]{1,0:T(8,128)(2,1)S(1)}, u32[]{:S(2)}, u32[]{:S(2)}) %collective-permute-start.7) | collective-permute-done | bytes 262176 | tf_op jit(solution)/shard_map/ppermute | solution.py:29
  169.3 2.6 %collective-permute-done.6 = bf16[128,1024]{1,0:T(8,128)(2,1)S(1)} collective-permute-done((bf16[128,1024]{1,0:T(8,128)(2,1)S(1)}, bf16[128,1024]{1,0:T(8,128)(2,1)S(1)}, u32[]{:S(2)}, u32[]{:S(2)}) %collective-permute-start.6) | collective-permute-done | bytes 262176 | tf_op jit(solution)/shard_map/ppermute | solution.py:29
  171.9 0.1 pad_maximum_fusion
  172.0 6.1 %collective-permute-start.12 = (bf16[512,1024]{1,0:T(8,128)(2,1)S(1)}, bf16[512,1024]{1,0:T(8,128)(2,1)S(1)}, u32[]{:S(2)}, u32[]{:S(2)}) collective-permute-start(bf16[512,1024]{1,0:T(8,128)(2,1)S(1)} %pad_maximum_fusion), channel_id=1, source_target_pairs={{0,1},{1,0},{2,3},{3,2},{4,5},{5,4},{6,7},{7,6},{8,9},{9,8},{10,11... | collective-permute-start | bytes 3145736 | tf_op jit(solution)/shard_map/ppermute | solution.py:29
  178.2 0.1 constant_dynamic-slice_fusion
  178.3 0.7 convolution_convert_fusion.3.near
  179.1 1.3 collective-permute-done.12
  180.4 0.7 convolution_convert_fusion.2.far
  181.1 3.7 %attention.1 = bf16[8,128,128]{2,1,0:T(8,128)(2,1)S(1)} custom-call(s32[8]{0:T(128)S(1)} %pad_add_fusion.1.ids, s32[1]{0:T(128)S(6)} %copy.75.train, bf16[512,384]{1,0:T(8,128)(2,1)S(1)} %convolution_convert_fusion.3.near, bf16[512,384]{1,0:T(8,128)(2,1)S(1)} %convolution_convert_fusion.2.far), custom_call_target="tpu_custom_call" | custom-call | tf_op jit(solution)/shard_map/attention/pallas_call | solution.py:120
  184.8 9.2 %all_to_all.25 = bf16[8,128,128]{2,1,0:T(8,128)(2,1)S(1)} all-to-all(bf16[8,128,128]{2,1,0:T(8,128)(2,1)S(1)} %attention.1), channel_id=1, replica_groups=mesh['exp'=64,'ctx'=8] {'ctx'}, dimensions={0} | all-to-all | bytes 524288 | tf_op jit(solution)/shard_map/all_to_all | solution.py:20
  194.1 0.2 copy.54
  194.3 0.9 copy.55
  (54 shorter events, 0.5 us)
Async XLA Ops:
  0.6 23.8 %copy-start = (bf16[16,1024]{1,0:T(8,128)(2,1)S(1)}, bf16[16,1024]{1,0:T(8,128)(2,1)}, u32[]{:S(2)}) copy-start(bf16[16,1024]{1,0:T(8,128)(2,1)} %param.19) | copy-start | bytes 98308
  2.3 21.6 %copy-start.6 = (s32[128,16]{0,1:T(8,128)S(1)}, s32[128,16]{0,1:T(8,128)}, u32[]{:S(2)}) copy-start(s32[128,16]{0,1:T(8,128)} %param.13) | copy-start | bytes 24580
  4.6 48.8 %all-to-all-start = ((bf16[64,4,1024]{2,1,0:T(4,128)(2,1)}), bf16[64,4,1024]{2,1,0:T(4,128)(2,1)S(1)}, u32[]{:S(2)}, u32[]{:S(2)}) async-start(bf16[64,4,1024]{2,1,0:T(4,128)(2,1)} %reshape.73), calls=%async_computation | async-start | bytes 1048576 | tf_op jit(solution)/shard_map/all_to_all | solution.py:20
  53.6 33.6 %copy-start.1 = (bf16[2,1024,256]{2,1,0:T(8,128)(2,1)S(1)}, bf16[2,1024,256]{2,1,0:T(8,128)(2,1)}, u32[]{:S(2)}) copy-start(bf16[2,1024,256]{2,1,0:T(8,128)(2,1)} %gate.1) | copy-start | bytes 3145732
  53.6 33.5 %copy-start.2 = (bf16[2,1024,256]{2,1,0:T(8,128)(2,1)S(1)}, bf16[2,1024,256]{2,1,0:T(8,128)(2,1)}, u32[]{:S(2)}) copy-start(bf16[2,1024,256]{2,1,0:T(8,128)(2,1)} %up.1) | copy-start | bytes 3145732
  53.8 24.0 %collective-permute-start = (bf16[16,384]{1,0:T(8,128)(2,1)S(1)}, bf16[16,384]{1,0:T(8,128)(2,1)S(1)}, u32[]{:S(2)}, u32[]{:S(2)}) collective-permute-start(bf16[16,384]{1,0:T(8,128)(2,1)S(1)} %pad_maximum_fusion.1), channel_id=1, source_target_pairs={{0,96},{8,104},{16,112},{24,120},{32,0},{40,8},{48,16},{56,24},{64... | collective-permute-start | bytes 36872 | tf_op jit(solution)/shard_map/ppermute | solution.py:29
  58.7 19.1 %collective-permute-start.1 = (bf16[16,384]{1,0:T(8,128)(2,1)S(1)}, bf16[16,384]{1,0:T(8,128)(2,1)S(1)}, u32[]{:S(2)}, u32[]{:S(2)}) collective-permute-start(bf16[16,384]{1,0:T(8,128)(2,1)S(1)} %pad_maximum_fusion.1), channel_id=1, source_target_pairs={{0,64},{8,72},{16,80},{24,88},{32,96},{40,104},{48,112},{56,120},{... | collective-permute-start | bytes 36872 | tf_op jit(solution)/shard_map/ppermute | solution.py:29
  65.8 12.0 %collective-permute-start.2 = (bf16[16,384]{1,0:T(8,128)(2,1)S(1)}, bf16[16,384]{1,0:T(8,128)(2,1)S(1)}, u32[]{:S(2)}, u32[]{:S(2)}) collective-permute-start(bf16[16,384]{1,0:T(8,128)(2,1)S(1)} %pad_maximum_fusion.1), channel_id=1, source_target_pairs={{0,32},{8,40},{16,48},{24,56},{32,64},{40,72},{48,80},{56,88},{64,... | collective-permute-start | bytes 36872 | tf_op jit(solution)/shard_map/ppermute | solution.py:29
  71.2 15.9 %all-to-all-start.1 = ((bf16[8,32,1024]{2,1,0:T(8,128)(2,1)}), bf16[8,32,1024]{2,1,0:T(8,128)(2,1)S(1)}, u32[]{:S(2)}, u32[]{:S(2)}) async-start(bf16[8,32,1024]{2,1,0:T(8,128)(2,1)} %broadcast_in_dim.13), calls=%async_computation.1 | async-start | bytes 1048576 | tf_op jit(solution)/shard_map/all_to_all | solution.py:20
  87.1 1.2 copy-start.3
  88.3 6.5 %copy-start.9 = (f32[2,16]{1,0:T(2,128)S(1)}, f32[2,16]{1,0:T(2,128)}, u32[]{:S(2)}) copy-start(f32[2,16]{1,0:T(2,128)} %param.14) | copy-start | bytes 388
  90.0 14.7 %collective-permute-start.3 = (bf16[4,16,384]{2,1,0:T(8,128)(2,1)S(1)}, bf16[4,16,384]{2,1,0:T(8,128)(2,1)S(1)}, u32[]{:S(2)}, u32[]{:S(2)}) collective-permute-start(bf16[4,16,384]{2,1,0:T(8,128)(2,1)S(1)} %constant_dynamic-slice_fusion.1), channel_id=1, source_target_pairs={{0,24},{8,0},{16,8},{24,16},{32,56},{40,32},{48,40},{56,48},{64,88... | collective-permute-start | bytes 147464 | tf_op jit(solution)/shard_map/ppermute | solution.py:29
  95.0 9.8 %collective-permute-start.4 = (bf16[4,16,384]{2,1,0:T(8,128)(2,1)S(1)}, bf16[4,16,384]{2,1,0:T(8,128)(2,1)S(1)}, u32[]{:S(2)}, u32[]{:S(2)}) collective-permute-start(bf16[4,16,384]{2,1,0:T(8,128)(2,1)S(1)} %constant_dynamic-slice_fusion.1), channel_id=1, source_target_pairs={{0,16},{8,24},{16,0},{24,8},{32,48},{40,56},{48,32},{56,40},{64,80... | collective-permute-start | bytes 147464 | tf_op jit(solution)/shard_map/ppermute | solution.py:29
  96.9 7.9 %collective-permute-start.5 = (bf16[4,16,384]{2,1,0:T(8,128)(2,1)S(1)}, bf16[4,16,384]{2,1,0:T(8,128)(2,1)S(1)}, u32[]{:S(2)}, u32[]{:S(2)}) collective-permute-start(bf16[4,16,384]{2,1,0:T(8,128)(2,1)S(1)} %constant_dynamic-slice_fusion.1), channel_id=1, source_target_pairs={{0,8},{8,16},{16,24},{24,0},{32,40},{40,48},{48,56},{56,32},{64,72... | collective-permute-start | bytes 147464 | tf_op jit(solution)/shard_map/ppermute | solution.py:29
  99.5 14.6 %all-to-all-start.2 = ((bf16[8,32,1024]{2,1,0:T(8,128)(2,1)}), bf16[8,32,1024]{2,1,0:T(8,128)(2,1)S(1)}, u32[]{:S(2)}, u32[]{:S(2)}) async-start(bf16[8,32,1024]{2,1,0:T(8,128)(2,1)} %experts.1), calls=%async_computation.2 | async-start | bytes 1048576 | tf_op jit(solution)/shard_map/all_to_all | solution.py:20
  114.2 12.0 %copy-start.8 = (s32[4]{0:T(128)S(1)}, s32[4]{0:T(128)}, u32[]{:S(2)}) copy-start(s32[4]{0:T(128)} %constant.116.clone) | copy-start | bytes 52
  115.6 40.1 %copy-start.5 = (bf16[128,1024]{1,0:T(8,128)(2,1)S(1)}, bf16[128,1024]{1,0:T(8,128)(2,1)}, u32[]{:S(2)}) copy-start(bf16[128,1024]{1,0:T(8,128)(2,1)} %param.12) | copy-start | bytes 786436
  115.6 39.9 %all-to-all-start.3 = ((bf16[64,4,1024]{2,1,0:T(4,128)(2,1)}), bf16[64,4,1024]{2,1,0:T(4,128)(2,1)S(1)}, u32[]{:S(2)}, u32[]{:S(2)}) async-start(bf16[64,4,1024]{2,1,0:T(4,128)(2,1)} %reshape.75), calls=%async_computation.3 | async-start | bytes 1048576 | tf_op jit(solution)/shard_map/all_to_all | solution.py:20
  126.2 10.1 %collective-permute-start.9 = (bf16[4,4,16,384]{3,2,1,0:T(8,128)(2,1)S(1)}, bf16[4,4,16,384]{3,2,1,0:T(8,128)(2,1)S(1)}, u32[]{:S(2)}, u32[]{:S(2)}) collective-permute-start(bf16[4,4,16,384]{3,2,1,0:T(8,128)(2,1)S(1)} %dynamic-slice_bitcast_fusion), channel_id=1, source_target_pairs={{0,384},{8,392},{16,400},{24,408},{32,416},{40,424},{48,432},{56,4... | collective-permute-start | bytes 589832 | tf_op jit(solution)/shard_map/ppermute | solution.py:29
  131.3 24.8 %copy-start.7 = (f32[1024]{0:T(1024)S(1)}, f32[1024]{0:T(1024)}, u32[]{:S(2)}) copy-start(f32[1024]{0:T(1024)} %param.18) | copy-start | bytes 12292
  131.3 9.8 %collective-permute-start.10 = (bf16[4,4,16,384]{3,2,1,0:T(8,128)(2,1)S(1)}, bf16[4,4,16,384]{3,2,1,0:T(8,128)(2,1)S(1)}, u32[]{:S(2)}, u32[]{:S(2)}) collective-permute-start(bf16[4,4,16,384]{3,2,1,0:T(8,128)(2,1)S(1)} %dynamic-slice_bitcast_fusion), channel_id=1, source_target_pairs={{0,256},{8,264},{16,272},{24,280},{32,288},{40,296},{48,304},{56,3... | collective-permute-start | bytes 589832 | tf_op jit(solution)/shard_map/ppermute | solution.py:29
  133.7 31.0 %collective-permute-start.11 = (bf16[4,4,16,384]{3,2,1,0:T(8,128)(2,1)S(1)}, bf16[4,4,16,384]{3,2,1,0:T(8,128)(2,1)S(1)}, u32[]{:S(2)}, u32[]{:S(2)}) collective-permute-start(bf16[4,4,16,384]{3,2,1,0:T(8,128)(2,1)S(1)} %dynamic-slice_bitcast_fusion), channel_id=1, source_target_pairs={{0,128},{8,136},{16,144},{24,152},{32,160},{40,168},{48,176},{56,1... | collective-permute-start | bytes 589832 | tf_op jit(solution)/shard_map/ppermute | solution.py:29
  156.1 15.9 %copy-start.4 = (bf16[128,1024]{1,0:T(8,128)(2,1)}, bf16[128,1024]{1,0:T(8,128)(2,1)S(1)}, u32[]{:S(2)}) copy-start(bf16[128,1024]{1,0:T(8,128)(2,1)S(1)} %get-tuple-element.25) | copy-start | bytes 786436
  156.2 8.6 %collective-permute-start.8 = (bf16[128,1024]{1,0:T(8,128)(2,1)S(1)}, bf16[128,1024]{1,0:T(8,128)(2,1)S(1)}, u32[]{:S(2)}, u32[]{:S(2)}) collective-permute-start(bf16[128,1024]{1,0:T(8,128)(2,1)S(1)} %fusion.3), channel_id=1, source_target_pairs={{0,4},{1,5},{2,6},{3,7},{4,0},{5,1},{6,2},{7,3},{8,12},{9,13},{10,... | collective-permute-start | bytes 786440 | tf_op jit(solution)/shard_map/ppermute | solution.py:29
  158.8 10.6 %collective-permute-start.7 = (bf16[128,1024]{1,0:T(8,128)(2,1)S(1)}, bf16[128,1024]{1,0:T(8,128)(2,1)S(1)}, u32[]{:S(2)}, u32[]{:S(2)}) collective-permute-start(bf16[128,1024]{1,0:T(8,128)(2,1)S(1)} %fusion.3), channel_id=1, source_target_pairs={{0,6},{1,7},{2,0},{3,1},{4,2},{5,3},{6,4},{7,5},{8,14},{9,15},{10,... | collective-permute-start | bytes 786440 | tf_op jit(solution)/shard_map/ppermute | solution.py:29
  162.8 9.1 %collective-permute-start.6 = (bf16[128,1024]{1,0:T(8,128)(2,1)S(1)}, bf16[128,1024]{1,0:T(8,128)(2,1)S(1)}, u32[]{:S(2)}, u32[]{:S(2)}) collective-permute-start(bf16[128,1024]{1,0:T(8,128)(2,1)S(1)} %fusion.3), channel_id=1, source_target_pairs={{0,2},{1,3},{2,4},{3,5},{4,6},{5,7},{6,0},{7,1},{8,10},{9,11},{10,... | collective-permute-start | bytes 786440 | tf_op jit(solution)/shard_map/ppermute | solution.py:29
  172.0 8.4 %collective-permute-start.12 = (bf16[512,1024]{1,0:T(8,128)(2,1)S(1)}, bf16[512,1024]{1,0:T(8,128)(2,1)S(1)}, u32[]{:S(2)}, u32[]{:S(2)}) collective-permute-start(bf16[512,1024]{1,0:T(8,128)(2,1)S(1)} %pad_maximum_fusion), channel_id=1, source_target_pairs={{0,1},{1,0},{2,3},{3,2},{4,5},{5,4},{6,7},{7,6},{8,9},{9,8},{10,11... | collective-permute-start | bytes 3145736 | tf_op jit(solution)/shard_map/ppermute | solution.py:29

commit v3 on v2

--- a/solution.py
+++ b/solution.py
@@ -49,17 +49,23 @@
     return lax.dynamic_slice_in_dim(turned, 3 - digit, 4, 0)
 
 
-def expert_kernel(chosen, gate, up, down, out):
+def expert_kernel(chosen, gate, up, down, out, down_here, sems):
     senders, _, width = chosen.shape
     experts = gate.shape[0]
     take = chosen.shape[1] // experts
+    moves = [
+        pltpu.make_async_copy(down.at[x], down_here.at[x], sems.at[x]) for x in range(experts)
+    ]
+    for move in moves:
+        move.start()
     for x in range(experts):
         slots = slice(x * take, (x + 1) * take)
         rows = chosen[:, slots, :].reshape(senders * take, width)
         gate_part = jnp.dot(rows, gate[x], preferred_element_type=jnp.float32)
         up_part = jnp.dot(rows, up[x], preferred_element_type=jnp.float32)
         hidden = (gate_part / (1.0 + jnp.exp(-gate_part)) * up_part).astype(jnp.bfloat16)
-        partial = jnp.dot(hidden, down[x], preferred_element_type=jnp.float32)
+        moves[x].wait()
+        partial = jnp.dot(hidden, down_here[x], preferred_element_type=jnp.float32)
         out[:, slots, :] = partial.astype(jnp.bfloat16).reshape(senders, take, width)
 
 
@@ -68,11 +74,15 @@
     return pl.pallas_call(
         expert_kernel,
         out_shape=jax.ShapeDtypeStruct(chosen.shape, chosen.dtype),
-        in_specs=[vmem] * 4,
+        in_specs=[vmem, vmem, vmem, pl.BlockSpec(memory_space=pltpu.HBM)],
         out_specs=vmem,
+        scratch_shapes=[
+            pltpu.VMEM(down.shape, down.dtype),
+            pltpu.SemaphoreType.DMA((down.shape[0],)),
+        ],
         compiler_params=pltpu.CompilerParams(vmem_limit_bytes=12 * 2**20),
         name="experts",
-    )(chosen, gate, up, down)
+    )(chosen, gate, up, pltpu.with_memory_space_constraint(down, pltpu.HBM))
 
 
 def attention_kernel(ids, train, near, far, out, queries, keys, values):
@@ -174,7 +184,10 @@
     outgoing = jnp.dot(owner_hit, inputs, preferred_element_type=jnp.float32)
     outgoing = outgoing.astype(jnp.bfloat16).reshape(exp_count, -1, model_width)
 
-    arrived = exchange(outgoing, "exp").reshape(-1, model_width)
+    outgoing, piece = lax.optimization_barrier((outgoing, piece))
+    quarter = gather_four(piece, exp_index // 4 % 4, 4)
+    arrived = exchange(outgoing, "exp")
+    arrived = arrived.reshape(-1, model_width)
 
     my_rows = lax.dynamic_slice_in_dim(selected, exp_index * experts, experts, 0)
     my_table = my_rows // table_rows
@@ -188,12 +201,10 @@
     slot_hit = (my_place == places).astype(jnp.bfloat16)
 
     compact = jnp.dot(slot_hit, arrived, preferred_element_type=jnp.float32).astype(jnp.bfloat16)
-    compact, piece = lax.optimization_barrier((compact, piece))
-    quarter = gather_four(piece, exp_index // 4 % 4, 4)
+    compact, quarter = lax.optimization_barrier((compact, quarter))
+    layer = jnp.moveaxis(gather_four(quarter, exp_index % 4, 1), 0, 1)
     chosen = exchange(copies(compact, ctx_count), "ctx")
     partials = expert_parts(chosen, gate_weight, up_weight, down_weight)
-    partials, quarter = lax.optimization_barrier((partials, quarter))
-    layer = jnp.moveaxis(gather_four(quarter, exp_index % 4, 1), 0, 1)
     parts = exchange(partials, "ctx")
     expert_out = jnp.sum(parts.astype(jnp.float32), axis=0)
     weighted = (expert_out * selection_gate.reshape(-1, 1)).astype(jnp.bfloat16)

time: 196 us -> 192 us (0.980)
  starting transfers between devices: 91.4 us -> 88 us
    all_to_all x4, starting transfers between devices: 41.7 us -> 28.7 us  [exchange(): return lax.all_to_all(blocks, axis, split_axis=0, concat_axis=0, tiled=True)]
    ppermute x13, starting transfers between devices: 49.7 us -> 59.3 us  [shift(): return lax.ppermute(v, axis, [(i, move(i)) for i in range(count)])]
where the time goes in v3:
time: 192 us; the launch traced here: 191 us
  starting transfers between devices  88 us (46%)
  waiting for transfers between devices  74.2 us (39%)
  blocking collectives  9.25 us (5%)
  local copies, waits for them, and re-layouts  6.61 us (3%)
  Pallas kernels  6.35 us (3%)
  matrix products  3.76 us (2%)
    all_to_all x4, waiting for transfers between devices, exchange(): return lax.all_to_all(blocks, axis, split_axis=0, concat_axis=0, tiled=True)  60.9 us
    ppermute x13, starting transfers between devices, shift(): return lax.ppermute(v, axis, [(i, move(i)) for i in range(count)])  59.3 us
    all_to_all x4, starting transfers between devices, exchange(): return lax.all_to_all(blocks, axis, split_axis=0, concat_axis=0, tiled=True)  28.7 us
    ppermute x13, waiting for transfers between devices, shift(): return lax.ppermute(v, axis, [(i, move(i)) for i in range(count)])  13.3 us
    all_to_all x1, blocking collectives, exchange(): return lax.all_to_all(blocks, axis, split_axis=0, concat_axis=0, tiled=True)  9.25 us
  transfers between devices with their start and end apart: 17, of which 9 were waited for; matrix products, arithmetic and copies ran while one was open for 2% of the time, Pallas kernels for 0%

profile of v3, /device:TPU:1, one launch (start us, length us, event | category | flops | bytes accessed | tf_op | source)
XLA Modules:
  0.0 191.4 jit_solution(682916270526902740)
XLA Ops:
  0.6 0.0 copy-start
  0.7 0.7 select_reduce_fusion.1
  1.4 0.1 reduce_max.12
  1.5 0.1 stack.61
  1.7 0.5 copy.47
  2.2 0.1 eq.49
  2.3 0.0 copy-start.5
  2.3 1.3 convolution_convert_fusion.1
  3.6 1.0 reshape.73
  4.6 0.7 constant_dynamic-slice_fusion.2
  5.4 13.4 %collective-permute-start = (bf16[16,384]{1,0:T(8,128)(2,1)S(1)}, bf16[16,384]{1,0:T(8,128)(2,1)S(1)}, u32[]{:S(2)}, u32[]{:S(2)}) collective-permute-start(bf16[16,384]{1,0:T(8,128)(2,1)S(1)} %pad_maximum_fusion.1), channel_id=1, source_target_pairs={{0,96},{8,104},{16,112},{24,120},{32,0},{40,8},{48,16},{56,24},{64... | collective-permute-start | bytes 36872 | tf_op jit(solution)/shard_map/ppermute | solution.py:29
  18.8 4.9 %collective-permute-start.1 = (bf16[16,384]{1,0:T(8,128)(2,1)S(1)}, bf16[16,384]{1,0:T(8,128)(2,1)S(1)}, u32[]{:S(2)}, u32[]{:S(2)}) collective-permute-start(bf16[16,384]{1,0:T(8,128)(2,1)S(1)} %pad_maximum_fusion.1), channel_id=1, source_target_pairs={{0,64},{8,72},{16,80},{24,88},{32,96},{40,104},{48,112},{56,120},{... | collective-permute-start | bytes 36872 | tf_op jit(solution)/shard_map/ppermute | solution.py:29
  23.7 7.3 %collective-permute-start.2 = (bf16[16,384]{1,0:T(8,128)(2,1)S(1)}, bf16[16,384]{1,0:T(8,128)(2,1)S(1)}, u32[]{:S(2)}, u32[]{:S(2)}) collective-permute-start(bf16[16,384]{1,0:T(8,128)(2,1)S(1)} %pad_maximum_fusion.1), channel_id=1, source_target_pairs={{0,32},{8,40},{16,48},{24,56},{32,64},{40,72},{48,80},{56,88},{64,... | collective-permute-start | bytes 36872 | tf_op jit(solution)/shard_map/ppermute | solution.py:29
  31.0 8.4 %all-to-all-start = ((bf16[64,4,1024]{2,1,0:T(4,128)(2,1)}), bf16[64,4,1024]{2,1,0:T(4,128)(2,1)S(1)}, u32[]{:S(2)}, u32[]{:S(2)}) async-start(bf16[64,4,1024]{2,1,0:T(4,128)(2,1)} %reshape.73), calls=%async_computation | async-start | bytes 1048576 | tf_op jit(solution)/shard_map/all_to_all | solution.py:20
  39.4 0.1 constant_dynamic-slice_fusion.5
  39.4 0.1 copy.56
  39.5 0.2 convert_reduce_fusion.1
  39.8 0.1 eq.56
  39.9 0.0 collective-permute-done
  40.0 28.0 %all-to-all-done = bf16[64,4,1024]{2,1,0:T(4,128)(2,1)S(1)} async-done(((bf16[64,4,1024]{2,1,0:T(4,128)(2,1)}), bf16[64,4,1024]{2,1,0:T(4,128)(2,1)S(1)}, u32[]{:S(2)}, u32[]{:S(2)}) %all-to-all-start) | async-done | bytes 524320 | tf_op jit(solution)/shard_map/all_to_all | solution.py:20
  68.0 0.1 reshape.74
  68.2 0.0 copy-start.1
  68.2 0.0 copy-start.2
  68.2 0.2 convolution_convert_fusion.4
  68.4 4.2 %collective-permute-start.3 = (bf16[4,16,384]{2,1,0:T(8,128)(2,1)S(1)}, bf16[4,16,384]{2,1,0:T(8,128)(2,1)S(1)}, u32[]{:S(2)}, u32[]{:S(2)}) collective-permute-start(bf16[4,16,384]{2,1,0:T(8,128)(2,1)S(1)} %constant_dynamic-slice_fusion.1), channel_id=1, source_target_pairs={{0,24},{8,0},{16,8},{24,16},{32,56},{40,32},{48,40},{56,48},{64,88... | collective-permute-start | bytes 147464 | tf_op jit(solution)/shard_map/ppermute | solution.py:29
  72.7 0.1 mul.59
  72.7 3.7 %collective-permute-start.4 = (bf16[4,16,384]{2,1,0:T(8,128)(2,1)S(1)}, bf16[4,16,384]{2,1,0:T(8,128)(2,1)S(1)}, u32[]{:S(2)}, u32[]{:S(2)}) collective-permute-start(bf16[4,16,384]{2,1,0:T(8,128)(2,1)S(1)} %constant_dynamic-slice_fusion.1), channel_id=1, source_target_pairs={{0,16},{8,24},{16,0},{24,8},{32,48},{40,56},{48,32},{56,40},{64,80... | collective-permute-start | bytes 147464 | tf_op jit(solution)/shard_map/ppermute | solution.py:29
  76.5 1.9 %collective-permute-start.5 = (bf16[4,16,384]{2,1,0:T(8,128)(2,1)S(1)}, bf16[4,16,384]{2,1,0:T(8,128)(2,1)S(1)}, u32[]{:S(2)}, u32[]{:S(2)}) collective-permute-start(bf16[4,16,384]{2,1,0:T(8,128)(2,1)S(1)} %constant_dynamic-slice_fusion.1), channel_id=1, source_target_pairs={{0,8},{8,16},{16,24},{24,0},{32,40},{40,48},{48,56},{56,32},{64,72... | collective-permute-start | bytes 147464 | tf_op jit(solution)/shard_map/ppermute | solution.py:29
  78.4 0.9 broadcast_in_dim.13
  79.2 7.8 %all-to-all-start.1 = ((bf16[8,32,1024]{2,1,0:T(8,128)(2,1)}), bf16[8,32,1024]{2,1,0:T(8,128)(2,1)S(1)}, u32[]{:S(2)}, u32[]{:S(2)}) async-start(bf16[8,32,1024]{2,1,0:T(8,128)(2,1)} %broadcast_in_dim.13), calls=%async_computation.1 | async-start | bytes 1048576 | tf_op jit(solution)/shard_map/all_to_all | solution.py:20
  87.2 9.2 %all-to-all-done.1.chosen = bf16[8,32,1024]{2,1,0:T(8,128)(2,1)S(1)} async-done(((bf16[8,32,1024]{2,1,0:T(8,128)(2,1)}), bf16[8,32,1024]{2,1,0:T(8,128)(2,1)S(1)}, u32[]{:S(2)}, u32[]{:S(2)}) %all-to-all-start.1) | async-done | bytes 524320 | tf_op jit(solution)/shard_map/all_to_all | solution.py:20
  96.4 2.6 %experts.1 = bf16[8,32,1024]{2,1,0:T(8,128)(2,1)} custom-call(bf16[8,32,1024]{2,1,0:T(8,128)(2,1)S(1)} %all-to-all-done.1.chosen, bf16[2,1024,256]{2,1,0:T(8,128)(2,1)S(1)} %copy-done.1, bf16[2,1024,256]{2,1,0:T(8,128)(2,1)S(1)} %copy-done.2, bf16[2,256,1024]{2,1,0:T(8,128)(2,1)} %down.1), custom_call_target="tpu_custom_call" | custom-call | tf_op jit(solution)/shard_map/experts/pallas_call | solution.py:74
  99.0 4.4 %all-to-all-start.2 = ((bf16[8,32,1024]{2,1,0:T(8,128)(2,1)}), bf16[8,32,1024]{2,1,0:T(8,128)(2,1)S(1)}, u32[]{:S(2)}, u32[]{:S(2)}) async-start(bf16[8,32,1024]{2,1,0:T(8,128)(2,1)} %experts.1), calls=%async_computation.2 | async-start | bytes 1048576 | tf_op jit(solution)/shard_map/all_to_all | solution.py:20
  103.5 9.3 %all-to-all-done.2 = bf16[8,32,1024]{2,1,0:T(8,128)(2,1)S(1)} async-done(((bf16[8,32,1024]{2,1,0:T(8,128)(2,1)}), bf16[8,32,1024]{2,1,0:T(8,128)(2,1)S(1)}, u32[]{:S(2)}, u32[]{:S(2)}) %all-to-all-start.2) | async-done | bytes 524320 | tf_op jit(solution)/shard_map/all_to_all | solution.py:20
  112.8 0.1 convert_reduce_fusion
  112.9 0.0 copy-start.7
  112.9 0.4 convolution_convert_fusion
  113.3 1.0 reshape.75
  114.3 8.2 %all-to-all-start.3 = ((bf16[64,4,1024]{2,1,0:T(4,128)(2,1)}), bf16[64,4,1024]{2,1,0:T(4,128)(2,1)S(1)}, u32[]{:S(2)}, u32[]{:S(2)}) async-start(bf16[64,4,1024]{2,1,0:T(4,128)(2,1)} %reshape.75), calls=%async_computation.3 | async-start | bytes 1048576 | tf_op jit(solution)/shard_map/all_to_all | solution.py:20
  122.5 4.3 %collective-permute-start.9 = (bf16[4,4,16,384]{3,2,1,0:T(8,128)(2,1)S(1)}, bf16[4,4,16,384]{3,2,1,0:T(8,128)(2,1)S(1)}, u32[]{:S(2)}, u32[]{:S(2)}) collective-permute-start(bf16[4,4,16,384]{3,2,1,0:T(8,128)(2,1)S(1)} %dynamic-slice_bitcast_fusion), channel_id=1, source_target_pairs={{0,384},{8,392},{16,400},{24,408},{32,416},{40,424},{48,432},{56,4... | collective-permute-start | bytes 589832 | tf_op jit(solution)/shard_map/ppermute | solution.py:29
  127.5 0.1 pad_add_fusion.1.ids
  127.6 2.4 %collective-permute-start.10 = (bf16[4,4,16,384]{3,2,1,0:T(8,128)(2,1)S(1)}, bf16[4,4,16,384]{3,2,1,0:T(8,128)(2,1)S(1)}, u32[]{:S(2)}, u32[]{:S(2)}) collective-permute-start(bf16[4,4,16,384]{3,2,1,0:T(8,128)(2,1)S(1)} %dynamic-slice_bitcast_fusion), channel_id=1, source_target_pairs={{0,256},{8,264},{16,272},{24,280},{32,288},{40,296},{48,304},{56,3... | collective-permute-start | bytes 589832 | tf_op jit(solution)/shard_map/ppermute | solution.py:29
  130.0 2.6 %collective-permute-start.11 = (bf16[4,4,16,384]{3,2,1,0:T(8,128)(2,1)S(1)}, bf16[4,4,16,384]{3,2,1,0:T(8,128)(2,1)S(1)}, u32[]{:S(2)}, u32[]{:S(2)}) collective-permute-start(bf16[4,4,16,384]{3,2,1,0:T(8,128)(2,1)S(1)} %dynamic-slice_bitcast_fusion), channel_id=1, source_target_pairs={{0,128},{8,136},{16,144},{24,152},{32,160},{40,168},{48,176},{56,1... | collective-permute-start | bytes 589832 | tf_op jit(solution)/shard_map/ppermute | solution.py:29
  132.7 4.8 %collective-permute-done.10 = bf16[4,4,16,384]{3,2,1,0:T(8,128)(2,1)S(1)} collective-permute-done((bf16[4,4,16,384]{3,2,1,0:T(8,128)(2,1)S(1)}, bf16[4,4,16,384]{3,2,1,0:T(8,128)(2,1)S(1)}, u32[]{:S(2)}, u32[]{:S(2)}) %collective-permute-start.10) | collective-permute-done | bytes 196640 | tf_op jit(solution)/shard_map/ppermute | solution.py:29
  137.5 14.3 %all-to-all-done.3 = bf16[64,4,1024]{2,1,0:T(4,128)(2,1)S(1)} async-done(((bf16[64,4,1024]{2,1,0:T(4,128)(2,1)}), bf16[64,4,1024]{2,1,0:T(4,128)(2,1)S(1)}, u32[]{:S(2)}, u32[]{:S(2)}) %all-to-all-start.3) | async-done | bytes 524320 | tf_op jit(solution)/shard_map/all_to_all | solution.py:20
  151.8 0.1 reshape.76
  151.9 0.4 fusion.1
  152.4 0.1 fusion.3
  152.5 2.5 %collective-permute-start.8 = (bf16[128,1024]{1,0:T(8,128)(2,1)S(1)}, bf16[128,1024]{1,0:T(8,128)(2,1)S(1)}, u32[]{:S(2)}, u32[]{:S(2)}) collective-permute-start(bf16[128,1024]{1,0:T(8,128)(2,1)S(1)} %fusion.3), channel_id=1, source_target_pairs={{0,4},{1,5},{2,6},{3,7},{4,0},{5,1},{6,2},{7,3},{8,12},{9,13},{10,... | collective-permute-start | bytes 786440 | tf_op jit(solution)/shard_map/ppermute | solution.py:29
  155.1 4.0 %collective-permute-start.7 = (bf16[128,1024]{1,0:T(8,128)(2,1)S(1)}, bf16[128,1024]{1,0:T(8,128)(2,1)S(1)}, u32[]{:S(2)}, u32[]{:S(2)}) collective-permute-start(bf16[128,1024]{1,0:T(8,128)(2,1)S(1)} %fusion.3), channel_id=1, source_target_pairs={{0,6},{1,7},{2,0},{3,1},{4,2},{5,3},{6,4},{7,5},{8,14},{9,15},{10,... | collective-permute-start | bytes 786440 | tf_op jit(solution)/shard_map/ppermute | solution.py:29
  159.1 1.9 %collective-permute-start.6 = (bf16[128,1024]{1,0:T(8,128)(2,1)S(1)}, bf16[128,1024]{1,0:T(8,128)(2,1)S(1)}, u32[]{:S(2)}, u32[]{:S(2)}) collective-permute-start(bf16[128,1024]{1,0:T(8,128)(2,1)S(1)} %fusion.3), channel_id=1, source_target_pairs={{0,2},{1,3},{2,4},{3,5},{4,6},{5,7},{6,0},{7,1},{8,10},{9,11},{10,... | collective-permute-start | bytes 786440 | tf_op jit(solution)/shard_map/ppermute | solution.py:29
  161.1 0.1 collective-permute-done.8
  161.2 4.4 %collective-permute-done.7 = bf16[128,1024]{1,0:T(8,128)(2,1)S(1)} collective-permute-done((bf16[128,1024]{1,0:T(8,128)(2,1)S(1)}, bf16[128,1024]{1,0:T(8,128)(2,1)S(1)}, u32[]{:S(2)}, u32[]{:S(2)}) %collective-permute-start.7) | collective-permute-done | bytes 262176 | tf_op jit(solution)/shard_map/ppermute | solution.py:29
  165.6 2.6 %collective-permute-done.6 = bf16[128,1024]{1,0:T(8,128)(2,1)S(1)} collective-permute-done((bf16[128,1024]{1,0:T(8,128)(2,1)S(1)}, bf16[128,1024]{1,0:T(8,128)(2,1)S(1)}, u32[]{:S(2)}, u32[]{:S(2)}) %collective-permute-start.6) | collective-permute-done | bytes 262176 | tf_op jit(solution)/shard_map/ppermute | solution.py:29
  168.2 0.1 pad_maximum_fusion
  168.3 6.1 %collective-permute-start.12 = (bf16[512,1024]{1,0:T(8,128)(2,1)S(1)}, bf16[512,1024]{1,0:T(8,128)(2,1)S(1)}, u32[]{:S(2)}, u32[]{:S(2)}) collective-permute-start(bf16[512,1024]{1,0:T(8,128)(2,1)S(1)} %pad_maximum_fusion), channel_id=1, source_target_pairs={{0,1},{1,0},{2,3},{3,2},{4,5},{5,4},{6,7},{7,6},{8,9},{9,8},{10,11... | collective-permute-start | bytes 3145736 | tf_op jit(solution)/shard_map/ppermute | solution.py:29
  174.5 0.1 constant_dynamic-slice_fusion
  174.6 0.7 convolution_convert_fusion.3.near
  175.4 1.3 collective-permute-done.12
  176.7 0.7 convolution_convert_fusion.2.far
  177.4 3.7 %attention.1 = bf16[8,128,128]{2,1,0:T(8,128)(2,1)S(1)} custom-call(s32[8]{0:T(128)S(1)} %pad_add_fusion.1.ids, s32[1]{0:T(128)S(6)} %copy.75.train, bf16[512,384]{1,0:T(8,128)(2,1)S(1)} %convolution_convert_fusion.3.near, bf16[512,384]{1,0:T(8,128)(2,1)S(1)} %convolution_convert_fusion.2.far), custom_call_target="tpu_custom_call" | custom-call | tf_op jit(solution)/shard_map/attention/pallas_call | solution.py:130
  181.1 9.2 %all_to_all.25 = bf16[8,128,128]{2,1,0:T(8,128)(2,1)S(1)} all-to-all(bf16[8,128,128]{2,1,0:T(8,128)(2,1)S(1)} %attention.1), channel_id=1, replica_groups=mesh['exp'=64,'ctx'=8] {'ctx'}, dimensions={0} | all-to-all | bytes 524288 | tf_op jit(solution)/shard_map/all_to_all | solution.py:20
  190.4 0.2 copy.54
  190.6 0.9 copy.55
  (52 shorter events, 0.5 us)
Async XLA Ops:
  0.6 4.0 %copy-start = (bf16[16,1024]{1,0:T(8,128)(2,1)S(1)}, bf16[16,1024]{1,0:T(8,128)(2,1)}, u32[]{:S(2)}) copy-start(bf16[16,1024]{1,0:T(8,128)(2,1)} %param.19) | copy-start | bytes 98308
  2.3 37.0 %copy-start.5 = (s32[128,16]{0,1:T(8,128)S(1)}, s32[128,16]{0,1:T(8,128)}, u32[]{:S(2)}) copy-start(s32[128,16]{0,1:T(8,128)} %param.13) | copy-start | bytes 24580
  5.4 67.3 %copy-start.8 = (f32[2,16]{1,0:T(2,128)S(1)}, f32[2,16]{1,0:T(2,128)}, u32[]{:S(2)}) copy-start(f32[2,16]{1,0:T(2,128)} %param.14) | copy-start | bytes 388
  5.4 34.5 %collective-permute-start = (bf16[16,384]{1,0:T(8,128)(2,1)S(1)}, bf16[16,384]{1,0:T(8,128)(2,1)S(1)}, u32[]{:S(2)}, u32[]{:S(2)}) collective-permute-start(bf16[16,384]{1,0:T(8,128)(2,1)S(1)} %pad_maximum_fusion.1), channel_id=1, source_target_pairs={{0,96},{8,104},{16,112},{24,120},{32,0},{40,8},{48,16},{56,24},{64... | collective-permute-start | bytes 36872 | tf_op jit(solution)/shard_map/ppermute | solution.py:29
  18.8 21.1 %collective-permute-start.1 = (bf16[16,384]{1,0:T(8,128)(2,1)S(1)}, bf16[16,384]{1,0:T(8,128)(2,1)S(1)}, u32[]{:S(2)}, u32[]{:S(2)}) collective-permute-start(bf16[16,384]{1,0:T(8,128)(2,1)S(1)} %pad_maximum_fusion.1), channel_id=1, source_target_pairs={{0,64},{8,72},{16,80},{24,88},{32,96},{40,104},{48,112},{56,120},{... | collective-permute-start | bytes 36872 | tf_op jit(solution)/shard_map/ppermute | solution.py:29
  23.7 16.2 %collective-permute-start.2 = (bf16[16,384]{1,0:T(8,128)(2,1)S(1)}, bf16[16,384]{1,0:T(8,128)(2,1)S(1)}, u32[]{:S(2)}, u32[]{:S(2)}) collective-permute-start(bf16[16,384]{1,0:T(8,128)(2,1)S(1)} %pad_maximum_fusion.1), channel_id=1, source_target_pairs={{0,32},{8,40},{16,48},{24,56},{32,64},{40,72},{48,80},{56,88},{64,... | collective-permute-start | bytes 36872 | tf_op jit(solution)/shard_map/ppermute | solution.py:29
  31.0 37.1 %all-to-all-start = ((bf16[64,4,1024]{2,1,0:T(4,128)(2,1)}), bf16[64,4,1024]{2,1,0:T(4,128)(2,1)S(1)}, u32[]{:S(2)}, u32[]{:S(2)}) async-start(bf16[64,4,1024]{2,1,0:T(4,128)(2,1)} %reshape.73), calls=%async_computation | async-start | bytes 1048576 | tf_op jit(solution)/shard_map/all_to_all | solution.py:20
  68.2 28.2 %copy-start.1 = (bf16[2,1024,256]{2,1,0:T(8,128)(2,1)S(1)}, bf16[2,1024,256]{2,1,0:T(8,128)(2,1)}, u32[]{:S(2)}) copy-start(bf16[2,1024,256]{2,1,0:T(8,128)(2,1)} %gate.1) | copy-start | bytes 3145732
  68.2 28.2 %copy-start.2 = (bf16[2,1024,256]{2,1,0:T(8,128)(2,1)S(1)}, bf16[2,1024,256]{2,1,0:T(8,128)(2,1)}, u32[]{:S(2)}) copy-start(bf16[2,1024,256]{2,1,0:T(8,128)(2,1)} %up.1) | copy-start | bytes 3145732
  68.4 18.6 %collective-permute-start.3 = (bf16[4,16,384]{2,1,0:T(8,128)(2,1)S(1)}, bf16[4,16,384]{2,1,0:T(8,128)(2,1)S(1)}, u32[]{:S(2)}, u32[]{:S(2)}) collective-permute-start(bf16[4,16,384]{2,1,0:T(8,128)(2,1)S(1)} %constant_dynamic-slice_fusion.1), channel_id=1, source_target_pairs={{0,24},{8,0},{16,8},{24,16},{32,56},{40,32},{48,40},{56,48},{64,88... | collective-permute-start | bytes 147464 | tf_op jit(solution)/shard_map/ppermute | solution.py:29
  72.7 14.3 %collective-permute-start.4 = (bf16[4,16,384]{2,1,0:T(8,128)(2,1)S(1)}, bf16[4,16,384]{2,1,0:T(8,128)(2,1)S(1)}, u32[]{:S(2)}, u32[]{:S(2)}) collective-permute-start(bf16[4,16,384]{2,1,0:T(8,128)(2,1)S(1)} %constant_dynamic-slice_fusion.1), channel_id=1, source_target_pairs={{0,16},{8,24},{16,0},{24,8},{32,48},{40,56},{48,32},{56,40},{64,80... | collective-permute-start | bytes 147464 | tf_op jit(solution)/shard_map/ppermute | solution.py:29
  76.5 10.6 %collective-permute-start.5 = (bf16[4,16,384]{2,1,0:T(8,128)(2,1)S(1)}, bf16[4,16,384]{2,1,0:T(8,128)(2,1)S(1)}, u32[]{:S(2)}, u32[]{:S(2)}) collective-permute-start(bf16[4,16,384]{2,1,0:T(8,128)(2,1)S(1)} %constant_dynamic-slice_fusion.1), channel_id=1, source_target_pairs={{0,8},{8,16},{16,24},{24,0},{32,40},{40,48},{48,56},{56,32},{64,72... | collective-permute-start | bytes 147464 | tf_op jit(solution)/shard_map/ppermute | solution.py:29
  79.2 17.1 %all-to-all-start.1 = ((bf16[8,32,1024]{2,1,0:T(8,128)(2,1)}), bf16[8,32,1024]{2,1,0:T(8,128)(2,1)S(1)}, u32[]{:S(2)}, u32[]{:S(2)}) async-start(bf16[8,32,1024]{2,1,0:T(8,128)(2,1)} %broadcast_in_dim.13), calls=%async_computation.1 | async-start | bytes 1048576 | tf_op jit(solution)/shard_map/all_to_all | solution.py:20
  99.0 13.8 %all-to-all-start.2 = ((bf16[8,32,1024]{2,1,0:T(8,128)(2,1)}), bf16[8,32,1024]{2,1,0:T(8,128)(2,1)S(1)}, u32[]{:S(2)}, u32[]{:S(2)}) async-start(bf16[8,32,1024]{2,1,0:T(8,128)(2,1)} %experts.1), calls=%async_computation.2 | async-start | bytes 1048576 | tf_op jit(solution)/shard_map/all_to_all | solution.py:20
  112.9 9.6 %copy-start.7 = (s32[4]{0:T(128)S(1)}, s32[4]{0:T(128)}, u32[]{:S(2)}) copy-start(s32[4]{0:T(128)} %constant.116.clone) | copy-start | bytes 52
  114.3 37.6 %copy-start.4 = (bf16[128,1024]{1,0:T(8,128)(2,1)S(1)}, bf16[128,1024]{1,0:T(8,128)(2,1)}, u32[]{:S(2)}) copy-start(bf16[128,1024]{1,0:T(8,128)(2,1)} %param.12) | copy-start | bytes 786436
  114.3 37.5 %all-to-all-start.3 = ((bf16[64,4,1024]{2,1,0:T(4,128)(2,1)}), bf16[64,4,1024]{2,1,0:T(4,128)(2,1)S(1)}, u32[]{:S(2)}, u32[]{:S(2)}) async-start(bf16[64,4,1024]{2,1,0:T(4,128)(2,1)} %reshape.75), calls=%async_computation.3 | async-start | bytes 1048576 | tf_op jit(solution)/shard_map/all_to_all | solution.py:20
  122.5 10.1 %collective-permute-start.9 = (bf16[4,4,16,384]{3,2,1,0:T(8,128)(2,1)S(1)}, bf16[4,4,16,384]{3,2,1,0:T(8,128)(2,1)S(1)}, u32[]{:S(2)}, u32[]{:S(2)}) collective-permute-start(bf16[4,4,16,384]{3,2,1,0:T(8,128)(2,1)S(1)} %dynamic-slice_bitcast_fusion), channel_id=1, source_target_pairs={{0,384},{8,392},{16,400},{24,408},{32,416},{40,424},{48,432},{56,4... | collective-permute-start | bytes 589832 | tf_op jit(solution)/shard_map/ppermute | solution.py:29
  127.6 24.8 %copy-start.6 = (f32[1024]{0:T(1024)S(1)}, f32[1024]{0:T(1024)}, u32[]{:S(2)}) copy-start(f32[1024]{0:T(1024)} %param.18) | copy-start | bytes 12292
  127.6 9.8 %collective-permute-start.10 = (bf16[4,4,16,384]{3,2,1,0:T(8,128)(2,1)S(1)}, bf16[4,4,16,384]{3,2,1,0:T(8,128)(2,1)S(1)}, u32[]{:S(2)}, u32[]{:S(2)}) collective-permute-start(bf16[4,4,16,384]{3,2,1,0:T(8,128)(2,1)S(1)} %dynamic-slice_bitcast_fusion), channel_id=1, source_target_pairs={{0,256},{8,264},{16,272},{24,280},{32,288},{40,296},{48,304},{56,3... | collective-permute-start | bytes 589832 | tf_op jit(solution)/shard_map/ppermute | solution.py:29
  130.0 31.0 %collective-permute-start.11 = (bf16[4,4,16,384]{3,2,1,0:T(8,128)(2,1)S(1)}, bf16[4,4,16,384]{3,2,1,0:T(8,128)(2,1)S(1)}, u32[]{:S(2)}, u32[]{:S(2)}) collective-permute-start(bf16[4,4,16,384]{3,2,1,0:T(8,128)(2,1)S(1)} %dynamic-slice_bitcast_fusion), channel_id=1, source_target_pairs={{0,128},{8,136},{16,144},{24,152},{32,160},{40,168},{48,176},{56,1... | collective-permute-start | bytes 589832 | tf_op jit(solution)/shard_map/ppermute | solution.py:29
  152.4 15.9 %copy-start.3 = (bf16[128,1024]{1,0:T(8,128)(2,1)}, bf16[128,1024]{1,0:T(8,128)(2,1)S(1)}, u32[]{:S(2)}) copy-start(bf16[128,1024]{1,0:T(8,128)(2,1)S(1)} %get-tuple-element.25) | copy-start | bytes 786436
  152.5 8.6 %collective-permute-start.8 = (bf16[128,1024]{1,0:T(8,128)(2,1)S(1)}, bf16[128,1024]{1,0:T(8,128)(2,1)S(1)}, u32[]{:S(2)}, u32[]{:S(2)}) collective-permute-start(bf16[128,1024]{1,0:T(8,128)(2,1)S(1)} %fusion.3), channel_id=1, source_target_pairs={{0,4},{1,5},{2,6},{3,7},{4,0},{5,1},{6,2},{7,3},{8,12},{9,13},{10,... | collective-permute-start | bytes 786440 | tf_op jit(solution)/shard_map/ppermute | solution.py:29
  155.1 10.5 %collective-permute-start.7 = (bf16[128,1024]{1,0:T(8,128)(2,1)S(1)}, bf16[128,1024]{1,0:T(8,128)(2,1)S(1)}, u32[]{:S(2)}, u32[]{:S(2)}) collective-permute-start(bf16[128,1024]{1,0:T(8,128)(2,1)S(1)} %fusion.3), channel_id=1, source_target_pairs={{0,6},{1,7},{2,0},{3,1},{4,2},{5,3},{6,4},{7,5},{8,14},{9,15},{10,... | collective-permute-start | bytes 786440 | tf_op jit(solution)/shard_map/ppermute | solution.py:29
  159.1 9.2 %collective-permute-start.6 = (bf16[128,1024]{1,0:T(8,128)(2,1)S(1)}, bf16[128,1024]{1,0:T(8,128)(2,1)S(1)}, u32[]{:S(2)}, u32[]{:S(2)}) collective-permute-start(bf16[128,1024]{1,0:T(8,128)(2,1)S(1)} %fusion.3), channel_id=1, source_target_pairs={{0,2},{1,3},{2,4},{3,5},{4,6},{5,7},{6,0},{7,1},{8,10},{9,11},{10,... | collective-permute-start | bytes 786440 | tf_op jit(solution)/shard_map/ppermute | solution.py:29
  168.3 8.4 %collective-permute-start.12 = (bf16[512,1024]{1,0:T(8,128)(2,1)S(1)}, bf16[512,1024]{1,0:T(8,128)(2,1)S(1)}, u32[]{:S(2)}, u32[]{:S(2)}) collective-permute-start(bf16[512,1024]{1,0:T(8,128)(2,1)S(1)} %pad_maximum_fusion), channel_id=1, source_target_pairs={{0,1},{1,0},{2,3},{3,2},{4,5},{5,4},{6,7},{7,6},{8,9},{9,8},{10,11... | collective-permute-start | bytes 3145736 | tf_op jit(solution)/shard_map/ppermute | solution.py:29

commit v4 on v3

--- a/solution.py
+++ b/solution.py
@@ -20,10 +20,6 @@
     return lax.all_to_all(blocks, axis, split_axis=0, concat_axis=0, tiled=True)
 
 
-def copies(shard, count):
-    return jnp.broadcast_to(shard, (count, *shard.shape))
-
-
 def shift(v, axis, move):
     count = lax.axis_size(axis)
     return lax.ppermute(v, axis, [(i, move(i)) for i in range(count)])
@@ -37,16 +33,91 @@
     return shift(v, "ctx", lambda i: i ^ 1)
 
 
-def gather_four(v, digit, stride):
-    def move(step):
-        return lambda i: i + ((i // stride + step) % 4 - i // stride % 4) * stride
-
-    others = []
-    for step in (1, 2, 3):
-        others.append(shift(v, "exp", move(step)))
-    one, two, three = others
-    turned = jnp.stack([three, two, one, v, three, two, one])
-    return lax.dynamic_slice_in_dim(turned, 3 - digit, 4, 0)
+def gather_pair(v, index, stride):
+    other = shift(v, "exp", lambda i: i ^ stride)
+    turned = jnp.stack([other, v, other])
+    return lax.dynamic_slice_in_dim(turned, 1 - index // stride % 2, 2, 0)
+
+
+def gather_four(v, index, stride):
+    pair = gather_pair(v, index, stride)
+    four = gather_pair(pair, index, 2 * stride)
+    return four.reshape(4, *v.shape)
+
+
+def whole(memory, count):
+    return [pl.BlockSpec(memory_space=memory) for _ in range(count)]
+
+
+def small_kernel(body, outs, *arrays, scalars=0):
+    return pl.pallas_call(
+        body,
+        out_shape=outs,
+        in_specs=whole(pltpu.SMEM, scalars) + whole(pltpu.VMEM, len(arrays) - scalars),
+        out_specs=pl.BlockSpec(memory_space=pltpu.VMEM),
+        compiler_params=pltpu.CompilerParams(vmem_limit_bytes=8 * 2**20),
+    )(*arrays)
+
+
+def take_kernel(block, selected, inputs, out):
+    row_count, width = inputs.shape
+    taken = selected[...] - block[0] * row_count
+    mine = (taken >= 0) & (taken < row_count)
+    lower = jnp.min(jnp.where(mine, taken, row_count), axis=0, keepdims=True)
+    upper = jnp.max(jnp.where(mine, taken, -1), axis=0, keepdims=True)
+    upper = jnp.where(upper > lower, upper, -1)
+    count = out.shape[0]
+    experts = selected.shape[1]
+    slot = lax.broadcasted_iota(jnp.int32, (count, experts), 0)
+    expert = lax.broadcasted_iota(jnp.int32, (count, experts), 1)
+    either = jnp.where(slot % 2 == 0, lower, upper)
+    own = jnp.where(slot // 8 * 2 + slot % 4 // 2 == expert, either, 0)
+    pick = jnp.dot(
+        own.astype(jnp.float32).astype(jnp.bfloat16),
+        jnp.ones((experts, row_count), jnp.bfloat16),
+        preferred_element_type=jnp.float32,
+    ).astype(jnp.int32)
+    slot = lax.broadcasted_iota(jnp.int32, (count, row_count), 0)
+    row = lax.broadcasted_iota(jnp.int32, (count, row_count), 1)
+    hit = pick == row
+    left = jnp.where(hit & (slot % 8 < 4), 1.0, 0.0).astype(jnp.bfloat16)
+    right = jnp.where(hit & (slot % 8 >= 4), 1.0, 0.0).astype(jnp.bfloat16)
+    half = width // 2
+    out[...] = (
+        jnp.dot(left, inputs[:, :half], preferred_element_type=jnp.float32)
+        + jnp.dot(right, inputs[:, half:], preferred_element_type=jnp.float32)
+    ).astype(out.dtype)
+
+
+def fill_kernel(place, arrived, out):
+    slots, half = place.shape[0], arrived.shape[1]
+    source = lax.broadcasted_iota(jnp.int32, (slots, arrived.shape[0]), 1)
+    for h in range(2):
+        hit = jnp.where(source == place[...] + 4 * h, 1.0, 0.0).astype(jnp.bfloat16)
+        rows = jnp.dot(hit, arrived[...], preferred_element_type=jnp.float32).astype(out.dtype)
+        for c in range(out.shape[0]):
+            out[c, :, h * half : (h + 1) * half] = rows
+
+
+def reply_kernel(place, gate, parts, out):
+    total = parts[0].astype(jnp.float32)
+    for c in range(1, parts.shape[0]):
+        total = total + parts[c].astype(jnp.float32)
+    weighted = (total * gate[...]).astype(jnp.bfloat16)
+    half = out.shape[1]
+    target = lax.broadcasted_iota(jnp.int32, (out.shape[0], place.shape[1]), 0)
+    left = jnp.where(target == place[...], 1.0, 0.0).astype(jnp.bfloat16)
+    right = jnp.where(target == place[...] + 4, 1.0, 0.0).astype(jnp.bfloat16)
+    out[...] = (
+        jnp.dot(left, weighted[:, :half], preferred_element_type=jnp.float32)
+        + jnp.dot(right, weighted[:, half:], preferred_element_type=jnp.float32)
+    ).astype(out.dtype)
+
+
+def join_kernel(pieces, out):
+    width = pieces.shape[2]
+    for c in range(pieces.shape[0]):
+        out[:, c * width : (c + 1) * width] = pieces[c]
 
 
 def expert_kernel(chosen, gate, up, down, out, down_here, sems):
@@ -173,21 +244,25 @@
         axis=1,
     )
     own_block = exp_index * ctx_count + ctx_index
+    half = model_width // 2
+    sent = (exp_count, 2 * experts * MOST, half)
+    flat = jax.ShapeDtypeStruct((sent[0] * sent[1], half), inputs.dtype)
+    outgoing = small_kernel(take_kernel, flat, own_block.reshape(1), selected.T, inputs, scalars=1)
+    arrived = exchange(outgoing.reshape(sent), "exp").reshape(flat.shape)
+    quarter = gather_four(piece, exp_index, 4)
+    arrived, quarter = lax.optimization_barrier((arrived, quarter))
+
     taken = selected.reshape(exp_count, experts, group_take) - own_block * row_count
     mine = (taken >= 0) & (taken < row_count)
     lower = jnp.min(jnp.where(mine, taken, row_count), axis=2)
     upper = jnp.max(jnp.where(mine, taken, -1), axis=2)
     upper = jnp.where(upper > lower, upper, -1)
-    picks = jnp.stack([lower, upper], axis=2)
-    row_ids = jnp.arange(row_count, dtype=jnp.int32)
-    owner_hit = (picks.reshape(-1, 1) == row_ids).astype(jnp.bfloat16)
-    outgoing = jnp.dot(owner_hit, inputs, preferred_element_type=jnp.float32)
-    outgoing = outgoing.astype(jnp.bfloat16).reshape(exp_count, -1, model_width)
-
-    outgoing, piece = lax.optimization_barrier((outgoing, piece))
-    quarter = gather_four(piece, exp_index // 4 % 4, 4)
-    arrived = exchange(outgoing, "exp")
-    arrived = arrived.reshape(-1, model_width)
+    lower = jnp.where(lower < row_count, lower, -1)
+    picks = jnp.stack([lower, upper], axis=2).reshape(exp_count, 1, experts * MOST)
+    halves = jnp.arange(2, dtype=jnp.int32)[None, :, None] * row_count
+    picks = jnp.where(picks < 0, -1, picks + halves).reshape(-1, 1)
+    row_ids = jnp.arange(2 * row_count, dtype=jnp.int32)
+    owner_hit = (picks == row_ids).astype(jnp.bfloat16)
 
     my_rows = lax.dynamic_slice_in_dim(selected, exp_index * experts, experts, 0)
     my_table = my_rows // table_rows
@@ -196,29 +271,26 @@
     )
     my_rank = jnp.sum(lower_rows.astype(jnp.int32), axis=2)
     expert_ids = jnp.arange(experts, dtype=jnp.int32)[:, None]
-    my_place = ((my_table * experts + expert_ids) * MOST + my_rank).reshape(-1, 1)
-    places = jnp.arange(exp_count * experts * MOST, dtype=jnp.int32)
-    slot_hit = (my_place == places).astype(jnp.bfloat16)
-
-    compact = jnp.dot(slot_hit, arrived, preferred_element_type=jnp.float32).astype(jnp.bfloat16)
-    compact, quarter = lax.optimization_barrier((compact, quarter))
-    layer = jnp.moveaxis(gather_four(quarter, exp_index % 4, 1), 0, 1)
-    chosen = exchange(copies(compact, ctx_count), "ctx")
+    my_place = (my_table * sent[1] + expert_ids * MOST + my_rank).reshape(-1)
+    gates = selection_gate.reshape(-1, 1)
+
+    chosen_shape = jax.ShapeDtypeStruct(
+        (ctx_count, experts * group_take, model_width), inputs.dtype
+    )
+    compact = small_kernel(fill_kernel, chosen_shape, my_place.reshape(-1, 1), arrived)
+    chosen = exchange(compact, "ctx")
+    layer = jnp.moveaxis(gather_four(quarter, exp_index, 1), 0, 1)
+    chosen, layer = lax.optimization_barrier((chosen, layer))
     partials = expert_parts(chosen, gate_weight, up_weight, down_weight)
     parts = exchange(partials, "ctx")
-    expert_out = jnp.sum(parts.astype(jnp.float32), axis=0)
-    weighted = (expert_out * selection_gate.reshape(-1, 1)).astype(jnp.bfloat16)
-    reply = lax.dot_general(
-        slot_hit, weighted, (((0,), (0,)), ((), ())), preferred_element_type=jnp.float32
-    )
-    reply = reply.astype(jnp.bfloat16).reshape(exp_count, -1, model_width)
-    reply, layer = lax.optimization_barrier((reply, layer))
-    weight_rows = gather_four(layer, exp_index // N_Z, N_Z).reshape(model_width, -1)
-    returned = exchange(reply, "exp")
-    returned = returned.reshape(-1, model_width)
-    moe_sum = lax.dot_general(
+    reply = small_kernel(reply_kernel, flat, my_place.reshape(1, -1), gates, parts)
+    returned = exchange(reply.reshape(sent), "exp").reshape(flat.shape)
+    weight_rows = gather_four(layer, exp_index, N_Z).reshape(model_width, -1)
+    returned, weight_rows = lax.optimization_barrier((returned, weight_rows))
+    sums = lax.dot_general(
         owner_hit, returned, (((0,), (0,)), ((), ())), preferred_element_type=jnp.float32
     )
+    moe_sum = jnp.concatenate([sums[:row_count], sums[row_count:]], axis=1)
 
     layer_out = (inputs.astype(jnp.float32) + moe_sum).astype(jnp.bfloat16)
     widened = layer_out.astype(jnp.float32)
@@ -239,7 +311,7 @@
         ids, train_count, near_rows.astype(jnp.bfloat16), far_rows.astype(jnp.bfloat16)
     )
     by_heads = exchange(mixed, "ctx")
-    context = jnp.moveaxis(by_heads, 0, 1).reshape(row_count, model_width)
+    context = small_kernel(join_kernel, jax.ShapeDtypeStruct(inputs.shape, inputs.dtype), by_heads)
     return (layer_out, context)
 
 

time: 192 us -> 187 us (0.974)
  waiting for transfers between devices: 74.2 us -> 63.7 us
  Pallas kernels: 6.35 us -> 11 us
  starting transfers between devices: 88 us -> 91.4 us
  local copies, waits for them, and re-layouts: 6.61 us -> 4.07 us
    all_to_all x4, waiting for transfers between devices: 60.9 us -> 14.5 us  [exchange(): return lax.all_to_all(blocks, axis, split_axis=0, concat_axis=0, tiled=True)]
    ppermute x13 -> x10, waiting for transfers between devices: 13.3 us -> 49.2 us  [shift(): return lax.ppermute(v, axis, [(i, move(i)) for i in range(count)])]
    all_to_all x4, starting transfers between devices: 28.7 us -> 45.9 us  [exchange(): return lax.all_to_all(blocks, axis, split_axis=0, concat_axis=0, tiled=True)]
    ppermute x13 -> x10, starting transfers between devices: 59.3 us -> 45.5 us  [shift(): return lax.ppermute(v, axis, [(i, move(i)) for i in range(count)])]
    pallas_call x0 -> x4, Pallas kernels: none -> 4.59 us  [small_kernel(): pl.pallas_call(body, out_shape=outs, in_specs=whole(pltpu.SMEM, scalars)...]
    reshape x4 -> x2, local copies, waits for them, and re-layouts: 2.23 us -> 0.18 us  [the longest x1 0.1 us: local(): jnp.stack([lower, upper], axis=2).reshape(exp_count, 1, experts * MOST)]
  transfers between devices with their start and end apart: 17 -> 14, of which waited for: 9 -> 12; matrix products, arithmetic and copies ran while one was open for 2% -> 2% of each run, Pallas kernels for 0% -> 0%
where the time goes in v4:
time: 187 us; the launch traced here: 186 us
  starting transfers between devices  91.4 us (49%)
  waiting for transfers between devices  63.7 us (34%)
  Pallas kernels  11 us (6%)
  blocking collectives  9.25 us (5%)
  local copies, waits for them, and re-layouts  4.07 us (2%)
  matrix products  3.06 us (2%)
  other arithmetic  2.17 us (1%)
    ppermute x10, waiting for transfers between devices, shift(): return lax.ppermute(v, axis, [(i, move(i)) for i in range(count)])  49.2 us
    all_to_all x4, starting transfers between devices, exchange(): return lax.all_to_all(blocks, axis, split_axis=0, concat_axis=0, tiled=True)  45.9 us
    ppermute x10, starting transfers between devices, shift(): return lax.ppermute(v, axis, [(i, move(i)) for i in range(count)])  45.5 us
    all_to_all x4, waiting for transfers between devices, exchange(): return lax.all_to_all(blocks, axis, split_axis=0, concat_axis=0, tiled=True)  14.5 us
    all_to_all x1, blocking collectives, exchange(): return lax.all_to_all(blocks, axis, split_axis=0, concat_axis=0, tiled=True)  9.25 us
    pallas_call x4, Pallas kernels, small_kernel(): pl.pallas_call(body, out_shape=outs, in_specs=whole(pltpu.SMEM, scalars)...  4.59 us
  transfers between devices with their start and end apart: 14, of which 12 were waited for; matrix products, arithmetic and copies ran while one was open for 2% of the time, Pallas kernels for 0%

profile of v4, /device:TPU:1, one launch (start us, length us, event | category | flops | bytes accessed | tf_op | source)
XLA Modules:
  0.0 186.4 jit_solution(5945681446225495300)
XLA Ops:
  0.7 0.9 copy-done.3
  1.6 0.7 copy-done.5
  2.3 1.4 shard_map.131
  3.7 19.3 %all-to-all-start = ((bf16[64,8,512]{2,1,0:T(8,128)(2,1)}), bf16[64,8,512]{2,1,0:T(8,128)(2,1)S(1)}, u32[]{:S(2)}, u32[]{:S(2)}) async-start(bf16[64,8,512]{2,1,0:T(8,128)(2,1)} %bitcast.3), calls=%async_computation | async-start | bytes 1048576 | tf_op jit(solution)/shard_map/all_to_all | solution.py:20
  23.0 0.7 constant_dynamic-slice_fusion
  23.7 6.8 %collective-permute-start = (bf16[16,384]{1,0:T(8,128)(2,1)S(1)}, bf16[16,384]{1,0:T(8,128)(2,1)S(1)}, u32[]{:S(2)}, u32[]{:S(2)}) collective-permute-start(bf16[16,384]{1,0:T(8,128)(2,1)S(1)} %get-tuple-element.25), channel_id=1, source_target_pairs={{0,32},{8,40},{16,48},{24,56},{32,0},{40,8},{48,16},{56,24},{64,96... | collective-permute-start | bytes 36872 | tf_op jit(solution)/shard_map/ppermute | solution.py:25
  30.6 0.1 constant_dynamic-slice_fusion.3
  30.6 0.1 copy.55
  30.7 0.2 convert_reduce_fusion
  30.9 0.1 add_add_fusion
  31.0 0.1 reshape_reshape.12.place
  31.1 14.8 %collective-permute-done = bf16[16,384]{1,0:T(8,128)(2,1)S(1)} collective-permute-done((bf16[16,384]{1,0:T(8,128)(2,1)S(1)}, bf16[16,384]{1,0:T(8,128)(2,1)S(1)}, u32[]{:S(2)}, u32[]{:S(2)}) %collective-permute-start) | collective-permute-done | bytes 12320 | tf_op jit(solution)/shard_map/ppermute | solution.py:25
  45.9 12.7 %collective-permute-start.1 = (bf16[2,16,384]{2,1,0:T(8,128)(2,1)S(1)}, bf16[2,16,384]{2,1,0:T(8,128)(2,1)S(1)}, u32[]{:S(2)}, u32[]{:S(2)}) collective-permute-start(bf16[2,16,384]{2,1,0:T(8,128)(2,1)S(1)} %fusion.17), channel_id=1, source_target_pairs={{0,64},{8,72},{16,80},{24,88},{32,96},{40,104},{48,112},{56,120},{... | collective-permute-start | bytes 73736 | tf_op jit(solution)/shard_map/ppermute | solution.py:25
  58.7 1.2 collective-permute-done.1
  59.9 1.2 shard_map.132
  61.1 10.3 %all-to-all-start.1 = ((bf16[8,32,1024]{2,1,0:T(8,128)(2,1)}), bf16[8,32,1024]{2,1,0:T(8,128)(2,1)S(1)}, u32[]{:S(2)}, u32[]{:S(2)}) async-start(bf16[8,32,1024]{2,1,0:T(8,128)(2,1)} %shard_map.132), calls=%async_computation.1 | async-start | bytes 1048576 | tf_op jit(solution)/shard_map/all_to_all | solution.py:20
  71.4 2.4 %collective-permute-start.2 = (bf16[4,16,384]{2,1,0:T(8,128)(2,1)S(1)}, bf16[4,16,384]{2,1,0:T(8,128)(2,1)S(1)}, u32[]{:S(2)}, u32[]{:S(2)}) collective-permute-start(bf16[4,16,384]{2,1,0:T(8,128)(2,1)S(1)} %bitcast.44), channel_id=1, source_target_pairs={{0,8},{8,0},{16,24},{24,16},{32,40},{40,32},{48,56},{56,48},{64,72... | collective-permute-start | bytes 147464 | tf_op jit(solution)/shard_map/ppermute | solution.py:25
  73.8 2.8 %collective-permute-done.2 = bf16[4,16,384]{2,1,0:T(8,128)(2,1)S(1)} collective-permute-done((bf16[4,16,384]{2,1,0:T(8,128)(2,1)S(1)}, bf16[4,16,384]{2,1,0:T(8,128)(2,1)S(1)}, u32[]{:S(2)}, u32[]{:S(2)}) %collective-permute-start.2) | collective-permute-done | bytes 49184 | tf_op jit(solution)/shard_map/ppermute | solution.py:25
  76.6 1.9 %collective-permute-start.3 = (bf16[2,4,16,384]{3,2,0,1:T(8,128)(2,1)S(1)}, bf16[2,4,16,384]{3,2,0,1:T(8,128)(2,1)S(1)}, u32[]{:S(2)}, u32[]{:S(2)}) collective-permute-start(bf16[2,4,16,384]{3,2,0,1:T(8,128)(2,1)S(1)} %fusion.13), channel_id=1, source_target_pairs={{0,16},{8,24},{16,0},{24,8},{32,48},{40,56},{48,32},{56,40},{64,80... | collective-permute-start | bytes 294920 | tf_op jit(solution)/shard_map/ppermute | solution.py:25
  78.6 0.1 fusion.29
  78.6 7.4 %collective-permute-done.3 = bf16[2,4,16,384]{3,2,0,1:T(8,128)(2,1)S(1)} collective-permute-done((bf16[2,4,16,384]{3,2,0,1:T(8,128)(2,1)S(1)}, bf16[2,4,16,384]{3,2,0,1:T(8,128)(2,1)S(1)}, u32[]{:S(2)}, u32[]{:S(2)}) %collective-permute-start.3) | collective-permute-done | bytes 98336 | tf_op jit(solution)/shard_map/ppermute | solution.py:25
  86.1 0.1 fusion.11
  86.2 2.6 %experts.1 = bf16[8,32,1024]{2,1,0:T(8,128)(2,1)} custom-call(bf16[8,32,1024]{2,1,0:T(8,128)(2,1)S(1)} %all-to-all-done.1.chosen, bf16[2,1024,256]{2,1,0:T(8,128)(2,1)S(1)} %copy-done.1, bf16[2,1024,256]{2,1,0:T(8,128)(2,1)S(1)} %copy-done.2, bf16[2,256,1024]{2,1,0:T(8,128)(2,1)} %down.1), custom_call_target="tpu_custom_call" | custom-call | tf_op jit(solution)/shard_map/experts/pallas_call | solution.py:145
  88.9 5.0 %all-to-all-start.2 = ((bf16[8,32,1024]{2,1,0:T(8,128)(2,1)}), bf16[8,32,1024]{2,1,0:T(8,128)(2,1)S(1)}, u32[]{:S(2)}, u32[]{:S(2)}) async-start(bf16[8,32,1024]{2,1,0:T(8,128)(2,1)} %experts.1), calls=%async_computation.2 | async-start | bytes 1048576 | tf_op jit(solution)/shard_map/all_to_all | solution.py:20
  93.9 0.1 reshape_reshape.9.place
  94.0 0.1 reshape.146.gate
  94.1 9.2 %all-to-all-done.2.parts = bf16[8,32,1024]{2,1,0:T(8,128)(2,1)S(1)} async-done(((bf16[8,32,1024]{2,1,0:T(8,128)(2,1)}), bf16[8,32,1024]{2,1,0:T(8,128)(2,1)S(1)}, u32[]{:S(2)}, u32[]{:S(2)}) %all-to-all-start.2) | async-done | bytes 524320 | tf_op jit(solution)/shard_map/all_to_all | solution.py:20
  103.2 1.3 shard_map.133
  104.5 11.3 %all-to-all-start.3 = ((bf16[64,8,512]{2,1,0:T(8,128)(2,1)}), bf16[64,8,512]{2,1,0:T(8,128)(2,1)S(1)}, u32[]{:S(2)}, u32[]{:S(2)}) async-start(bf16[64,8,512]{2,1,0:T(8,128)(2,1)} %bitcast.17), calls=%async_computation.3 | async-start | bytes 1048576 | tf_op jit(solution)/shard_map/all_to_all | solution.py:20
  115.9 0.1 reduce_min.12
  116.1 0.1 reduce_max.12
  116.2 0.1 copy.47
  116.3 0.1 copy.48
  116.4 2.9 %collective-permute-start.4 = (bf16[4,4,16,384]{3,2,1,0:T(8,128)(2,1)S(1)}, bf16[4,4,16,384]{3,2,1,0:T(8,128)(2,1)S(1)}, u32[]{:S(2)}, u32[]{:S(2)}) collective-permute-start(bf16[4,4,16,384]{3,2,1,0:T(8,128)(2,1)S(1)} %bitcast.37), channel_id=1, source_target_pairs={{0,128},{8,136},{16,144},{24,152},{32,160},{40,168},{48,176},{56,1... | collective-permute-start | bytes 589832 | tf_op jit(solution)/shard_map/ppermute | solution.py:25
  119.3 4.9 %collective-permute-done.4 = bf16[4,4,16,384]{3,2,1,0:T(8,128)(2,1)S(1)} collective-permute-done((bf16[4,4,16,384]{3,2,1,0:T(8,128)(2,1)S(1)}, bf16[4,4,16,384]{3,2,1,0:T(8,128)(2,1)S(1)}, u32[]{:S(2)}, u32[]{:S(2)}) %collective-permute-start.4) | collective-permute-done | bytes 196640 | tf_op jit(solution)/shard_map/ppermute | solution.py:25
  124.2 0.2 fusion.8
  124.5 4.2 %collective-permute-start.5 = (bf16[2,4,4,16,384]{4,3,2,1,0:T(8,128)(2,1)S(1)}, bf16[2,4,4,16,384]{4,3,2,1,0:T(8,128)(2,1)S(1)}, u32[]{:S(2)}, u32[]{:S(2)}) collective-permute-start(bf16[2,4,4,16,384]{4,3,2,1,0:T(8,128)(2,1)S(1)} %fusion.8), channel_id=1, source_target_pairs={{0,256},{8,264},{16,272},{24,280},{32,288},{40,296},{48,304},{56,3... | collective-permute-start | bytes 1179656 | tf_op jit(solution)/shard_map/ppermute | solution.py:25
  128.7 0.1 copy.50
  128.8 0.1 copy.49
  129.0 0.1 add_select_fusion
  129.1 0.1 select_n.134
  129.2 0.2 fusion.28
  129.4 10.0 %collective-permute-done.5 = bf16[2,4,4,16,384]{4,3,2,1,0:T(8,128)(2,1)S(1)} collective-permute-done((bf16[2,4,4,16,384]{4,3,2,1,0:T(8,128)(2,1)S(1)}, bf16[2,4,4,16,384]{4,3,2,1,0:T(8,128)(2,1)S(1)}, u32[]{:S(2)}, u32[]{:S(2)}) %collective-permute-start.5) | collective-permute-done | bytes 393248 | tf_op jit(solution)/shard_map/ppermute | solution.py:25
  139.4 0.5 fusion.1
  139.9 5.3 %all-to-all-done.3 = bf16[64,8,512]{2,1,0:T(8,128)(2,1)S(1)} async-done(((bf16[64,8,512]{2,1,0:T(8,128)(2,1)}), bf16[64,8,512]{2,1,0:T(8,128)(2,1)S(1)}, u32[]{:S(2)}, u32[]{:S(2)}) %all-to-all-start.3) | async-done | bytes 524320 | tf_op jit(solution)/shard_map/all_to_all | solution.py:20
  145.2 0.4 fusion.6
  145.7 0.5 copy-done.4
  146.1 0.2 fusion.2
  146.3 0.1 fusion.4
  146.5 2.6 %collective-permute-start.8 = (bf16[128,1024]{1,0:T(8,128)(2,1)S(1)}, bf16[128,1024]{1,0:T(8,128)(2,1)S(1)}, u32[]{:S(2)}, u32[]{:S(2)}) collective-permute-start(bf16[128,1024]{1,0:T(8,128)(2,1)S(1)} %fusion.4), channel_id=1, source_target_pairs={{0,4},{1,5},{2,6},{3,7},{4,0},{5,1},{6,2},{7,3},{8,12},{9,13},{10,... | collective-permute-start | bytes 786440 | tf_op jit(solution)/shard_map/ppermute | solution.py:25
  149.1 3.9 %collective-permute-start.7 = (bf16[128,1024]{1,0:T(8,128)(2,1)S(1)}, bf16[128,1024]{1,0:T(8,128)(2,1)S(1)}, u32[]{:S(2)}, u32[]{:S(2)}) collective-permute-start(bf16[128,1024]{1,0:T(8,128)(2,1)S(1)} %fusion.4), channel_id=1, source_target_pairs={{0,6},{1,7},{2,0},{3,1},{4,2},{5,3},{6,4},{7,5},{8,14},{9,15},{10,... | collective-permute-start | bytes 786440 | tf_op jit(solution)/shard_map/ppermute | solution.py:25
  153.0 1.9 %collective-permute-start.6 = (bf16[128,1024]{1,0:T(8,128)(2,1)S(1)}, bf16[128,1024]{1,0:T(8,128)(2,1)S(1)}, u32[]{:S(2)}, u32[]{:S(2)}) collective-permute-start(bf16[128,1024]{1,0:T(8,128)(2,1)S(1)} %fusion.4), channel_id=1, source_target_pairs={{0,2},{1,3},{2,4},{3,5},{4,6},{5,7},{6,0},{7,1},{8,10},{9,11},{10,... | collective-permute-start | bytes 786440 | tf_op jit(solution)/shard_map/ppermute | solution.py:25
  154.9 0.2 collective-permute-done.8
  155.1 4.5 %collective-permute-done.7 = bf16[128,1024]{1,0:T(8,128)(2,1)S(1)} collective-permute-done((bf16[128,1024]{1,0:T(8,128)(2,1)S(1)}, bf16[128,1024]{1,0:T(8,128)(2,1)S(1)}, u32[]{:S(2)}, u32[]{:S(2)}) %collective-permute-start.7) | collective-permute-done | bytes 262176 | tf_op jit(solution)/shard_map/ppermute | solution.py:25
  159.6 2.6 %collective-permute-done.6 = bf16[128,1024]{1,0:T(8,128)(2,1)S(1)} collective-permute-done((bf16[128,1024]{1,0:T(8,128)(2,1)S(1)}, bf16[128,1024]{1,0:T(8,128)(2,1)S(1)}, u32[]{:S(2)}, u32[]{:S(2)}) %collective-permute-start.6) | collective-permute-done | bytes 262176 | tf_op jit(solution)/shard_map/ppermute | solution.py:25
  162.1 0.1 pad_maximum_fusion
  162.2 6.1 %collective-permute-start.9 = (bf16[512,1024]{1,0:T(8,128)(2,1)S(1)}, bf16[512,1024]{1,0:T(8,128)(2,1)}, u32[]{:S(2)}, u32[]{:S(2)}) collective-permute-start(bf16[512,1024]{1,0:T(8,128)(2,1)S(1)} %pad_maximum_fusion), channel_id=1, source_target_pairs={{0,1},{1,0},{2,3},{3,2},{4,5},{5,4},{6,7},{7,6},{8,9},{9,8},{10,11... | collective-permute-start | bytes 3145736 | tf_op jit(solution)/shard_map/ppermute | solution.py:25
  169.1 0.1 pad_add_fusion.1.ids
  169.1 0.7 convolution_convert_fusion.1.near
  169.8 0.9 collective-permute-done.9
  170.7 1.9 %convolution_convert_fusion.far = bf16[512,384]{1,0:T(8,128)(2,1)S(1)} fusion(bf16[512,1024]{1,0:T(8,128)(2,1)} %collective-permute-done.9, bf16[1024,384]{1,0:T(8,128)(2,1)S(1)} %bitcast.41), kind=kOutput, calls=%fused_computation | convolution fusion | flops 402849792 | bytes 2228224 | tf_op jit(solution)/shard_map/dot_general | solution.py:309
  172.7 3.7 %attention.1 = bf16[8,128,128]{2,1,0:T(8,128)(2,1)S(1)} custom-call(s32[8]{0:T(128)S(1)} %pad_add_fusion.1.ids, s32[1]{0:T(128)S(6)} %copy.56.train, bf16[512,384]{1,0:T(8,128)(2,1)S(1)} %convolution_convert_fusion.1.near, bf16[512,384]{1,0:T(8,128)(2,1)S(1)} %convolution_convert_fusion.far), custom_call_target="tpu_custom_call" | custom-call | tf_op jit(solution)/shard_map/attention/pallas_call | solution.py:201
  176.4 9.2 %all_to_all.25.pieces = bf16[8,128,128]{2,1,0:T(8,128)(2,1)S(1)} all-to-all(bf16[8,128,128]{2,1,0:T(8,128)(2,1)S(1)} %attention.1), channel_id=1, replica_groups=mesh['exp'=64,'ctx'=8] {'ctx'}, dimensions={0} | all-to-all | bytes 524288 | tf_op jit(solution)/shard_map/all_to_all | solution.py:20
  185.7 0.8 shard_map.134
  (38 shorter events, 0.4 us)
Async XLA Ops:
  0.6 22.3 %copy-start = (bf16[16,1024]{1,0:T(8,128)(2,1)S(1)}, bf16[16,1024]{1,0:T(8,128)(2,1)}, u32[]{:S(2)}) copy-start(bf16[16,1024]{1,0:T(8,128)(2,1)} %param.19) | copy-start | bytes 98308
  0.6 29.9 %copy-start.6 = (s32[128,16]{0,1:T(8,128)S(1)}, s32[128,16]{0,1:T(8,128)}, u32[]{:S(2)}) copy-start(s32[128,16]{0,1:T(8,128)} %param.13) | copy-start | bytes 24580
  0.7 1.0 copy-start.3
  1.6 0.7 copy-start.5
  3.7 56.2 %all-to-all-start = ((bf16[64,8,512]{2,1,0:T(8,128)(2,1)}), bf16[64,8,512]{2,1,0:T(8,128)(2,1)S(1)}, u32[]{:S(2)}, u32[]{:S(2)}) async-start(bf16[64,8,512]{2,1,0:T(8,128)(2,1)} %bitcast.3), calls=%async_computation | async-start | bytes 1048576 | tf_op jit(solution)/shard_map/all_to_all | solution.py:20
  23.7 22.2 %collective-permute-start = (bf16[16,384]{1,0:T(8,128)(2,1)S(1)}, bf16[16,384]{1,0:T(8,128)(2,1)S(1)}, u32[]{:S(2)}, u32[]{:S(2)}) collective-permute-start(bf16[16,384]{1,0:T(8,128)(2,1)S(1)} %get-tuple-element.25), channel_id=1, source_target_pairs={{0,32},{8,40},{16,48},{24,56},{32,0},{40,8},{48,16},{56,24},{64,96... | collective-permute-start | bytes 36872 | tf_op jit(solution)/shard_map/ppermute | solution.py:25
  45.9 13.9 %collective-permute-start.1 = (bf16[2,16,384]{2,1,0:T(8,128)(2,1)S(1)}, bf16[2,16,384]{2,1,0:T(8,128)(2,1)S(1)}, u32[]{:S(2)}, u32[]{:S(2)}) collective-permute-start(bf16[2,16,384]{2,1,0:T(8,128)(2,1)S(1)} %fusion.17), channel_id=1, source_target_pairs={{0,64},{8,72},{16,80},{24,88},{32,96},{40,104},{48,112},{56,120},{... | collective-permute-start | bytes 73736 | tf_op jit(solution)/shard_map/ppermute | solution.py:25
  59.9 26.3 %copy-start.2 = (bf16[2,1024,256]{2,1,0:T(8,128)(2,1)S(1)}, bf16[2,1024,256]{2,1,0:T(8,128)(2,1)}, u32[]{:S(2)}) copy-start(bf16[2,1024,256]{2,1,0:T(8,128)(2,1)} %up.1) | copy-start | bytes 3145732
  61.1 25.1 %copy-start.1 = (bf16[2,1024,256]{2,1,0:T(8,128)(2,1)S(1)}, bf16[2,1024,256]{2,1,0:T(8,128)(2,1)}, u32[]{:S(2)}) copy-start(bf16[2,1024,256]{2,1,0:T(8,128)(2,1)} %gate.1) | copy-start | bytes 3145732
  61.1 25.1 %all-to-all-start.1 = ((bf16[8,32,1024]{2,1,0:T(8,128)(2,1)}), bf16[8,32,1024]{2,1,0:T(8,128)(2,1)S(1)}, u32[]{:S(2)}, u32[]{:S(2)}) async-start(bf16[8,32,1024]{2,1,0:T(8,128)(2,1)} %shard_map.132), calls=%async_computation.1 | async-start | bytes 1048576 | tf_op jit(solution)/shard_map/all_to_all | solution.py:20
  71.4 5.2 %collective-permute-start.2 = (bf16[4,16,384]{2,1,0:T(8,128)(2,1)S(1)}, bf16[4,16,384]{2,1,0:T(8,128)(2,1)S(1)}, u32[]{:S(2)}, u32[]{:S(2)}) collective-permute-start(bf16[4,16,384]{2,1,0:T(8,128)(2,1)S(1)} %bitcast.44), channel_id=1, source_target_pairs={{0,8},{8,0},{16,24},{24,16},{32,40},{40,32},{48,56},{56,48},{64,72... | collective-permute-start | bytes 147464 | tf_op jit(solution)/shard_map/ppermute | solution.py:25
  76.6 9.4 %collective-permute-start.3 = (bf16[2,4,16,384]{3,2,0,1:T(8,128)(2,1)S(1)}, bf16[2,4,16,384]{3,2,0,1:T(8,128)(2,1)S(1)}, u32[]{:S(2)}, u32[]{:S(2)}) collective-permute-start(bf16[2,4,16,384]{3,2,0,1:T(8,128)(2,1)S(1)} %fusion.13), channel_id=1, source_target_pairs={{0,16},{8,24},{16,0},{24,8},{32,48},{40,56},{48,32},{56,40},{64,80... | collective-permute-start | bytes 294920 | tf_op jit(solution)/shard_map/ppermute | solution.py:25
  88.9 5.1 %copy-start.9 = (f32[2,16]{1,0:T(2,128)S(1)}, f32[2,16]{1,0:T(2,128)}, u32[]{:S(2)}) copy-start(f32[2,16]{1,0:T(2,128)} %param.14) | copy-start | bytes 388
  88.9 14.4 %all-to-all-start.2 = ((bf16[8,32,1024]{2,1,0:T(8,128)(2,1)}), bf16[8,32,1024]{2,1,0:T(8,128)(2,1)S(1)}, u32[]{:S(2)}, u32[]{:S(2)}) async-start(bf16[8,32,1024]{2,1,0:T(8,128)(2,1)} %experts.1), calls=%async_computation.2 | async-start | bytes 1048576 | tf_op jit(solution)/shard_map/all_to_all | solution.py:20
  104.5 40.7 %all-to-all-start.3 = ((bf16[64,8,512]{2,1,0:T(8,128)(2,1)}), bf16[64,8,512]{2,1,0:T(8,128)(2,1)S(1)}, u32[]{:S(2)}, u32[]{:S(2)}) async-start(bf16[64,8,512]{2,1,0:T(8,128)(2,1)} %bitcast.17), calls=%async_computation.3 | async-start | bytes 1048576 | tf_op jit(solution)/shard_map/all_to_all | solution.py:20
  116.4 7.8 %collective-permute-start.4 = (bf16[4,4,16,384]{3,2,1,0:T(8,128)(2,1)S(1)}, bf16[4,4,16,384]{3,2,1,0:T(8,128)(2,1)S(1)}, u32[]{:S(2)}, u32[]{:S(2)}) collective-permute-start(bf16[4,4,16,384]{3,2,1,0:T(8,128)(2,1)S(1)} %bitcast.37), channel_id=1, source_target_pairs={{0,128},{8,136},{16,144},{24,152},{32,160},{40,168},{48,176},{56,1... | collective-permute-start | bytes 589832 | tf_op jit(solution)/shard_map/ppermute | solution.py:25
  124.5 14.9 %collective-permute-start.5 = (bf16[2,4,4,16,384]{4,3,2,1,0:T(8,128)(2,1)S(1)}, bf16[2,4,4,16,384]{4,3,2,1,0:T(8,128)(2,1)S(1)}, u32[]{:S(2)}, u32[]{:S(2)}) collective-permute-start(bf16[2,4,4,16,384]{4,3,2,1,0:T(8,128)(2,1)S(1)} %fusion.8), channel_id=1, source_target_pairs={{0,256},{8,264},{16,272},{24,280},{32,288},{40,296},{48,304},{56,3... | collective-permute-start | bytes 1179656 | tf_op jit(solution)/shard_map/ppermute | solution.py:25
  145.2 1.0 copy-start.4
  145.6 0.7 copy-start.8
  146.3 15.9 %copy-start.7 = (bf16[128,1024]{1,0:T(8,128)(2,1)}, bf16[128,1024]{1,0:T(8,128)(2,1)S(1)}, u32[]{:S(2)}) copy-start(bf16[128,1024]{1,0:T(8,128)(2,1)S(1)} %get-tuple-element.17) | copy-start | bytes 786436
  146.5 22.6 %copy-start.10 = (s32[4]{0:T(128)S(1)}, s32[4]{0:T(128)}, u32[]{:S(2)}) copy-start(s32[4]{0:T(128)} %constant.174.clone) | copy-start | bytes 52
  146.5 8.6 %collective-permute-start.8 = (bf16[128,1024]{1,0:T(8,128)(2,1)S(1)}, bf16[128,1024]{1,0:T(8,128)(2,1)S(1)}, u32[]{:S(2)}, u32[]{:S(2)}) collective-permute-start(bf16[128,1024]{1,0:T(8,128)(2,1)S(1)} %fusion.4), channel_id=1, source_target_pairs={{0,4},{1,5},{2,6},{3,7},{4,0},{5,1},{6,2},{7,3},{8,12},{9,13},{10,... | collective-permute-start | bytes 786440 | tf_op jit(solution)/shard_map/ppermute | solution.py:25
  149.1 10.5 %collective-permute-start.7 = (bf16[128,1024]{1,0:T(8,128)(2,1)S(1)}, bf16[128,1024]{1,0:T(8,128)(2,1)S(1)}, u32[]{:S(2)}, u32[]{:S(2)}) collective-permute-start(bf16[128,1024]{1,0:T(8,128)(2,1)S(1)} %fusion.4), channel_id=1, source_target_pairs={{0,6},{1,7},{2,0},{3,1},{4,2},{5,3},{6,4},{7,5},{8,14},{9,15},{10,... | collective-permute-start | bytes 786440 | tf_op jit(solution)/shard_map/ppermute | solution.py:25
  153.0 9.2 %collective-permute-start.6 = (bf16[128,1024]{1,0:T(8,128)(2,1)S(1)}, bf16[128,1024]{1,0:T(8,128)(2,1)S(1)}, u32[]{:S(2)}, u32[]{:S(2)}) collective-permute-start(bf16[128,1024]{1,0:T(8,128)(2,1)S(1)} %fusion.4), channel_id=1, source_target_pairs={{0,2},{1,3},{2,4},{3,5},{4,6},{5,7},{6,0},{7,1},{8,10},{9,11},{10,... | collective-permute-start | bytes 786440 | tf_op jit(solution)/shard_map/ppermute | solution.py:25
  162.2 8.5 %collective-permute-start.9 = (bf16[512,1024]{1,0:T(8,128)(2,1)S(1)}, bf16[512,1024]{1,0:T(8,128)(2,1)}, u32[]{:S(2)}, u32[]{:S(2)}) collective-permute-start(bf16[512,1024]{1,0:T(8,128)(2,1)S(1)} %pad_maximum_fusion), channel_id=1, source_target_pairs={{0,1},{1,0},{2,3},{3,2},{4,5},{5,4},{6,7},{7,6},{8,9},{9,8},{10,11... | collective-permute-start | bytes 3145736 | tf_op jit(solution)/shard_map/ppermute | solution.py:25

commit v5 on v4

--- a/solution.py
+++ b/solution.py
@@ -33,16 +33,16 @@
     return shift(v, "ctx", lambda i: i ^ 1)
 
 
-def gather_pair(v, index, stride):
-    other = shift(v, "exp", lambda i: i ^ stride)
-    turned = jnp.stack([other, v, other])
-    return lax.dynamic_slice_in_dim(turned, 1 - index // stride % 2, 2, 0)
-
-
-def gather_four(v, index, stride):
-    pair = gather_pair(v, index, stride)
-    four = gather_pair(pair, index, 2 * stride)
-    return four.reshape(4, *v.shape)
+def gather_four(v, digit, stride):
+    def move(step):
+        return lambda i: i + ((i // stride + step) % 4 - i // stride % 4) * stride
+
+    others = []
+    for step in (1, 2, 3):
+        others.append(shift(v, "exp", move(step)))
+    one, two, three = others
+    turned = jnp.stack([three, two, one, v, three, two, one])
+    return lax.dynamic_slice_in_dim(turned, 3 - digit, 4, 0)
 
 
 def whole(memory, count):
@@ -57,6 +57,10 @@
         out_specs=pl.BlockSpec(memory_space=pltpu.VMEM),
         compiler_params=pltpu.CompilerParams(vmem_limit_bytes=8 * 2**20),
     )(*arrays)
+
+
+def in_hbm(v):
+    return pltpu.with_memory_space_constraint(v, pltpu.HBM)
 
 
 def take_kernel(block, selected, inputs, out):
@@ -153,7 +157,7 @@
         ],
         compiler_params=pltpu.CompilerParams(vmem_limit_bytes=12 * 2**20),
         name="experts",
-    )(chosen, gate, up, pltpu.with_memory_space_constraint(down, pltpu.HBM))
+    )(chosen, gate, up, in_hbm(down))
 
 
 def attention_kernel(ids, train, near, far, out, queries, keys, values):
@@ -247,10 +251,11 @@
     half = model_width // 2
     sent = (exp_count, 2 * experts * MOST, half)
     flat = jax.ShapeDtypeStruct((sent[0] * sent[1], half), inputs.dtype)
-    outgoing = small_kernel(take_kernel, flat, own_block.reshape(1), selected.T, inputs, scalars=1)
+    outgoing = small_kernel(
+        take_kernel, flat, own_block.reshape(1), in_hbm(selected.T), in_hbm(inputs), scalars=1
+    )
     arrived = exchange(outgoing.reshape(sent), "exp").reshape(flat.shape)
-    quarter = gather_four(piece, exp_index, 4)
-    arrived, quarter = lax.optimization_barrier((arrived, quarter))
+    quarter = gather_four(piece, exp_index // 4 % 4, 4)
 
     taken = selected.reshape(exp_count, experts, group_take) - own_block * row_count
     mine = (taken >= 0) & (taken < row_count)
@@ -279,14 +284,13 @@
     )
     compact = small_kernel(fill_kernel, chosen_shape, my_place.reshape(-1, 1), arrived)
     chosen = exchange(compact, "ctx")
-    layer = jnp.moveaxis(gather_four(quarter, exp_index, 1), 0, 1)
-    chosen, layer = lax.optimization_barrier((chosen, layer))
+    layer = jnp.moveaxis(gather_four(quarter, exp_index % 4, 1), 0, 1)
     partials = expert_parts(chosen, gate_weight, up_weight, down_weight)
     parts = exchange(partials, "ctx")
     reply = small_kernel(reply_kernel, flat, my_place.reshape(1, -1), gates, parts)
+    reply, layer = lax.optimization_barrier((reply, layer))
     returned = exchange(reply.reshape(sent), "exp").reshape(flat.shape)
-    weight_rows = gather_four(layer, exp_index, N_Z).reshape(model_width, -1)
-    returned, weight_rows = lax.optimization_barrier((returned, weight_rows))
+    weight_rows = gather_four(layer, exp_index // N_Z, N_Z).reshape(model_width, -1)
     sums = lax.dot_general(
         owner_hit, returned, (((0,), (0,)), ((), ())), preferred_element_type=jnp.float32
     )

time: 187 us -> 184 us (0.984)
    all_to_all x4, waiting for transfers between devices: 14.5 us -> 34.5 us  [exchange(): return lax.all_to_all(blocks, axis, split_axis=0, concat_axis=0, tiled=True)]
    ppermute x10 -> x13, waiting for transfers between devices: 49.2 us -> 29.5 us  [shift(): return lax.ppermute(v, axis, [(i, move(i)) for i in range(count)])]
    all_to_all x4, starting transfers between devices: 45.9 us -> 31.1 us  [exchange(): return lax.all_to_all(blocks, axis, split_axis=0, concat_axis=0, tiled=True)]
    ppermute x10 -> x13, starting transfers between devices: 45.5 us -> 58.5 us  [shift(): return lax.ppermute(v, axis, [(i, move(i)) for i in range(count)])]
  transfers between devices with their start and end apart: 14 -> 17, of which waited for: 12 -> 11; matrix products, arithmetic and copies ran while one was open for 2% -> 2% of each run, Pallas kernels for 0% -> 2%
where the time goes in v5:
time: 184 us; the launch traced here: 183 us
  starting transfers between devices  89.6 us (49%)
  waiting for transfers between devices  64 us (35%)
  Pallas kernels  11.9 us (6%)
  blocking collectives  9.25 us (5%)
  local copies, waits for them, and re-layouts  3.15 us (2%)
  between operations  1.93 us (1%)
  matrix products  1.87 us (1%)
    ppermute x13, starting transfers between devices, shift(): return lax.ppermute(v, axis, [(i, move(i)) for i in range(count)])  58.5 us
    all_to_all x4, waiting for transfers between devices, exchange(): return lax.all_to_all(blocks, axis, split_axis=0, concat_axis=0, tiled=True)  34.5 us
    all_to_all x4, starting transfers between devices, exchange(): return lax.all_to_all(blocks, axis, split_axis=0, concat_axis=0, tiled=True)  31.1 us
    ppermute x13, waiting for transfers between devices, shift(): return lax.ppermute(v, axis, [(i, move(i)) for i in range(count)])  29.5 us
    all_to_all x1, blocking collectives, exchange(): return lax.all_to_all(blocks, axis, split_axis=0, concat_axis=0, tiled=True)  9.25 us
    pallas_call x4, Pallas kernels, small_kernel(): pl.pallas_call(body, out_shape=outs, in_specs=whole(pltpu.SMEM, scalars)...  5.56 us
    pallas_call x1, Pallas kernels, attention(): pl.pallas_call(attention_kernel, out_shape=jax.ShapeDtypeStruct((chunks,...  3.73 us
  transfers between devices with their start and end apart: 17, of which 11 were waited for; matrix products, arithmetic and copies ran while one was open for 2% of the time, Pallas kernels for 2%

profile of v5, /device:TPU:1, one launch (start us, length us, event | category | flops | bytes accessed | tf_op | source)
XLA Modules:
  0.0 182.6 jit_solution(4181525477608366198)
XLA Ops:
  0.6 0.0 copy-start
  0.7 0.7 copy-done
  1.4 0.7 constant_dynamic-slice_fusion.2
  2.1 13.3 %collective-permute-start = (bf16[16,384]{1,0:T(8,128)(2,1)S(1)}, bf16[16,384]{1,0:T(8,128)(2,1)S(1)}, u32[]{:S(2)}, u32[]{:S(2)}) collective-permute-start(bf16[16,384]{1,0:T(8,128)(2,1)S(1)} %pad_maximum_fusion.1), channel_id=1, source_target_pairs={{0,96},{8,104},{16,112},{24,120},{32,0},{40,8},{48,16},{56,24},{64... | collective-permute-start | bytes 36872 | tf_op jit(solution)/shard_map/ppermute | solution.py:25
  15.4 4.9 %collective-permute-start.1 = (bf16[16,384]{1,0:T(8,128)(2,1)S(1)}, bf16[16,384]{1,0:T(8,128)(2,1)S(1)}, u32[]{:S(2)}, u32[]{:S(2)}) collective-permute-start(bf16[16,384]{1,0:T(8,128)(2,1)S(1)} %pad_maximum_fusion.1), channel_id=1, source_target_pairs={{0,64},{8,72},{16,80},{24,88},{32,96},{40,104},{48,112},{56,120},{... | collective-permute-start | bytes 36872 | tf_op jit(solution)/shard_map/ppermute | solution.py:25
  20.3 7.3 %collective-permute-start.2 = (bf16[16,384]{1,0:T(8,128)(2,1)S(1)}, bf16[16,384]{1,0:T(8,128)(2,1)S(1)}, u32[]{:S(2)}, u32[]{:S(2)}) collective-permute-start(bf16[16,384]{1,0:T(8,128)(2,1)S(1)} %pad_maximum_fusion.1), channel_id=1, source_target_pairs={{0,32},{8,40},{16,48},{24,56},{32,64},{40,72},{48,80},{56,88},{64,... | collective-permute-start | bytes 36872 | tf_op jit(solution)/shard_map/ppermute | solution.py:25
  27.6 2.3 %shard_map.131 = bf16[512,512]{1,0:T(8,128)(2,1)} custom-call(s32[1]{0:T(128)} %bitcast.1.block, s32[16,128]{1,0:T(8,128)} %bitcast.57, bf16[128,1024]{1,0:T(8,128)(2,1)} %inputs.1), custom_call_target="tpu_custom_call" | custom-call | tf_op jit(solution)/shard_map/pallas_call | solution.py:53
  29.9 8.4 %all-to-all-start = ((bf16[64,8,512]{2,1,0:T(8,128)(2,1)}), bf16[64,8,512]{2,1,0:T(8,128)(2,1)S(1)}, u32[]{:S(2)}, u32[]{:S(2)}) async-start(bf16[64,8,512]{2,1,0:T(8,128)(2,1)} %bitcast.3), calls=%async_computation | async-start | bytes 1048576 | tf_op jit(solution)/shard_map/all_to_all | solution.py:20
  38.3 0.1 constant_dynamic-slice_fusion.5
  38.4 0.1 copy.64
  38.5 0.2 convert_reduce_fusion
  38.9 0.0 copy-start.1
  38.9 4.8 %collective-permute-start.3 = (bf16[4,16,384]{2,1,0:T(8,128)(2,1)S(1)}, bf16[4,16,384]{2,1,0:T(8,128)(2,1)S(1)}, u32[]{:S(2)}, u32[]{:S(2)}) collective-permute-start(bf16[4,16,384]{2,1,0:T(8,128)(2,1)S(1)} %constant_dynamic-slice_fusion.1), channel_id=1, source_target_pairs={{0,24},{8,0},{16,8},{24,16},{32,56},{40,32},{48,40},{56,48},{64,88... | collective-permute-start | bytes 147464 | tf_op jit(solution)/shard_map/ppermute | solution.py:25
  43.8 0.1 add_add_fusion
  43.8 0.1 reshape_reshape.6.place
  43.9 0.1 reshape_reshape.8.place
  44.0 0.1 reshape.142.gate
  44.1 1.9 %collective-permute-start.4 = (bf16[4,16,384]{2,1,0:T(8,128)(2,1)S(1)}, bf16[4,16,384]{2,1,0:T(8,128)(2,1)S(1)}, u32[]{:S(2)}, u32[]{:S(2)}) collective-permute-start(bf16[4,16,384]{2,1,0:T(8,128)(2,1)S(1)} %constant_dynamic-slice_fusion.1), channel_id=1, source_target_pairs={{0,16},{8,24},{16,0},{24,8},{32,48},{40,56},{48,32},{56,40},{64,80... | collective-permute-start | bytes 147464 | tf_op jit(solution)/shard_map/ppermute | solution.py:25
  46.0 2.5 %collective-permute-start.5 = (bf16[4,16,384]{2,1,0:T(8,128)(2,1)S(1)}, bf16[4,16,384]{2,1,0:T(8,128)(2,1)S(1)}, u32[]{:S(2)}, u32[]{:S(2)}) collective-permute-start(bf16[4,16,384]{2,1,0:T(8,128)(2,1)S(1)} %constant_dynamic-slice_fusion.1), channel_id=1, source_target_pairs={{0,8},{8,16},{16,24},{24,0},{32,40},{40,48},{48,56},{56,32},{64,72... | collective-permute-start | bytes 147464 | tf_op jit(solution)/shard_map/ppermute | solution.py:25
  48.5 10.5 %collective-permute-done.3 = bf16[4,16,384]{2,1,0:T(8,128)(2,1)S(1)} collective-permute-done((bf16[4,16,384]{2,1,0:T(8,128)(2,1)S(1)}, bf16[4,16,384]{2,1,0:T(8,128)(2,1)S(1)}, u32[]{:S(2)}, u32[]{:S(2)}) %collective-permute-start.3) | collective-permute-done | bytes 49184 | tf_op jit(solution)/shard_map/ppermute | solution.py:25
  59.0 5.9 %collective-permute-done.4 = bf16[4,16,384]{2,1,0:T(8,128)(2,1)S(1)} collective-permute-done((bf16[4,16,384]{2,1,0:T(8,128)(2,1)S(1)}, bf16[4,16,384]{2,1,0:T(8,128)(2,1)S(1)}, u32[]{:S(2)}, u32[]{:S(2)}) %collective-permute-start.4) | collective-permute-done | bytes 49184 | tf_op jit(solution)/shard_map/ppermute | solution.py:25
  64.9 2.5 %all-to-all-done = bf16[64,8,512]{2,1,0:T(8,128)(2,1)S(1)} async-done(((bf16[64,8,512]{2,1,0:T(8,128)(2,1)}), bf16[64,8,512]{2,1,0:T(8,128)(2,1)S(1)}, u32[]{:S(2)}, u32[]{:S(2)}) %all-to-all-start) | async-done | bytes 524320 | tf_op jit(solution)/shard_map/all_to_all | solution.py:20
  67.3 1.2 shard_map.132
  68.5 8.8 %all-to-all-start.1 = ((bf16[8,32,1024]{2,1,0:T(8,128)(2,1)}), bf16[8,32,1024]{2,1,0:T(8,128)(2,1)S(1)}, u32[]{:S(2)}, u32[]{:S(2)}) async-start(bf16[8,32,1024]{2,1,0:T(8,128)(2,1)} %shard_map.132), calls=%async_computation.1 | async-start | bytes 1048576 | tf_op jit(solution)/shard_map/all_to_all | solution.py:20
  77.4 9.3 %all-to-all-done.1.chosen = bf16[8,32,1024]{2,1,0:T(8,128)(2,1)S(1)} async-done(((bf16[8,32,1024]{2,1,0:T(8,128)(2,1)}), bf16[8,32,1024]{2,1,0:T(8,128)(2,1)S(1)}, u32[]{:S(2)}, u32[]{:S(2)}) %all-to-all-start.1) | async-done | bytes 524320 | tf_op jit(solution)/shard_map/all_to_all | solution.py:20
  86.7 2.6 %experts.1 = bf16[8,32,1024]{2,1,0:T(8,128)(2,1)} custom-call(bf16[8,32,1024]{2,1,0:T(8,128)(2,1)S(1)} %all-to-all-done.1.chosen, bf16[2,1024,256]{2,1,0:T(8,128)(2,1)S(1)} %copy-done.1, bf16[2,1024,256]{2,1,0:T(8,128)(2,1)S(1)} %copy-done.2, bf16[2,256,1024]{2,1,0:T(8,128)(2,1)} %down.1), custom_call_target="tpu_custom_call" | custom-call | tf_op jit(solution)/shard_map/experts/pallas_call | solution.py:149
  89.4 4.4 %all-to-all-start.2 = ((bf16[8,32,1024]{2,1,0:T(8,128)(2,1)}), bf16[8,32,1024]{2,1,0:T(8,128)(2,1)S(1)}, u32[]{:S(2)}, u32[]{:S(2)}) async-start(bf16[8,32,1024]{2,1,0:T(8,128)(2,1)} %experts.1), calls=%async_computation.2 | async-start | bytes 1048576 | tf_op jit(solution)/shard_map/all_to_all | solution.py:20
  93.8 0.0 copy-start.8
  93.8 9.3 %all-to-all-done.2.parts = bf16[8,32,1024]{2,1,0:T(8,128)(2,1)S(1)} async-done(((bf16[8,32,1024]{2,1,0:T(8,128)(2,1)}), bf16[8,32,1024]{2,1,0:T(8,128)(2,1)S(1)}, u32[]{:S(2)}, u32[]{:S(2)}) %all-to-all-start.2) | async-done | bytes 524320 | tf_op jit(solution)/shard_map/all_to_all | solution.py:20
  103.1 1.3 shard_map.133
  104.4 9.5 %all-to-all-start.3 = ((bf16[64,8,512]{2,1,0:T(8,128)(2,1)}), bf16[64,8,512]{2,1,0:T(8,128)(2,1)S(1)}, u32[]{:S(2)}, u32[]{:S(2)}) async-start(bf16[64,8,512]{2,1,0:T(8,128)(2,1)} %bitcast.18), calls=%async_computation.3 | async-start | bytes 1048576 | tf_op jit(solution)/shard_map/all_to_all | solution.py:20
  113.9 0.1 reduce_min.12
  114.1 0.1 reduce_max.12
  114.2 0.1 copy.54
  114.3 0.1 copy.53
  114.4 0.1 copy.56
  114.5 0.1 copy.55
  114.7 0.1 add_select_fusion
  114.8 4.3 %collective-permute-start.9 = (bf16[4,4,16,384]{3,2,1,0:T(8,128)(2,1)S(1)}, bf16[4,4,16,384]{3,2,1,0:T(8,128)(2,1)S(1)}, u32[]{:S(2)}, u32[]{:S(2)}) collective-permute-start(bf16[4,4,16,384]{3,2,1,0:T(8,128)(2,1)S(1)} %dynamic-slice_bitcast_fusion), channel_id=1, source_target_pairs={{0,384},{8,392},{16,400},{24,408},{32,416},{40,424},{48,432},{56,4... | collective-permute-start | bytes 589832 | tf_op jit(solution)/shard_map/ppermute | solution.py:25
  119.1 0.1 select_n.99
  119.9 0.1 pad_add_fusion.1.ids
  120.0 2.4 %collective-permute-start.10 = (bf16[4,4,16,384]{3,2,1,0:T(8,128)(2,1)S(1)}, bf16[4,4,16,384]{3,2,1,0:T(8,128)(2,1)S(1)}, u32[]{:S(2)}, u32[]{:S(2)}) collective-permute-start(bf16[4,4,16,384]{3,2,1,0:T(8,128)(2,1)S(1)} %dynamic-slice_bitcast_fusion), channel_id=1, source_target_pairs={{0,256},{8,264},{16,272},{24,280},{32,288},{40,296},{48,304},{56,3... | collective-permute-start | bytes 589832 | tf_op jit(solution)/shard_map/ppermute | solution.py:25
  122.4 2.6 %collective-permute-start.11 = (bf16[4,4,16,384]{3,2,1,0:T(8,128)(2,1)S(1)}, bf16[4,4,16,384]{3,2,1,0:T(8,128)(2,1)S(1)}, u32[]{:S(2)}, u32[]{:S(2)}) collective-permute-start(bf16[4,4,16,384]{3,2,1,0:T(8,128)(2,1)S(1)} %dynamic-slice_bitcast_fusion), channel_id=1, source_target_pairs={{0,128},{8,136},{16,144},{24,152},{32,160},{40,168},{48,176},{56,1... | collective-permute-start | bytes 589832 | tf_op jit(solution)/shard_map/ppermute | solution.py:25
  125.1 4.7 %collective-permute-done.10 = bf16[4,4,16,384]{3,2,1,0:T(8,128)(2,1)S(1)} collective-permute-done((bf16[4,4,16,384]{3,2,1,0:T(8,128)(2,1)S(1)}, bf16[4,4,16,384]{3,2,1,0:T(8,128)(2,1)S(1)}, u32[]{:S(2)}, u32[]{:S(2)}) %collective-permute-start.10) | collective-permute-done | bytes 196640 | tf_op jit(solution)/shard_map/ppermute | solution.py:25
  129.8 0.0 copy-start.6
  129.8 13.4 %all-to-all-done.3 = bf16[64,8,512]{2,1,0:T(8,128)(2,1)S(1)} async-done(((bf16[64,8,512]{2,1,0:T(8,128)(2,1)}), bf16[64,8,512]{2,1,0:T(8,128)(2,1)S(1)}, u32[]{:S(2)}, u32[]{:S(2)}) %all-to-all-start.3) | async-done | bytes 524320 | tf_op jit(solution)/shard_map/all_to_all | solution.py:20
  143.2 0.4 fusion.4
  143.7 0.2 fusion
  143.9 0.1 fusion.2
  144.0 2.5 %collective-permute-start.8 = (bf16[128,1024]{1,0:T(8,128)(2,1)S(1)}, bf16[128,1024]{1,0:T(8,128)(2,1)S(1)}, u32[]{:S(2)}, u32[]{:S(2)}) collective-permute-start(bf16[128,1024]{1,0:T(8,128)(2,1)S(1)} %fusion.2), channel_id=1, source_target_pairs={{0,4},{1,5},{2,6},{3,7},{4,0},{5,1},{6,2},{7,3},{8,12},{9,13},{10,... | collective-permute-start | bytes 786440 | tf_op jit(solution)/shard_map/ppermute | solution.py:25
  146.6 4.0 %collective-permute-start.7 = (bf16[128,1024]{1,0:T(8,128)(2,1)S(1)}, bf16[128,1024]{1,0:T(8,128)(2,1)S(1)}, u32[]{:S(2)}, u32[]{:S(2)}) collective-permute-start(bf16[128,1024]{1,0:T(8,128)(2,1)S(1)} %fusion.2), channel_id=1, source_target_pairs={{0,6},{1,7},{2,0},{3,1},{4,2},{5,3},{6,4},{7,5},{8,14},{9,15},{10,... | collective-permute-start | bytes 786440 | tf_op jit(solution)/shard_map/ppermute | solution.py:25
  150.5 1.9 %collective-permute-start.6 = (bf16[128,1024]{1,0:T(8,128)(2,1)S(1)}, bf16[128,1024]{1,0:T(8,128)(2,1)S(1)}, u32[]{:S(2)}, u32[]{:S(2)}) collective-permute-start(bf16[128,1024]{1,0:T(8,128)(2,1)S(1)} %fusion.2), channel_id=1, source_target_pairs={{0,2},{1,3},{2,4},{3,5},{4,6},{5,7},{6,0},{7,1},{8,10},{9,11},{10,... | collective-permute-start | bytes 786440 | tf_op jit(solution)/shard_map/ppermute | solution.py:25
  152.6 0.1 collective-permute-done.8
  152.7 4.4 %collective-permute-done.7 = bf16[128,1024]{1,0:T(8,128)(2,1)S(1)} collective-permute-done((bf16[128,1024]{1,0:T(8,128)(2,1)S(1)}, bf16[128,1024]{1,0:T(8,128)(2,1)S(1)}, u32[]{:S(2)}, u32[]{:S(2)}) %collective-permute-start.7) | collective-permute-done | bytes 262176 | tf_op jit(solution)/shard_map/ppermute | solution.py:25
  157.1 2.6 %collective-permute-done.6 = bf16[128,1024]{1,0:T(8,128)(2,1)S(1)} collective-permute-done((bf16[128,1024]{1,0:T(8,128)(2,1)S(1)}, bf16[128,1024]{1,0:T(8,128)(2,1)S(1)}, u32[]{:S(2)}, u32[]{:S(2)}) %collective-permute-start.6) | collective-permute-done | bytes 262176 | tf_op jit(solution)/shard_map/ppermute | solution.py:25
  159.7 0.1 pad_maximum_fusion
  159.8 6.1 %collective-permute-start.12 = (bf16[512,1024]{1,0:T(8,128)(2,1)S(1)}, bf16[512,1024]{1,0:T(8,128)(2,1)S(1)}, u32[]{:S(2)}, u32[]{:S(2)}) collective-permute-start(bf16[512,1024]{1,0:T(8,128)(2,1)S(1)} %pad_maximum_fusion), channel_id=1, source_target_pairs={{0,1},{1,0},{2,3},{3,2},{4,5},{5,4},{6,7},{7,6},{8,9},{9,8},{10,11... | collective-permute-start | bytes 3145736 | tf_op jit(solution)/shard_map/ppermute | solution.py:25
  166.0 0.1 constant_dynamic-slice_fusion
  166.1 0.7 convolution_convert_fusion.1.near
  166.8 1.3 collective-permute-done.12
  168.2 0.7 convolution_convert_fusion.far
  168.9 3.7 %attention.1 = bf16[8,128,128]{2,1,0:T(8,128)(2,1)S(1)} custom-call(s32[8]{0:T(128)S(1)} %pad_add_fusion.1.ids, s32[1]{0:T(128)S(6)} %copy.83.train, bf16[512,384]{1,0:T(8,128)(2,1)S(1)} %convolution_convert_fusion.1.near, bf16[512,384]{1,0:T(8,128)(2,1)S(1)} %convolution_convert_fusion.far), custom_call_target="tpu_custom_call" | custom-call | tf_op jit(solution)/shard_map/attention/pallas_call | solution.py:205
  172.6 9.2 %all_to_all.25.pieces = bf16[8,128,128]{2,1,0:T(8,128)(2,1)S(1)} all-to-all(bf16[8,128,128]{2,1,0:T(8,128)(2,1)S(1)} %attention.1), channel_id=1, replica_groups=mesh['exp'=64,'ctx'=8] {'ctx'}, dimensions={0} | all-to-all | bytes 524288 | tf_op jit(solution)/shard_map/all_to_all | solution.py:20
  181.9 0.8 shard_map.134
  (55 shorter events, 0.6 us)
Async XLA Ops:
  0.6 0.8 copy-start
  0.6 37.7 %copy-start.5 = (s32[128,16]{0,1:T(8,128)S(1)}, s32[128,16]{0,1:T(8,128)}, u32[]{:S(2)}) copy-start(s32[128,16]{0,1:T(8,128)} %param.13) | copy-start | bytes 24580
  0.7 43.4 %copy-start.7 = (f32[2,16]{1,0:T(2,128)S(1)}, f32[2,16]{1,0:T(2,128)}, u32[]{:S(2)}) copy-start(f32[2,16]{1,0:T(2,128)} %param.14) | copy-start | bytes 388
  2.1 36.6 %collective-permute-start = (bf16[16,384]{1,0:T(8,128)(2,1)S(1)}, bf16[16,384]{1,0:T(8,128)(2,1)S(1)}, u32[]{:S(2)}, u32[]{:S(2)}) collective-permute-start(bf16[16,384]{1,0:T(8,128)(2,1)S(1)} %pad_maximum_fusion.1), channel_id=1, source_target_pairs={{0,96},{8,104},{16,112},{24,120},{32,0},{40,8},{48,16},{56,24},{64... | collective-permute-start | bytes 36872 | tf_op jit(solution)/shard_map/ppermute | solution.py:25
  15.4 23.4 %collective-permute-start.1 = (bf16[16,384]{1,0:T(8,128)(2,1)S(1)}, bf16[16,384]{1,0:T(8,128)(2,1)S(1)}, u32[]{:S(2)}, u32[]{:S(2)}) collective-permute-start(bf16[16,384]{1,0:T(8,128)(2,1)S(1)} %pad_maximum_fusion.1), channel_id=1, source_target_pairs={{0,64},{8,72},{16,80},{24,88},{32,96},{40,104},{48,112},{56,120},{... | collective-permute-start | bytes 36872 | tf_op jit(solution)/shard_map/ppermute | solution.py:25
  20.3 18.5 %collective-permute-start.2 = (bf16[16,384]{1,0:T(8,128)(2,1)S(1)}, bf16[16,384]{1,0:T(8,128)(2,1)S(1)}, u32[]{:S(2)}, u32[]{:S(2)}) collective-permute-start(bf16[16,384]{1,0:T(8,128)(2,1)S(1)} %pad_maximum_fusion.1), channel_id=1, source_target_pairs={{0,32},{8,40},{16,48},{24,56},{32,64},{40,72},{48,80},{56,88},{64,... | collective-permute-start | bytes 36872 | tf_op jit(solution)/shard_map/ppermute | solution.py:25
  29.9 37.4 %all-to-all-start = ((bf16[64,8,512]{2,1,0:T(8,128)(2,1)}), bf16[64,8,512]{2,1,0:T(8,128)(2,1)S(1)}, u32[]{:S(2)}, u32[]{:S(2)}) async-start(bf16[64,8,512]{2,1,0:T(8,128)(2,1)} %bitcast.3), calls=%async_computation | async-start | bytes 1048576 | tf_op jit(solution)/shard_map/all_to_all | solution.py:20
  38.9 47.8 %copy-start.1 = (bf16[2,1024,256]{2,1,0:T(8,128)(2,1)S(1)}, bf16[2,1024,256]{2,1,0:T(8,128)(2,1)}, u32[]{:S(2)}) copy-start(bf16[2,1024,256]{2,1,0:T(8,128)(2,1)} %gate.1) | copy-start | bytes 3145732
  38.9 47.8 %copy-start.2 = (bf16[2,1024,256]{2,1,0:T(8,128)(2,1)S(1)}, bf16[2,1024,256]{2,1,0:T(8,128)(2,1)}, u32[]{:S(2)}) copy-start(bf16[2,1024,256]{2,1,0:T(8,128)(2,1)} %up.1) | copy-start | bytes 3145732
  38.9 20.1 %collective-permute-start.3 = (bf16[4,16,384]{2,1,0:T(8,128)(2,1)S(1)}, bf16[4,16,384]{2,1,0:T(8,128)(2,1)S(1)}, u32[]{:S(2)}, u32[]{:S(2)}) collective-permute-start(bf16[4,16,384]{2,1,0:T(8,128)(2,1)S(1)} %constant_dynamic-slice_fusion.1), channel_id=1, source_target_pairs={{0,24},{8,0},{16,8},{24,16},{32,56},{40,32},{48,40},{56,48},{64,88... | collective-permute-start | bytes 147464 | tf_op jit(solution)/shard_map/ppermute | solution.py:25
  44.1 20.8 %collective-permute-start.4 = (bf16[4,16,384]{2,1,0:T(8,128)(2,1)S(1)}, bf16[4,16,384]{2,1,0:T(8,128)(2,1)S(1)}, u32[]{:S(2)}, u32[]{:S(2)}) collective-permute-start(bf16[4,16,384]{2,1,0:T(8,128)(2,1)S(1)} %constant_dynamic-slice_fusion.1), channel_id=1, source_target_pairs={{0,16},{8,24},{16,0},{24,8},{32,48},{40,56},{48,32},{56,40},{64,80... | collective-permute-start | bytes 147464 | tf_op jit(solution)/shard_map/ppermute | solution.py:25
  46.0 31.3 %collective-permute-start.5 = (bf16[4,16,384]{2,1,0:T(8,128)(2,1)S(1)}, bf16[4,16,384]{2,1,0:T(8,128)(2,1)S(1)}, u32[]{:S(2)}, u32[]{:S(2)}) collective-permute-start(bf16[4,16,384]{2,1,0:T(8,128)(2,1)S(1)} %constant_dynamic-slice_fusion.1), channel_id=1, source_target_pairs={{0,8},{8,16},{16,24},{24,0},{32,40},{40,48},{48,56},{56,32},{64,72... | collective-permute-start | bytes 147464 | tf_op jit(solution)/shard_map/ppermute | solution.py:25
  68.5 18.2 %all-to-all-start.1 = ((bf16[8,32,1024]{2,1,0:T(8,128)(2,1)}), bf16[8,32,1024]{2,1,0:T(8,128)(2,1)S(1)}, u32[]{:S(2)}, u32[]{:S(2)}) async-start(bf16[8,32,1024]{2,1,0:T(8,128)(2,1)} %shard_map.132), calls=%async_computation.1 | async-start | bytes 1048576 | tf_op jit(solution)/shard_map/all_to_all | solution.py:20
  89.4 13.7 %all-to-all-start.2 = ((bf16[8,32,1024]{2,1,0:T(8,128)(2,1)}), bf16[8,32,1024]{2,1,0:T(8,128)(2,1)S(1)}, u32[]{:S(2)}, u32[]{:S(2)}) async-start(bf16[8,32,1024]{2,1,0:T(8,128)(2,1)} %experts.1), calls=%async_computation.2 | async-start | bytes 1048576 | tf_op jit(solution)/shard_map/all_to_all | solution.py:20
  93.8 20.9 %copy-start.8 = (s32[4]{0:T(128)S(1)}, s32[4]{0:T(128)}, u32[]{:S(2)}) copy-start(s32[4]{0:T(128)} %constant.120.clone) | copy-start | bytes 52
  104.4 38.8 %all-to-all-start.3 = ((bf16[64,8,512]{2,1,0:T(8,128)(2,1)}), bf16[64,8,512]{2,1,0:T(8,128)(2,1)S(1)}, u32[]{:S(2)}, u32[]{:S(2)}) async-start(bf16[64,8,512]{2,1,0:T(8,128)(2,1)} %bitcast.18), calls=%async_computation.3 | async-start | bytes 1048576 | tf_op jit(solution)/shard_map/all_to_all | solution.py:20
  114.8 10.2 %collective-permute-start.9 = (bf16[4,4,16,384]{3,2,1,0:T(8,128)(2,1)S(1)}, bf16[4,4,16,384]{3,2,1,0:T(8,128)(2,1)S(1)}, u32[]{:S(2)}, u32[]{:S(2)}) collective-permute-start(bf16[4,4,16,384]{3,2,1,0:T(8,128)(2,1)S(1)} %dynamic-slice_bitcast_fusion), channel_id=1, source_target_pairs={{0,384},{8,392},{16,400},{24,408},{32,416},{40,424},{48,432},{56,4... | collective-permute-start | bytes 589832 | tf_op jit(solution)/shard_map/ppermute | solution.py:25
  120.0 23.7 %copy-start.4 = (bf16[128,1024]{1,0:T(8,128)(2,1)S(1)}, bf16[128,1024]{1,0:T(8,128)(2,1)}, u32[]{:S(2)}) copy-start(bf16[128,1024]{1,0:T(8,128)(2,1)} %inputs.1) | copy-start | bytes 786436
  120.0 9.7 %collective-permute-start.10 = (bf16[4,4,16,384]{3,2,1,0:T(8,128)(2,1)S(1)}, bf16[4,4,16,384]{3,2,1,0:T(8,128)(2,1)S(1)}, u32[]{:S(2)}, u32[]{:S(2)}) collective-permute-start(bf16[4,4,16,384]{3,2,1,0:T(8,128)(2,1)S(1)} %dynamic-slice_bitcast_fusion), channel_id=1, source_target_pairs={{0,256},{8,264},{16,272},{24,280},{32,288},{40,296},{48,304},{56,3... | collective-permute-start | bytes 589832 | tf_op jit(solution)/shard_map/ppermute | solution.py:25
  122.4 30.0 %collective-permute-start.11 = (bf16[4,4,16,384]{3,2,1,0:T(8,128)(2,1)S(1)}, bf16[4,4,16,384]{3,2,1,0:T(8,128)(2,1)S(1)}, u32[]{:S(2)}, u32[]{:S(2)}) collective-permute-start(bf16[4,4,16,384]{3,2,1,0:T(8,128)(2,1)S(1)} %dynamic-slice_bitcast_fusion), channel_id=1, source_target_pairs={{0,128},{8,136},{16,144},{24,152},{32,160},{40,168},{48,176},{56,1... | collective-permute-start | bytes 589832 | tf_op jit(solution)/shard_map/ppermute | solution.py:25
  129.8 14.1 %copy-start.6 = (f32[1024]{0:T(1024)S(1)}, f32[1024]{0:T(1024)}, u32[]{:S(2)}) copy-start(f32[1024]{0:T(1024)} %param.18) | copy-start | bytes 12292
  143.9 15.9 %copy-start.3 = (bf16[128,1024]{1,0:T(8,128)(2,1)}, bf16[128,1024]{1,0:T(8,128)(2,1)S(1)}, u32[]{:S(2)}) copy-start(bf16[128,1024]{1,0:T(8,128)(2,1)S(1)} %get-tuple-element.9) | copy-start | bytes 786436
  144.0 8.6 %collective-permute-start.8 = (bf16[128,1024]{1,0:T(8,128)(2,1)S(1)}, bf16[128,1024]{1,0:T(8,128)(2,1)S(1)}, u32[]{:S(2)}, u32[]{:S(2)}) collective-permute-start(bf16[128,1024]{1,0:T(8,128)(2,1)S(1)} %fusion.2), channel_id=1, source_target_pairs={{0,4},{1,5},{2,6},{3,7},{4,0},{5,1},{6,2},{7,3},{8,12},{9,13},{10,... | collective-permute-start | bytes 786440 | tf_op jit(solution)/shard_map/ppermute | solution.py:25
  146.6 10.6 %collective-permute-start.7 = (bf16[128,1024]{1,0:T(8,128)(2,1)S(1)}, bf16[128,1024]{1,0:T(8,128)(2,1)S(1)}, u32[]{:S(2)}, u32[]{:S(2)}) collective-permute-start(bf16[128,1024]{1,0:T(8,128)(2,1)S(1)} %fusion.2), channel_id=1, source_target_pairs={{0,6},{1,7},{2,0},{3,1},{4,2},{5,3},{6,4},{7,5},{8,14},{9,15},{10,... | collective-permute-start | bytes 786440 | tf_op jit(solution)/shard_map/ppermute | solution.py:25
  150.5 9.1 %collective-permute-start.6 = (bf16[128,1024]{1,0:T(8,128)(2,1)S(1)}, bf16[128,1024]{1,0:T(8,128)(2,1)S(1)}, u32[]{:S(2)}, u32[]{:S(2)}) collective-permute-start(bf16[128,1024]{1,0:T(8,128)(2,1)S(1)} %fusion.2), channel_id=1, source_target_pairs={{0,2},{1,3},{2,4},{3,5},{4,6},{5,7},{6,0},{7,1},{8,10},{9,11},{10,... | collective-permute-start | bytes 786440 | tf_op jit(solution)/shard_map/ppermute | solution.py:25
  159.8 8.4 %collective-permute-start.12 = (bf16[512,1024]{1,0:T(8,128)(2,1)S(1)}, bf16[512,1024]{1,0:T(8,128)(2,1)S(1)}, u32[]{:S(2)}, u32[]{:S(2)}) collective-permute-start(bf16[512,1024]{1,0:T(8,128)(2,1)S(1)} %pad_maximum_fusion), channel_id=1, source_target_pairs={{0,1},{1,0},{2,3},{3,2},{4,5},{5,4},{6,7},{7,6},{8,9},{9,8},{10,11... | collective-permute-start | bytes 3145736 | tf_op jit(solution)/shard_map/ppermute | solution.py:25

commit v6 on v5

--- a/solution.py
+++ b/solution.py
@@ -33,13 +33,15 @@
     return shift(v, "ctx", lambda i: i ^ 1)
 
 
-def gather_four(v, digit, stride):
+def gather_four(v, digit, stride, after=None):
     def move(step):
         return lambda i: i + ((i // stride + step) % 4 - i // stride % 4) * stride
 
     others = []
     for step in (1, 2, 3):
         others.append(shift(v, "exp", move(step)))
+    if after is not None:
+        *others, _ = lax.optimization_barrier((*others, after()))
     one, two, three = others
     turned = jnp.stack([three, two, one, v, three, two, one])
     return lax.dynamic_slice_in_dim(turned, 3 - digit, 4, 0)
@@ -160,16 +162,16 @@
     )(chosen, gate, up, in_hbm(down))
 
 
-def attention_kernel(ids, train, near, far, out, queries, keys, values):
+def attention_kernel(ids, train, *refs):
+    *sources, out, queries, keys, values = refs
     rows, width = 128, 2 * HEAD_DIM
-    half = near.shape[0] // rows
-    chunks = 2 * half
+    chunks = out.shape[0]
+    places = [(source, at) for source in sources for at in range(0, source.shape[0], rows)]
     lane = lax.broadcasted_iota(jnp.int32, (rows, width), 1)
     first = lane < HEAD_DIM
     one_lane = jnp.where(lane == 0, 1.0, 0.0).astype(jnp.bfloat16)
     for j in range(chunks):
-        source = near if j < half else far
-        at = (j % half) * rows
+        source, at = places[j]
         here = slice(j * rows, (j + 1) * rows)
         low, high = slice(2 * j * rows, (2 * j + 1) * rows), slice((2 * j + 1) * rows, (2 * j + 2) * rows)
         q = source[at : at + rows, 0:width]
@@ -197,7 +199,7 @@
         out[ids[j]] = jnp.where(first, blended[:rows], blended[rows:]).astype(jnp.bfloat16)
 
 
-def attention(ids, train, near, far):
+def attention(ids, train, sources):
     chunks = ids.shape[0]
     rows, width = 128, 2 * HEAD_DIM
     vmem = pl.BlockSpec(memory_space=pltpu.VMEM)
@@ -205,7 +207,7 @@
     return pl.pallas_call(
         attention_kernel,
         out_shape=jax.ShapeDtypeStruct((chunks, rows, width), jnp.bfloat16),
-        in_specs=[smem, smem, vmem, vmem],
+        in_specs=[smem, smem] + [vmem] * len(sources),
         out_specs=vmem,
         scratch_shapes=[
             pltpu.VMEM((2 * chunks * rows, 2 * width), jnp.bfloat16),
@@ -214,7 +216,7 @@
         ],
         compiler_params=pltpu.CompilerParams(vmem_limit_bytes=20 * 2**20),
         name="attention",
-    )(ids, train, near, far)
+    )(ids, train, *sources)
 
 
 def local(
@@ -255,8 +257,6 @@
         take_kernel, flat, own_block.reshape(1), in_hbm(selected.T), in_hbm(inputs), scalars=1
     )
     arrived = exchange(outgoing.reshape(sent), "exp").reshape(flat.shape)
-    quarter = gather_four(piece, exp_index // 4 % 4, 4)
-
     taken = selected.reshape(exp_count, experts, group_take) - own_block * row_count
     mine = (taken >= 0) & (taken < row_count)
     lower = jnp.min(jnp.where(mine, taken, row_count), axis=2)
@@ -284,6 +284,7 @@
     )
     compact = small_kernel(fill_kernel, chosen_shape, my_place.reshape(-1, 1), arrived)
     chosen = exchange(compact, "ctx")
+    quarter = gather_four(piece, exp_index // 4 % 4, 4, lambda: compact)
     layer = jnp.moveaxis(gather_four(quarter, exp_index % 4, 1), 0, 1)
     partials = expert_parts(chosen, gate_weight, up_weight, down_weight)
     parts = exchange(partials, "ctx")
@@ -301,19 +302,22 @@
     scale_row = lax.rsqrt(jnp.mean(widened * widened, axis=1, keepdims=True) + EPSILON)
     normed = (widened * scale_row * norm_gain).astype(jnp.bfloat16)
 
-    near = jnp.concatenate(
-        [normed, shift_chip(normed, 1), shift_chip(normed, -1), shift_chip(normed, 2)], axis=0
-    )
-    far = swap_core(near)
+    arrived = []
+    for step in (1, -1, 2):
+        arrived.append(shift_chip(normed, step))
+    near = [normed, jnp.concatenate(arrived[:2], axis=0), arrived[2]]
+    far = []
+    for chunk in near:
+        far.append(swap_core(chunk))
     chip, core = ctx_index // N_CORE, ctx_index % N_CORE
     steps = jnp.array([0, N_X - 1, 1, 2], jnp.int32)
     chips = (chip + steps) % N_X
     ids = jnp.concatenate([chips * N_CORE + core, chips * N_CORE + 1 - core])
-    near_rows = jnp.dot(near, weight_rows, preferred_element_type=jnp.float32)
-    far_rows = jnp.dot(far, weight_rows, preferred_element_type=jnp.float32)
-    mixed = attention(
-        ids, train_count, near_rows.astype(jnp.bfloat16), far_rows.astype(jnp.bfloat16)
-    )
+    projected = [
+        jnp.dot(rows, weight_rows, preferred_element_type=jnp.float32).astype(jnp.bfloat16)
+        for rows in near + far
+    ]
+    mixed = attention(ids, train_count, projected)
     by_heads = exchange(mixed, "ctx")
     context = small_kernel(join_kernel, jax.ShapeDtypeStruct(inputs.shape, inputs.dtype), by_heads)
     return (layer_out, context)

time: 184 us -> 174 us (0.946)
  waiting for transfers between devices: 64 us -> 41.6 us
  starting transfers between devices: 89.6 us -> 99.3 us
  blocking collectives: 9.25 us -> 11.5 us
    all_to_all x4, waiting for transfers between devices: 34.5 us -> 22.3 us  [exchange(): return lax.all_to_all(blocks, axis, split_axis=0, concat_axis=0, tiled=True)]
    ppermute x13 -> x15, waiting for transfers between devices: 29.5 us -> 19.4 us  [shift(): return lax.ppermute(v, axis, [(i, move(i)) for i in range(count)])]
    all_to_all x4, starting transfers between devices: 31.1 us -> 39.9 us  [exchange(): return lax.all_to_all(blocks, axis, split_axis=0, concat_axis=0, tiled=True)]
    all_to_all x1, blocking collectives: 9.25 us -> 11.5 us  [exchange(): return lax.all_to_all(blocks, axis, split_axis=0, concat_axis=0, tiled=True)]
    ppermute x13 -> x15, starting transfers between devices: 58.5 us -> 59.4 us  [shift(): return lax.ppermute(v, axis, [(i, move(i)) for i in range(count)])]
  transfers between devices with their start and end apart: 17 -> 19, of which waited for: 11 -> 9; matrix products, arithmetic and copies ran while one was open for 2% -> 3% of each run, Pallas kernels for 2% -> 1%
where the time goes in v6:
time: 174 us; the launch traced here: 172 us
  starting transfers between devices  99.3 us (57%)
  waiting for transfers between devices  41.6 us (24%)
  Pallas kernels  11.9 us (7%)
  blocking collectives  11.5 us (7%)
  matrix products  2.57 us (1%)
  local copies, waits for them, and re-layouts  2.48 us (1%)
  between operations  1.93 us (1%)
    ppermute x15, starting transfers between devices, shift(): return lax.ppermute(v, axis, [(i, move(i)) for i in range(count)])  59.4 us
    all_to_all x4, starting transfers between devices, exchange(): return lax.all_to_all(blocks, axis, split_axis=0, concat_axis=0, tiled=True)  39.9 us
    all_to_all x4, waiting for transfers between devices, exchange(): return lax.all_to_all(blocks, axis, split_axis=0, concat_axis=0, tiled=True)  22.3 us
    ppermute x15, waiting for transfers between devices, shift(): return lax.ppermute(v, axis, [(i, move(i)) for i in range(count)])  19.4 us
    all_to_all x1, blocking collectives, exchange(): return lax.all_to_all(blocks, axis, split_axis=0, concat_axis=0, tiled=True)  11.5 us
    pallas_call x4, Pallas kernels, small_kernel(): pl.pallas_call(body, out_shape=outs, in_specs=whole(pltpu.SMEM, scalars)...  5.53 us
    pallas_call x1, Pallas kernels, attention(): pl.pallas_call(attention_kernel, out_shape=jax.ShapeDtypeStruct((chunks,...  3.73 us
  transfers between devices with their start and end apart: 19, of which 9 were waited for; matrix products, arithmetic and copies ran while one was open for 3% of the time, Pallas kernels for 1%

profile of v6, /device:TPU:1, one launch (start us, length us, event | category | flops | bytes accessed | tf_op | source)
XLA Modules:
  0.0 172.1 jit_solution(3176408635153105701)
XLA Ops:
  0.6 0.0 copy-start
  0.7 2.3 %shard_map.131 = bf16[512,512]{1,0:T(8,128)(2,1)} custom-call(s32[1]{0:T(128)} %bitcast.1.block, s32[16,128]{1,0:T(8,128)} %bitcast.70, bf16[128,1024]{1,0:T(8,128)(2,1)} %inputs.1), custom_call_target="tpu_custom_call" | custom-call | tf_op jit(solution)/shard_map/pallas_call | solution.py:55
  3.0 19.4 %all-to-all-start = ((bf16[64,8,512]{2,1,0:T(8,128)(2,1)}), bf16[64,8,512]{2,1,0:T(8,128)(2,1)S(1)}, u32[]{:S(2)}, u32[]{:S(2)}) async-start(bf16[64,8,512]{2,1,0:T(8,128)(2,1)} %bitcast.3), calls=%async_computation | async-start | bytes 1048576 | tf_op jit(solution)/shard_map/all_to_all | solution.py:20
  22.4 0.7 constant_dynamic-slice_fusion.2
  23.2 6.8 %collective-permute-start = (bf16[16,384]{1,0:T(8,128)(2,1)S(1)}, bf16[16,384]{1,0:T(8,128)(2,1)S(1)}, u32[]{:S(2)}, u32[]{:S(2)}) collective-permute-start(bf16[16,384]{1,0:T(8,128)(2,1)S(1)} %pad_maximum_fusion), channel_id=1, source_target_pairs={{0,32},{8,40},{16,48},{24,56},{32,64},{40,72},{48,80},{56,88},{64,... | collective-permute-start | bytes 36872 | tf_op jit(solution)/shard_map/ppermute | solution.py:25
  30.0 7.0 %collective-permute-start.1 = (bf16[16,384]{1,0:T(8,128)(2,1)S(1)}, bf16[16,384]{1,0:T(8,128)(2,1)S(1)}, u32[]{:S(2)}, u32[]{:S(2)}) collective-permute-start(bf16[16,384]{1,0:T(8,128)(2,1)S(1)} %pad_maximum_fusion), channel_id=1, source_target_pairs={{0,64},{8,72},{16,80},{24,88},{32,96},{40,104},{48,112},{56,120},{... | collective-permute-start | bytes 36872 | tf_op jit(solution)/shard_map/ppermute | solution.py:25
  37.0 7.0 %collective-permute-start.2 = (bf16[16,384]{1,0:T(8,128)(2,1)S(1)}, bf16[16,384]{1,0:T(8,128)(2,1)S(1)}, u32[]{:S(2)}, u32[]{:S(2)}) collective-permute-start(bf16[16,384]{1,0:T(8,128)(2,1)S(1)} %pad_maximum_fusion), channel_id=1, source_target_pairs={{0,96},{8,104},{16,112},{24,120},{32,0},{40,8},{48,16},{56,24},{64... | collective-permute-start | bytes 36872 | tf_op jit(solution)/shard_map/ppermute | solution.py:25
  44.0 0.1 constant_dynamic-slice_fusion.5
  44.1 0.1 copy.64
  44.2 0.1 reduce_min.12
  44.3 0.1 reduce_max.12
  44.5 0.1 copy.54
  44.6 0.1 copy.53
  44.7 0.2 convert_reduce_fusion
  44.9 0.1 add_add_fusion
  45.0 0.1 copy.56
  45.1 0.1 reshape_reshape.8.place
  45.1 0.1 copy.55
  45.3 6.5 %all-to-all-done = bf16[64,8,512]{2,1,0:T(8,128)(2,1)S(1)} async-done(((bf16[64,8,512]{2,1,0:T(8,128)(2,1)}), bf16[64,8,512]{2,1,0:T(8,128)(2,1)S(1)}, u32[]{:S(2)}, u32[]{:S(2)}) %all-to-all-start) | async-done | bytes 524320 | tf_op jit(solution)/shard_map/all_to_all | solution.py:20
  51.7 1.1 shard_map.132
  52.9 2.3 %collective-permute-done.1 = bf16[16,384]{1,0:T(8,128)(2,1)S(1)} collective-permute-done((bf16[16,384]{1,0:T(8,128)(2,1)S(1)}, bf16[16,384]{1,0:T(8,128)(2,1)S(1)}, u32[]{:S(2)}, u32[]{:S(2)}) %collective-permute-start.1) | collective-permute-done | bytes 12320 | tf_op jit(solution)/shard_map/ppermute | solution.py:25
  55.3 2.3 %collective-permute-start.3 = (bf16[4,16,384]{2,1,0:T(8,128)(2,1)S(1)}, bf16[4,16,384]{2,1,0:T(8,128)(2,1)S(1)}, u32[]{:S(2)}, u32[]{:S(2)}) collective-permute-start(bf16[4,16,384]{2,1,0:T(8,128)(2,1)S(1)} %constant_dynamic-slice_fusion.1), channel_id=1, source_target_pairs={{0,24},{8,0},{16,8},{24,16},{32,56},{40,32},{48,40},{56,48},{64,88... | collective-permute-start | bytes 147464 | tf_op jit(solution)/shard_map/ppermute | solution.py:25
  57.6 0.1 add_select_fusion
  57.8 0.1 reshape_reshape.6.place
  57.8 0.1 reshape.142.gate
  57.9 7.8 %all-to-all-start.1 = ((bf16[8,32,1024]{2,1,0:T(8,128)(2,1)}), bf16[8,32,1024]{2,1,0:T(8,128)(2,1)S(1)}, u32[]{:S(2)}, u32[]{:S(2)}) async-start(bf16[8,32,1024]{2,1,0:T(8,128)(2,1)} %shard_map.132), calls=%async_computation.1 | async-start | bytes 1048576 | tf_op jit(solution)/shard_map/all_to_all | solution.py:20
  65.8 2.4 %collective-permute-start.4 = (bf16[4,16,384]{2,1,0:T(8,128)(2,1)S(1)}, bf16[4,16,384]{2,1,0:T(8,128)(2,1)S(1)}, u32[]{:S(2)}, u32[]{:S(2)}) collective-permute-start(bf16[4,16,384]{2,1,0:T(8,128)(2,1)S(1)} %constant_dynamic-slice_fusion.1), channel_id=1, source_target_pairs={{0,16},{8,24},{16,0},{24,8},{32,48},{40,56},{48,32},{56,40},{64,80... | collective-permute-start | bytes 147464 | tf_op jit(solution)/shard_map/ppermute | solution.py:25
  68.1 2.5 %collective-permute-start.5 = (bf16[4,16,384]{2,1,0:T(8,128)(2,1)S(1)}, bf16[4,16,384]{2,1,0:T(8,128)(2,1)S(1)}, u32[]{:S(2)}, u32[]{:S(2)}) collective-permute-start(bf16[4,16,384]{2,1,0:T(8,128)(2,1)S(1)} %constant_dynamic-slice_fusion.1), channel_id=1, source_target_pairs={{0,8},{8,16},{16,24},{24,0},{32,40},{40,48},{48,56},{56,32},{64,72... | collective-permute-start | bytes 147464 | tf_op jit(solution)/shard_map/ppermute | solution.py:25
  70.6 2.4 %collective-permute-done.4 = bf16[4,16,384]{2,1,0:T(8,128)(2,1)S(1)} collective-permute-done((bf16[4,16,384]{2,1,0:T(8,128)(2,1)S(1)}, bf16[4,16,384]{2,1,0:T(8,128)(2,1)S(1)}, u32[]{:S(2)}, u32[]{:S(2)}) %collective-permute-start.4) | collective-permute-done | bytes 49184 | tf_op jit(solution)/shard_map/ppermute | solution.py:25
  73.1 2.0 %collective-permute-done.5 = bf16[4,16,384]{2,1,0:T(8,128)(2,1)S(1)} collective-permute-done((bf16[4,16,384]{2,1,0:T(8,128)(2,1)S(1)}, bf16[4,16,384]{2,1,0:T(8,128)(2,1)S(1)}, u32[]{:S(2)}, u32[]{:S(2)}) %collective-permute-start.5) | collective-permute-done | bytes 49184 | tf_op jit(solution)/shard_map/ppermute | solution.py:25
  75.2 2.6 %experts.1 = bf16[8,32,1024]{2,1,0:T(8,128)(2,1)} custom-call(bf16[8,32,1024]{2,1,0:T(8,128)(2,1)S(1)} %all-to-all-done.1.chosen, bf16[2,1024,256]{2,1,0:T(8,128)(2,1)S(1)} %copy-done.1, bf16[2,1024,256]{2,1,0:T(8,128)(2,1)S(1)} %copy-done.2, bf16[2,256,1024]{2,1,0:T(8,128)(2,1)} %down.1), custom_call_target="tpu_custom_call" | custom-call | tf_op jit(solution)/shard_map/experts/pallas_call | solution.py:151
  77.8 5.9 %all-to-all-start.2 = ((bf16[8,32,1024]{2,1,0:T(8,128)(2,1)}), bf16[8,32,1024]{2,1,0:T(8,128)(2,1)S(1)}, u32[]{:S(2)}, u32[]{:S(2)}) async-start(bf16[8,32,1024]{2,1,0:T(8,128)(2,1)} %experts.1), calls=%async_computation.2 | async-start | bytes 1048576 | tf_op jit(solution)/shard_map/all_to_all | solution.py:20
  83.8 9.3 %all-to-all-done.2.parts = bf16[8,32,1024]{2,1,0:T(8,128)(2,1)S(1)} async-done(((bf16[8,32,1024]{2,1,0:T(8,128)(2,1)}), bf16[8,32,1024]{2,1,0:T(8,128)(2,1)S(1)}, u32[]{:S(2)}, u32[]{:S(2)}) %all-to-all-start.2) | async-done | bytes 524320 | tf_op jit(solution)/shard_map/all_to_all | solution.py:20
  93.1 1.3 shard_map.133
  94.4 6.7 %all-to-all-start.3 = ((bf16[64,8,512]{2,1,0:T(8,128)(2,1)}), bf16[64,8,512]{2,1,0:T(8,128)(2,1)S(1)}, u32[]{:S(2)}, u32[]{:S(2)}) async-start(bf16[64,8,512]{2,1,0:T(8,128)(2,1)} %bitcast.18), calls=%async_computation.3 | async-start | bytes 1048576 | tf_op jit(solution)/shard_map/all_to_all | solution.py:20
  101.1 4.3 %collective-permute-start.6 = (bf16[4,4,16,384]{3,2,1,0:T(8,128)(2,1)S(1)}, bf16[4,4,16,384]{3,2,1,0:T(8,128)(2,1)S(1)}, u32[]{:S(2)}, u32[]{:S(2)}) collective-permute-start(bf16[4,4,16,384]{3,2,1,0:T(8,128)(2,1)S(1)} %dynamic-slice_bitcast_fusion), channel_id=1, source_target_pairs={{0,384},{8,392},{16,400},{24,408},{32,416},{40,424},{48,432},{56,4... | collective-permute-start | bytes 589832 | tf_op jit(solution)/shard_map/ppermute | solution.py:25
  105.5 0.1 select_n.99
  106.3 0.1 pad_add_fusion.1.ids
  106.3 2.3 %collective-permute-start.7 = (bf16[4,4,16,384]{3,2,1,0:T(8,128)(2,1)S(1)}, bf16[4,4,16,384]{3,2,1,0:T(8,128)(2,1)S(1)}, u32[]{:S(2)}, u32[]{:S(2)}) collective-permute-start(bf16[4,4,16,384]{3,2,1,0:T(8,128)(2,1)S(1)} %dynamic-slice_bitcast_fusion), channel_id=1, source_target_pairs={{0,256},{8,264},{16,272},{24,280},{32,288},{40,296},{48,304},{56,3... | collective-permute-start | bytes 589832 | tf_op jit(solution)/shard_map/ppermute | solution.py:25
  108.6 2.6 %collective-permute-start.8 = (bf16[4,4,16,384]{3,2,1,0:T(8,128)(2,1)S(1)}, bf16[4,4,16,384]{3,2,1,0:T(8,128)(2,1)S(1)}, u32[]{:S(2)}, u32[]{:S(2)}) collective-permute-start(bf16[4,4,16,384]{3,2,1,0:T(8,128)(2,1)S(1)} %dynamic-slice_bitcast_fusion), channel_id=1, source_target_pairs={{0,128},{8,136},{16,144},{24,152},{32,160},{40,168},{48,176},{56,1... | collective-permute-start | bytes 589832 | tf_op jit(solution)/shard_map/ppermute | solution.py:25
  111.2 4.8 %collective-permute-done.7 = bf16[4,4,16,384]{3,2,1,0:T(8,128)(2,1)S(1)} collective-permute-done((bf16[4,4,16,384]{3,2,1,0:T(8,128)(2,1)S(1)}, bf16[4,4,16,384]{3,2,1,0:T(8,128)(2,1)S(1)}, u32[]{:S(2)}, u32[]{:S(2)}) %collective-permute-start.7) | collective-permute-done | bytes 196640 | tf_op jit(solution)/shard_map/ppermute | solution.py:25
  116.1 7.6 %collective-permute-done.8 = bf16[4,4,16,384]{3,2,1,0:T(8,128)(2,1)S(1)} collective-permute-done((bf16[4,4,16,384]{3,2,1,0:T(8,128)(2,1)S(1)}, bf16[4,4,16,384]{3,2,1,0:T(8,128)(2,1)S(1)}, u32[]{:S(2)}, u32[]{:S(2)}) %collective-permute-start.8) | collective-permute-done | bytes 196640 | tf_op jit(solution)/shard_map/ppermute | solution.py:25
  123.8 0.0 copy-start.4
  123.9 6.5 %all-to-all-done.3 = bf16[64,8,512]{2,1,0:T(8,128)(2,1)S(1)} async-done(((bf16[64,8,512]{2,1,0:T(8,128)(2,1)}), bf16[64,8,512]{2,1,0:T(8,128)(2,1)S(1)}, u32[]{:S(2)}, u32[]{:S(2)}) %all-to-all-start.3) | async-done | bytes 524320 | tf_op jit(solution)/shard_map/all_to_all | solution.py:20
  130.4 0.4 fusion.4
  130.9 0.2 fusion
  131.1 0.1 fusion.2
  131.2 2.2 %collective-permute-start.9 = (bf16[128,1024]{1,0:T(8,128)(2,1)S(1)}, bf16[128,1024]{1,0:T(8,128)(2,1)S(1)}, u32[]{:S(2)}, u32[]{:S(2)}) collective-permute-start(bf16[128,1024]{1,0:T(8,128)(2,1)S(1)} %fusion.2), channel_id=1, source_target_pairs={{0,2},{1,3},{2,4},{3,5},{4,6},{5,7},{6,0},{7,1},{8,10},{9,11},{10,... | collective-permute-start | bytes 786440 | tf_op jit(solution)/shard_map/ppermute | solution.py:25
  133.4 0.1 constant_dynamic-slice_fusion
  133.5 4.3 %collective-permute-start.10 = (bf16[128,1024]{1,0:T(8,128)(2,1)S(1)}, bf16[128,1024]{1,0:T(8,128)(2,1)S(1)}, u32[]{:S(2)}, u32[]{:S(2)}) collective-permute-start(bf16[128,1024]{1,0:T(8,128)(2,1)S(1)} %fusion.2), channel_id=1, source_target_pairs={{0,6},{1,7},{2,0},{3,1},{4,2},{5,3},{6,4},{7,5},{8,14},{9,15},{10,... | collective-permute-start | bytes 786440 | tf_op jit(solution)/shard_map/ppermute | solution.py:25
  137.8 1.9 %collective-permute-start.11 = (bf16[128,1024]{1,0:T(8,128)(2,1)S(1)}, bf16[128,1024]{1,0:T(8,128)(2,1)S(1)}, u32[]{:S(2)}, u32[]{:S(2)}) collective-permute-start(bf16[128,1024]{1,0:T(8,128)(2,1)S(1)} %fusion.2), channel_id=1, source_target_pairs={{0,4},{1,5},{2,6},{3,7},{4,0},{5,1},{6,2},{7,3},{8,12},{9,13},{10,... | collective-permute-start | bytes 786440 | tf_op jit(solution)/shard_map/ppermute | solution.py:25
  139.8 5.8 %collective-permute-start.12 = (bf16[128,1024]{1,0:T(8,128)(2,1)S(1)}, bf16[128,1024]{1,0:T(8,128)(2,1)S(1)}, u32[]{:S(2)}, u32[]{:S(2)}) collective-permute-start(bf16[128,1024]{1,0:T(8,128)(2,1)S(1)} %fusion.2), channel_id=1, source_target_pairs={{0,1},{1,0},{2,3},{3,2},{4,5},{5,4},{6,7},{7,6},{8,9},{9,8},{10,11... | collective-permute-start | bytes 786440 | tf_op jit(solution)/shard_map/ppermute | solution.py:25
  145.5 0.3 convolution_convert_fusion.5.refs_0_
  146.0 6.0 %collective-permute-start.13 = (bf16[256,1024]{1,0:T(8,128)(2,1)S(1)}, bf16[256,1024]{1,0:T(8,128)(2,1)S(1)}, u32[]{:S(2)}, u32[]{:S(2)}) collective-permute-start(bf16[256,1024]{1,0:T(8,128)(2,1)S(1)} %constant_dynamic-update-slice_fusion.7), channel_id=1, source_target_pairs={{0,1},{1,0},{2,3},{3,2},{4,5},{5,4},{6,7},{7,6},{8,9},{9,8},{10,11... | collective-permute-start | bytes 1572872 | tf_op jit(solution)/shard_map/ppermute | solution.py:25
  151.9 2.1 %collective-permute-start.14 = (bf16[128,1024]{1,0:T(8,128)(2,1)S(1)}, bf16[128,1024]{1,0:T(8,128)(2,1)S(1)}, u32[]{:S(2)}, u32[]{:S(2)}) collective-permute-start(bf16[128,1024]{1,0:T(8,128)(2,1)S(1)} %collective-permute-done.11), channel_id=1, source_target_pairs={{0,1},{1,0},{2,3},{3,2},{4,5},{5,4},{6,7},{7,6},{8,9},{9,8},{10,11... | collective-permute-start | bytes 786440 | tf_op jit(solution)/shard_map/ppermute | solution.py:25
  154.1 0.3 convolution_convert_fusion.4.refs_2_
  154.4 0.3 convolution_convert_fusion.3.refs_3_
  154.7 0.4 convolution_convert_fusion.1.refs_1_
  155.2 0.2 collective-permute-done.14
  155.4 0.3 convolution_convert_fusion.2.refs_5_
  155.7 0.4 convolution_convert_fusion.refs_4_
  156.1 3.7 %attention.1 = bf16[8,128,128]{2,1,0:T(8,128)(2,1)S(1)} custom-call(s32[8]{0:T(128)S(1)} %pad_add_fusion.1.ids, s32[1]{0:T(128)S(6)} %copy.84.train, bf16[128,384]{1,0:T(8,128)(2,1)S(1)} %convolution_convert_fusion.5.refs_0_, bf16[256,384]{1,0:T(8,128)(2,1)S(1)} %convolution_convert_fusion.1.refs_1_, bf16[128,384]{1,0:T(8,128)(2,1)S(1)} %convolution_convert_fusion.4.refs_2_, ...), custom_call_target="tpu_custom_call" | custom-call | tf_op jit(solution)/shard_map/attention/pallas_call | solution.py:207
  159.9 11.5 %all_to_all.25.pieces = bf16[8,128,128]{2,1,0:T(8,128)(2,1)S(1)} all-to-all(bf16[8,128,128]{2,1,0:T(8,128)(2,1)S(1)} %attention.1), channel_id=1, replica_groups=mesh['exp'=64,'ctx'=8] {'ctx'}, dimensions={0} | all-to-all | bytes 524288 | tf_op jit(solution)/shard_map/all_to_all | solution.py:20
  171.4 0.8 shard_map.134
  (64 shorter events, 0.7 us)
Async XLA Ops:
  0.6 21.8 %copy-start = (bf16[16,1024]{1,0:T(8,128)(2,1)S(1)}, bf16[16,1024]{1,0:T(8,128)(2,1)}, u32[]{:S(2)}) copy-start(bf16[16,1024]{1,0:T(8,128)(2,1)} %param.19) | copy-start | bytes 98308
  0.6 43.4 %copy-start.5 = (s32[128,16]{0,1:T(8,128)S(1)}, s32[128,16]{0,1:T(8,128)}, u32[]{:S(2)}) copy-start(s32[128,16]{0,1:T(8,128)} %param.13) | copy-start | bytes 24580
  3.0 54.8 %copy-start.7 = (f32[2,16]{1,0:T(2,128)S(1)}, f32[2,16]{1,0:T(2,128)}, u32[]{:S(2)}) copy-start(f32[2,16]{1,0:T(2,128)} %param.14) | copy-start | bytes 388
  3.0 48.7 %all-to-all-start = ((bf16[64,8,512]{2,1,0:T(8,128)(2,1)}), bf16[64,8,512]{2,1,0:T(8,128)(2,1)S(1)}, u32[]{:S(2)}, u32[]{:S(2)}) async-start(bf16[64,8,512]{2,1,0:T(8,128)(2,1)} %bitcast.3), calls=%async_computation | async-start | bytes 1048576 | tf_op jit(solution)/shard_map/all_to_all | solution.py:20
  23.2 29.7 %collective-permute-start = (bf16[16,384]{1,0:T(8,128)(2,1)S(1)}, bf16[16,384]{1,0:T(8,128)(2,1)S(1)}, u32[]{:S(2)}, u32[]{:S(2)}) collective-permute-start(bf16[16,384]{1,0:T(8,128)(2,1)S(1)} %pad_maximum_fusion), channel_id=1, source_target_pairs={{0,32},{8,40},{16,48},{24,56},{32,64},{40,72},{48,80},{56,88},{64,... | collective-permute-start | bytes 36872 | tf_op jit(solution)/shard_map/ppermute | solution.py:25
  30.0 25.2 %collective-permute-start.1 = (bf16[16,384]{1,0:T(8,128)(2,1)S(1)}, bf16[16,384]{1,0:T(8,128)(2,1)S(1)}, u32[]{:S(2)}, u32[]{:S(2)}) collective-permute-start(bf16[16,384]{1,0:T(8,128)(2,1)S(1)} %pad_maximum_fusion), channel_id=1, source_target_pairs={{0,64},{8,72},{16,80},{24,88},{32,96},{40,104},{48,112},{56,120},{... | collective-permute-start | bytes 36872 | tf_op jit(solution)/shard_map/ppermute | solution.py:25
  37.0 18.2 %collective-permute-start.2 = (bf16[16,384]{1,0:T(8,128)(2,1)S(1)}, bf16[16,384]{1,0:T(8,128)(2,1)S(1)}, u32[]{:S(2)}, u32[]{:S(2)}) collective-permute-start(bf16[16,384]{1,0:T(8,128)(2,1)S(1)} %pad_maximum_fusion), channel_id=1, source_target_pairs={{0,96},{8,104},{16,112},{24,120},{32,0},{40,8},{48,16},{56,24},{64... | collective-permute-start | bytes 36872 | tf_op jit(solution)/shard_map/ppermute | solution.py:25
  51.7 23.4 %copy-start.1 = (bf16[2,1024,256]{2,1,0:T(8,128)(2,1)S(1)}, bf16[2,1024,256]{2,1,0:T(8,128)(2,1)}, u32[]{:S(2)}) copy-start(bf16[2,1024,256]{2,1,0:T(8,128)(2,1)} %gate.1) | copy-start | bytes 3145732
  51.7 23.4 %copy-start.2 = (bf16[2,1024,256]{2,1,0:T(8,128)(2,1)S(1)}, bf16[2,1024,256]{2,1,0:T(8,128)(2,1)}, u32[]{:S(2)}) copy-start(bf16[2,1024,256]{2,1,0:T(8,128)(2,1)} %up.1) | copy-start | bytes 3145732
  55.3 15.3 %collective-permute-start.3 = (bf16[4,16,384]{2,1,0:T(8,128)(2,1)S(1)}, bf16[4,16,384]{2,1,0:T(8,128)(2,1)S(1)}, u32[]{:S(2)}, u32[]{:S(2)}) collective-permute-start(bf16[4,16,384]{2,1,0:T(8,128)(2,1)S(1)} %constant_dynamic-slice_fusion.1), channel_id=1, source_target_pairs={{0,24},{8,0},{16,8},{24,16},{32,56},{40,32},{48,40},{56,48},{64,88... | collective-permute-start | bytes 147464 | tf_op jit(solution)/shard_map/ppermute | solution.py:25
  57.9 17.2 %all-to-all-start.1 = ((bf16[8,32,1024]{2,1,0:T(8,128)(2,1)}), bf16[8,32,1024]{2,1,0:T(8,128)(2,1)S(1)}, u32[]{:S(2)}, u32[]{:S(2)}) async-start(bf16[8,32,1024]{2,1,0:T(8,128)(2,1)} %shard_map.132), calls=%async_computation.1 | async-start | bytes 1048576 | tf_op jit(solution)/shard_map/all_to_all | solution.py:20
  65.8 7.3 %collective-permute-start.4 = (bf16[4,16,384]{2,1,0:T(8,128)(2,1)S(1)}, bf16[4,16,384]{2,1,0:T(8,128)(2,1)S(1)}, u32[]{:S(2)}, u32[]{:S(2)}) collective-permute-start(bf16[4,16,384]{2,1,0:T(8,128)(2,1)S(1)} %constant_dynamic-slice_fusion.1), channel_id=1, source_target_pairs={{0,16},{8,24},{16,0},{24,8},{32,48},{40,56},{48,32},{56,40},{64,80... | collective-permute-start | bytes 147464 | tf_op jit(solution)/shard_map/ppermute | solution.py:25
  68.1 6.9 %collective-permute-start.5 = (bf16[4,16,384]{2,1,0:T(8,128)(2,1)S(1)}, bf16[4,16,384]{2,1,0:T(8,128)(2,1)S(1)}, u32[]{:S(2)}, u32[]{:S(2)}) collective-permute-start(bf16[4,16,384]{2,1,0:T(8,128)(2,1)S(1)} %constant_dynamic-slice_fusion.1), channel_id=1, source_target_pairs={{0,8},{8,16},{16,24},{24,0},{32,40},{40,48},{48,56},{56,32},{64,72... | collective-permute-start | bytes 147464 | tf_op jit(solution)/shard_map/ppermute | solution.py:25
  77.8 15.3 %all-to-all-start.2 = ((bf16[8,32,1024]{2,1,0:T(8,128)(2,1)}), bf16[8,32,1024]{2,1,0:T(8,128)(2,1)S(1)}, u32[]{:S(2)}, u32[]{:S(2)}) async-start(bf16[8,32,1024]{2,1,0:T(8,128)(2,1)} %experts.1), calls=%async_computation.2 | async-start | bytes 1048576 | tf_op jit(solution)/shard_map/all_to_all | solution.py:20
  83.7 17.3 %copy-start.8 = (s32[4]{0:T(128)S(1)}, s32[4]{0:T(128)}, u32[]{:S(2)}) copy-start(s32[4]{0:T(128)} %constant.120.clone) | copy-start | bytes 52
  94.4 36.0 %all-to-all-start.3 = ((bf16[64,8,512]{2,1,0:T(8,128)(2,1)}), bf16[64,8,512]{2,1,0:T(8,128)(2,1)S(1)}, u32[]{:S(2)}, u32[]{:S(2)}) async-start(bf16[64,8,512]{2,1,0:T(8,128)(2,1)} %bitcast.18), calls=%async_computation.3 | async-start | bytes 1048576 | tf_op jit(solution)/shard_map/all_to_all | solution.py:20
  101.1 10.1 %collective-permute-start.6 = (bf16[4,4,16,384]{3,2,1,0:T(8,128)(2,1)S(1)}, bf16[4,4,16,384]{3,2,1,0:T(8,128)(2,1)S(1)}, u32[]{:S(2)}, u32[]{:S(2)}) collective-permute-start(bf16[4,4,16,384]{3,2,1,0:T(8,128)(2,1)S(1)} %dynamic-slice_bitcast_fusion), channel_id=1, source_target_pairs={{0,384},{8,392},{16,400},{24,408},{32,416},{40,424},{48,432},{56,4... | collective-permute-start | bytes 589832 | tf_op jit(solution)/shard_map/ppermute | solution.py:25
  106.3 9.7 %collective-permute-start.7 = (bf16[4,4,16,384]{3,2,1,0:T(8,128)(2,1)S(1)}, bf16[4,4,16,384]{3,2,1,0:T(8,128)(2,1)S(1)}, u32[]{:S(2)}, u32[]{:S(2)}) collective-permute-start(bf16[4,4,16,384]{3,2,1,0:T(8,128)(2,1)S(1)} %dynamic-slice_bitcast_fusion), channel_id=1, source_target_pairs={{0,256},{8,264},{16,272},{24,280},{32,288},{40,296},{48,304},{56,3... | collective-permute-start | bytes 589832 | tf_op jit(solution)/shard_map/ppermute | solution.py:25
  108.6 15.0 %collective-permute-start.8 = (bf16[4,4,16,384]{3,2,1,0:T(8,128)(2,1)S(1)}, bf16[4,4,16,384]{3,2,1,0:T(8,128)(2,1)S(1)}, u32[]{:S(2)}, u32[]{:S(2)}) collective-permute-start(bf16[4,4,16,384]{3,2,1,0:T(8,128)(2,1)S(1)} %dynamic-slice_bitcast_fusion), channel_id=1, source_target_pairs={{0,128},{8,136},{16,144},{24,152},{32,160},{40,168},{48,176},{56,1... | collective-permute-start | bytes 589832 | tf_op jit(solution)/shard_map/ppermute | solution.py:25
  123.8 7.1 %copy-start.4 = (bf16[128,1024]{1,0:T(8,128)(2,1)S(1)}, bf16[128,1024]{1,0:T(8,128)(2,1)}, u32[]{:S(2)}) copy-start(bf16[128,1024]{1,0:T(8,128)(2,1)} %inputs.1) | copy-start | bytes 786436
  123.9 7.2 %copy-start.6 = (f32[1024]{0:T(1024)S(1)}, f32[1024]{0:T(1024)}, u32[]{:S(2)}) copy-start(f32[1024]{0:T(1024)} %param.18) | copy-start | bytes 12292
  131.1 14.8 %copy-start.3 = (bf16[128,1024]{1,0:T(8,128)(2,1)}, bf16[128,1024]{1,0:T(8,128)(2,1)S(1)}, u32[]{:S(2)}) copy-start(bf16[128,1024]{1,0:T(8,128)(2,1)S(1)} %get-tuple-element.15) | copy-start | bytes 786436
  131.2 14.7 %collective-permute-start.9 = (bf16[128,1024]{1,0:T(8,128)(2,1)S(1)}, bf16[128,1024]{1,0:T(8,128)(2,1)S(1)}, u32[]{:S(2)}, u32[]{:S(2)}) collective-permute-start(bf16[128,1024]{1,0:T(8,128)(2,1)S(1)} %fusion.2), channel_id=1, source_target_pairs={{0,2},{1,3},{2,4},{3,5},{4,6},{5,7},{6,0},{7,1},{8,10},{9,11},{10,... | collective-permute-start | bytes 786440 | tf_op jit(solution)/shard_map/ppermute | solution.py:25
  133.5 12.4 %collective-permute-start.10 = (bf16[128,1024]{1,0:T(8,128)(2,1)S(1)}, bf16[128,1024]{1,0:T(8,128)(2,1)S(1)}, u32[]{:S(2)}, u32[]{:S(2)}) collective-permute-start(bf16[128,1024]{1,0:T(8,128)(2,1)S(1)} %fusion.2), channel_id=1, source_target_pairs={{0,6},{1,7},{2,0},{3,1},{4,2},{5,3},{6,4},{7,5},{8,14},{9,15},{10,... | collective-permute-start | bytes 786440 | tf_op jit(solution)/shard_map/ppermute | solution.py:25
  137.8 14.1 %collective-permute-start.11 = (bf16[128,1024]{1,0:T(8,128)(2,1)S(1)}, bf16[128,1024]{1,0:T(8,128)(2,1)S(1)}, u32[]{:S(2)}, u32[]{:S(2)}) collective-permute-start(bf16[128,1024]{1,0:T(8,128)(2,1)S(1)} %fusion.2), channel_id=1, source_target_pairs={{0,4},{1,5},{2,6},{3,7},{4,0},{5,1},{6,2},{7,3},{8,12},{9,13},{10,... | collective-permute-start | bytes 786440 | tf_op jit(solution)/shard_map/ppermute | solution.py:25
  139.8 14.6 %collective-permute-start.12 = (bf16[128,1024]{1,0:T(8,128)(2,1)S(1)}, bf16[128,1024]{1,0:T(8,128)(2,1)S(1)}, u32[]{:S(2)}, u32[]{:S(2)}) collective-permute-start(bf16[128,1024]{1,0:T(8,128)(2,1)S(1)} %fusion.2), channel_id=1, source_target_pairs={{0,1},{1,0},{2,3},{3,2},{4,5},{5,4},{6,7},{7,6},{8,9},{9,8},{10,11... | collective-permute-start | bytes 786440 | tf_op jit(solution)/shard_map/ppermute | solution.py:25
  146.0 9.7 %collective-permute-start.13 = (bf16[256,1024]{1,0:T(8,128)(2,1)S(1)}, bf16[256,1024]{1,0:T(8,128)(2,1)S(1)}, u32[]{:S(2)}, u32[]{:S(2)}) collective-permute-start(bf16[256,1024]{1,0:T(8,128)(2,1)S(1)} %constant_dynamic-update-slice_fusion.7), channel_id=1, source_target_pairs={{0,1},{1,0},{2,3},{3,2},{4,5},{5,4},{6,7},{7,6},{8,9},{9,8},{10,11... | collective-permute-start | bytes 1572872 | tf_op jit(solution)/shard_map/ppermute | solution.py:25
  151.9 3.4 %collective-permute-start.14 = (bf16[128,1024]{1,0:T(8,128)(2,1)S(1)}, bf16[128,1024]{1,0:T(8,128)(2,1)S(1)}, u32[]{:S(2)}, u32[]{:S(2)}) collective-permute-start(bf16[128,1024]{1,0:T(8,128)(2,1)S(1)} %collective-permute-done.11), channel_id=1, source_target_pairs={{0,1},{1,0},{2,3},{3,2},{4,5},{5,4},{6,7},{7,6},{8,9},{9,8},{10,11... | collective-permute-start | bytes 786440 | tf_op jit(solution)/shard_map/ppermute | solution.py:25

commit v7 on v5

--- a/solution.py
+++ b/solution.py
@@ -33,13 +33,15 @@
     return shift(v, "ctx", lambda i: i ^ 1)
 
 
-def gather_four(v, digit, stride):
+def gather_four(v, digit, stride, after=None):
     def move(step):
         return lambda i: i + ((i // stride + step) % 4 - i // stride % 4) * stride
 
     others = []
     for step in (1, 2, 3):
         others.append(shift(v, "exp", move(step)))
+    if after is not None:
+        *others, _ = lax.optimization_barrier((*others, after))
     one, two, three = others
     turned = jnp.stack([three, two, one, v, three, two, one])
     return lax.dynamic_slice_in_dim(turned, 3 - digit, 4, 0)
@@ -255,8 +257,6 @@
         take_kernel, flat, own_block.reshape(1), in_hbm(selected.T), in_hbm(inputs), scalars=1
     )
     arrived = exchange(outgoing.reshape(sent), "exp").reshape(flat.shape)
-    quarter = gather_four(piece, exp_index // 4 % 4, 4)
-
     taken = selected.reshape(exp_count, experts, group_take) - own_block * row_count
     mine = (taken >= 0) & (taken < row_count)
     lower = jnp.min(jnp.where(mine, taken, row_count), axis=2)
@@ -284,6 +284,7 @@
     )
     compact = small_kernel(fill_kernel, chosen_shape, my_place.reshape(-1, 1), arrived)
     chosen = exchange(compact, "ctx")
+    quarter = gather_four(piece, exp_index // 4 % 4, 4, compact)
     layer = jnp.moveaxis(gather_four(quarter, exp_index % 4, 1), 0, 1)
     partials = expert_parts(chosen, gate_weight, up_weight, down_weight)
     parts = exchange(partials, "ctx")
@@ -302,11 +303,11 @@
     normed = (widened * scale_row * norm_gain).astype(jnp.bfloat16)
 
     near = jnp.concatenate(
-        [normed, shift_chip(normed, 1), shift_chip(normed, -1), shift_chip(normed, 2)], axis=0
+        [normed, shift_chip(normed, 2), shift_chip(normed, 1), shift_chip(normed, -1)], axis=0
     )
     far = swap_core(near)
     chip, core = ctx_index // N_CORE, ctx_index % N_CORE
-    steps = jnp.array([0, N_X - 1, 1, 2], jnp.int32)
+    steps = jnp.array([0, 2, N_X - 1, 1], jnp.int32)
     chips = (chip + steps) % N_X
     ids = jnp.concatenate([chips * N_CORE + core, chips * N_CORE + 1 - core])
     near_rows = jnp.dot(near, weight_rows, preferred_element_type=jnp.float32)

time: 184 us -> 172 us (0.935)
  waiting for transfers between devices: 64 us -> 51.6 us
    all_to_all x4, starting transfers between devices: 31.1 us -> 39.9 us  [exchange(): return lax.all_to_all(blocks, axis, split_axis=0, concat_axis=0, tiled=True)]
    ppermute x13, waiting for transfers between devices: 29.5 us -> 21.7 us  [shift(): return lax.ppermute(v, axis, [(i, move(i)) for i in range(count)])]
    ppermute x13, starting transfers between devices: 58.5 us -> 51 us  [shift(): return lax.ppermute(v, axis, [(i, move(i)) for i in range(count)])]
    all_to_all x4, waiting for transfers between devices: 34.5 us -> 29.9 us  [exchange(): return lax.all_to_all(blocks, axis, split_axis=0, concat_axis=0, tiled=True)]
  transfers between devices with their start and end apart: 17 -> 17, of which waited for: 11 -> 10; matrix products, arithmetic and copies ran while one was open for 2% -> 3% of each run, Pallas kernels for 2% -> 1%
where the time goes in v7:
time: 172 us; the launch traced here: 171 us
  starting transfers between devices  90.8 us (53%)
  waiting for transfers between devices  51.6 us (30%)
  Pallas kernels  11.9 us (7%)
  blocking collectives  9.25 us (5%)
  local copies, waits for them, and re-layouts  2.44 us (1%)
  between operations  1.88 us (1%)
  matrix products  1.86 us (1%)
    ppermute x13, starting transfers between devices, shift(): return lax.ppermute(v, axis, [(i, move(i)) for i in range(count)])  51 us
    all_to_all x4, starting transfers between devices, exchange(): return lax.all_to_all(blocks, axis, split_axis=0, concat_axis=0, tiled=True)  39.9 us
    all_to_all x4, waiting for transfers between devices, exchange(): return lax.all_to_all(blocks, axis, split_axis=0, concat_axis=0, tiled=True)  29.9 us
    ppermute x13, waiting for transfers between devices, shift(): return lax.ppermute(v, axis, [(i, move(i)) for i in range(count)])  21.7 us
    all_to_all x1, blocking collectives, exchange(): return lax.all_to_all(blocks, axis, split_axis=0, concat_axis=0, tiled=True)  9.25 us
    pallas_call x4, Pallas kernels, small_kernel(): pl.pallas_call(body, out_shape=outs, in_specs=whole(pltpu.SMEM, scalars)...  5.56 us
    pallas_call x1, Pallas kernels, attention(): pl.pallas_call(attention_kernel, out_shape=jax.ShapeDtypeStruct((chunks,...  3.73 us
  transfers between devices with their start and end apart: 17, of which 10 were waited for; matrix products, arithmetic and copies ran while one was open for 3% of the time, Pallas kernels for 1%

profile of v7, /device:TPU:1, one launch (start us, length us, event | category | flops | bytes accessed | tf_op | source)
XLA Modules:
  0.0 170.7 jit_solution(6496608155201721383)
XLA Ops:
  0.6 0.0 copy-start
  0.7 2.3 %shard_map.131 = bf16[512,512]{1,0:T(8,128)(2,1)} custom-call(s32[1]{0:T(128)} %bitcast.1.block, s32[16,128]{1,0:T(8,128)} %bitcast.57, bf16[128,1024]{1,0:T(8,128)(2,1)} %inputs.1), custom_call_target="tpu_custom_call" | custom-call | tf_op jit(solution)/shard_map/pallas_call | solution.py:55
  3.0 19.4 %all-to-all-start = ((bf16[64,8,512]{2,1,0:T(8,128)(2,1)}), bf16[64,8,512]{2,1,0:T(8,128)(2,1)S(1)}, u32[]{:S(2)}, u32[]{:S(2)}) async-start(bf16[64,8,512]{2,1,0:T(8,128)(2,1)} %bitcast.3), calls=%async_computation | async-start | bytes 1048576 | tf_op jit(solution)/shard_map/all_to_all | solution.py:20
  22.5 0.7 constant_dynamic-slice_fusion.2
  23.2 6.8 %collective-permute-start = (bf16[16,384]{1,0:T(8,128)(2,1)S(1)}, bf16[16,384]{1,0:T(8,128)(2,1)S(1)}, u32[]{:S(2)}, u32[]{:S(2)}) collective-permute-start(bf16[16,384]{1,0:T(8,128)(2,1)S(1)} %pad_maximum_fusion.1), channel_id=1, source_target_pairs={{0,32},{8,40},{16,48},{24,56},{32,64},{40,72},{48,80},{56,88},{64,... | collective-permute-start | bytes 36872 | tf_op jit(solution)/shard_map/ppermute | solution.py:25
  30.0 7.0 %collective-permute-start.1 = (bf16[16,384]{1,0:T(8,128)(2,1)S(1)}, bf16[16,384]{1,0:T(8,128)(2,1)S(1)}, u32[]{:S(2)}, u32[]{:S(2)}) collective-permute-start(bf16[16,384]{1,0:T(8,128)(2,1)S(1)} %pad_maximum_fusion.1), channel_id=1, source_target_pairs={{0,64},{8,72},{16,80},{24,88},{32,96},{40,104},{48,112},{56,120},{... | collective-permute-start | bytes 36872 | tf_op jit(solution)/shard_map/ppermute | solution.py:25
  37.0 7.0 %collective-permute-start.2 = (bf16[16,384]{1,0:T(8,128)(2,1)S(1)}, bf16[16,384]{1,0:T(8,128)(2,1)S(1)}, u32[]{:S(2)}, u32[]{:S(2)}) collective-permute-start(bf16[16,384]{1,0:T(8,128)(2,1)S(1)} %pad_maximum_fusion.1), channel_id=1, source_target_pairs={{0,96},{8,104},{16,112},{24,120},{32,0},{40,8},{48,16},{56,24},{64... | collective-permute-start | bytes 36872 | tf_op jit(solution)/shard_map/ppermute | solution.py:25
  44.0 0.1 constant_dynamic-slice_fusion.5
  44.1 0.1 copy.64
  44.2 0.2 convert_reduce_fusion
  44.4 0.1 add_add_fusion
  44.5 0.1 reshape_reshape.8.place
  44.5 7.2 %all-to-all-done = bf16[64,8,512]{2,1,0:T(8,128)(2,1)S(1)} async-done(((bf16[64,8,512]{2,1,0:T(8,128)(2,1)}), bf16[64,8,512]{2,1,0:T(8,128)(2,1)S(1)}, u32[]{:S(2)}, u32[]{:S(2)}) %all-to-all-start) | async-done | bytes 524320 | tf_op jit(solution)/shard_map/all_to_all | solution.py:20
  51.7 1.2 shard_map.132
  52.9 0.0 collective-permute-done
  52.9 2.3 %collective-permute-done.1 = bf16[16,384]{1,0:T(8,128)(2,1)S(1)} collective-permute-done((bf16[16,384]{1,0:T(8,128)(2,1)S(1)}, bf16[16,384]{1,0:T(8,128)(2,1)S(1)}, u32[]{:S(2)}, u32[]{:S(2)}) %collective-permute-start.1) | collective-permute-done | bytes 12320 | tf_op jit(solution)/shard_map/ppermute | solution.py:25
  55.3 2.3 %collective-permute-start.3 = (bf16[4,16,384]{2,1,0:T(8,128)(2,1)S(1)}, bf16[4,16,384]{2,1,0:T(8,128)(2,1)S(1)}, u32[]{:S(2)}, u32[]{:S(2)}) collective-permute-start(bf16[4,16,384]{2,1,0:T(8,128)(2,1)S(1)} %constant_dynamic-slice_fusion.1), channel_id=1, source_target_pairs={{0,24},{8,0},{16,8},{24,16},{32,56},{40,32},{48,40},{56,48},{64,88... | collective-permute-start | bytes 147464 | tf_op jit(solution)/shard_map/ppermute | solution.py:25
  57.7 0.1 reshape_reshape.6.place
  57.7 0.1 reshape.142.gate
  57.8 7.8 %all-to-all-start.1 = ((bf16[8,32,1024]{2,1,0:T(8,128)(2,1)}), bf16[8,32,1024]{2,1,0:T(8,128)(2,1)S(1)}, u32[]{:S(2)}, u32[]{:S(2)}) async-start(bf16[8,32,1024]{2,1,0:T(8,128)(2,1)} %shard_map.132), calls=%async_computation.1 | async-start | bytes 1048576 | tf_op jit(solution)/shard_map/all_to_all | solution.py:20
  65.7 2.4 %collective-permute-start.4 = (bf16[4,16,384]{2,1,0:T(8,128)(2,1)S(1)}, bf16[4,16,384]{2,1,0:T(8,128)(2,1)S(1)}, u32[]{:S(2)}, u32[]{:S(2)}) collective-permute-start(bf16[4,16,384]{2,1,0:T(8,128)(2,1)S(1)} %constant_dynamic-slice_fusion.1), channel_id=1, source_target_pairs={{0,16},{8,24},{16,0},{24,8},{32,48},{40,56},{48,32},{56,40},{64,80... | collective-permute-start | bytes 147464 | tf_op jit(solution)/shard_map/ppermute | solution.py:25
  68.0 2.5 %collective-permute-start.5 = (bf16[4,16,384]{2,1,0:T(8,128)(2,1)S(1)}, bf16[4,16,384]{2,1,0:T(8,128)(2,1)S(1)}, u32[]{:S(2)}, u32[]{:S(2)}) collective-permute-start(bf16[4,16,384]{2,1,0:T(8,128)(2,1)S(1)} %constant_dynamic-slice_fusion.1), channel_id=1, source_target_pairs={{0,8},{8,16},{16,24},{24,0},{32,40},{40,48},{48,56},{56,32},{64,72... | collective-permute-start | bytes 147464 | tf_op jit(solution)/shard_map/ppermute | solution.py:25
  70.5 0.0 collective-permute-done.3
  70.5 2.4 %collective-permute-done.4 = bf16[4,16,384]{2,1,0:T(8,128)(2,1)S(1)} collective-permute-done((bf16[4,16,384]{2,1,0:T(8,128)(2,1)S(1)}, bf16[4,16,384]{2,1,0:T(8,128)(2,1)S(1)}, u32[]{:S(2)}, u32[]{:S(2)}) %collective-permute-start.4) | collective-permute-done | bytes 49184 | tf_op jit(solution)/shard_map/ppermute | solution.py:25
  73.0 2.0 %collective-permute-done.5 = bf16[4,16,384]{2,1,0:T(8,128)(2,1)S(1)} collective-permute-done((bf16[4,16,384]{2,1,0:T(8,128)(2,1)S(1)}, bf16[4,16,384]{2,1,0:T(8,128)(2,1)S(1)}, u32[]{:S(2)}, u32[]{:S(2)}) %collective-permute-start.5) | collective-permute-done | bytes 49184 | tf_op jit(solution)/shard_map/ppermute | solution.py:25
  75.0 0.0 all-to-all-done.1.chosen
  75.1 2.6 %experts.1 = bf16[8,32,1024]{2,1,0:T(8,128)(2,1)} custom-call(bf16[8,32,1024]{2,1,0:T(8,128)(2,1)S(1)} %all-to-all-done.1.chosen, bf16[2,1024,256]{2,1,0:T(8,128)(2,1)S(1)} %copy-done.1, bf16[2,1024,256]{2,1,0:T(8,128)(2,1)S(1)} %copy-done.2, bf16[2,256,1024]{2,1,0:T(8,128)(2,1)} %down.1), custom_call_target="tpu_custom_call" | custom-call | tf_op jit(solution)/shard_map/experts/pallas_call | solution.py:151
  77.7 5.9 %all-to-all-start.2 = ((bf16[8,32,1024]{2,1,0:T(8,128)(2,1)}), bf16[8,32,1024]{2,1,0:T(8,128)(2,1)S(1)}, u32[]{:S(2)}, u32[]{:S(2)}) async-start(bf16[8,32,1024]{2,1,0:T(8,128)(2,1)} %experts.1), calls=%async_computation.2 | async-start | bytes 1048576 | tf_op jit(solution)/shard_map/all_to_all | solution.py:20
  83.7 0.0 copy-start.8
  83.7 9.3 %all-to-all-done.2.parts = bf16[8,32,1024]{2,1,0:T(8,128)(2,1)S(1)} async-done(((bf16[8,32,1024]{2,1,0:T(8,128)(2,1)}), bf16[8,32,1024]{2,1,0:T(8,128)(2,1)S(1)}, u32[]{:S(2)}, u32[]{:S(2)}) %all-to-all-start.2) | async-done | bytes 524320 | tf_op jit(solution)/shard_map/all_to_all | solution.py:20
  93.0 1.3 shard_map.133
  94.3 6.7 %all-to-all-start.3 = ((bf16[64,8,512]{2,1,0:T(8,128)(2,1)}), bf16[64,8,512]{2,1,0:T(8,128)(2,1)S(1)}, u32[]{:S(2)}, u32[]{:S(2)}) async-start(bf16[64,8,512]{2,1,0:T(8,128)(2,1)} %bitcast.18), calls=%async_computation.3 | async-start | bytes 1048576 | tf_op jit(solution)/shard_map/all_to_all | solution.py:20
  101.0 0.1 reduce_min.12
  101.2 0.1 reduce_max.12
  101.3 0.1 copy.54
  101.4 0.1 copy.53
  101.5 0.1 copy.56
  101.6 0.1 copy.55
  101.8 0.1 add_select_fusion
  101.9 4.3 %collective-permute-start.9 = (bf16[4,4,16,384]{3,2,1,0:T(8,128)(2,1)S(1)}, bf16[4,4,16,384]{3,2,1,0:T(8,128)(2,1)S(1)}, u32[]{:S(2)}, u32[]{:S(2)}) collective-permute-start(bf16[4,4,16,384]{3,2,1,0:T(8,128)(2,1)S(1)} %dynamic-slice_bitcast_fusion), channel_id=1, source_target_pairs={{0,384},{8,392},{16,400},{24,408},{32,416},{40,424},{48,432},{56,4... | collective-permute-start | bytes 589832 | tf_op jit(solution)/shard_map/ppermute | solution.py:25
  106.2 0.1 select_n.99
  107.0 0.1 pad_add_fusion.1.ids
  107.1 2.4 %collective-permute-start.10 = (bf16[4,4,16,384]{3,2,1,0:T(8,128)(2,1)S(1)}, bf16[4,4,16,384]{3,2,1,0:T(8,128)(2,1)S(1)}, u32[]{:S(2)}, u32[]{:S(2)}) collective-permute-start(bf16[4,4,16,384]{3,2,1,0:T(8,128)(2,1)S(1)} %dynamic-slice_bitcast_fusion), channel_id=1, source_target_pairs={{0,256},{8,264},{16,272},{24,280},{32,288},{40,296},{48,304},{56,3... | collective-permute-start | bytes 589832 | tf_op jit(solution)/shard_map/ppermute | solution.py:25
  109.5 2.6 %collective-permute-start.11 = (bf16[4,4,16,384]{3,2,1,0:T(8,128)(2,1)S(1)}, bf16[4,4,16,384]{3,2,1,0:T(8,128)(2,1)S(1)}, u32[]{:S(2)}, u32[]{:S(2)}) collective-permute-start(bf16[4,4,16,384]{3,2,1,0:T(8,128)(2,1)S(1)} %dynamic-slice_bitcast_fusion), channel_id=1, source_target_pairs={{0,128},{8,136},{16,144},{24,152},{32,160},{40,168},{48,176},{56,1... | collective-permute-start | bytes 589832 | tf_op jit(solution)/shard_map/ppermute | solution.py:25
  112.2 4.6 %collective-permute-done.10 = bf16[4,4,16,384]{3,2,1,0:T(8,128)(2,1)S(1)} collective-permute-done((bf16[4,4,16,384]{3,2,1,0:T(8,128)(2,1)S(1)}, bf16[4,4,16,384]{3,2,1,0:T(8,128)(2,1)S(1)}, u32[]{:S(2)}, u32[]{:S(2)}) %collective-permute-start.10) | collective-permute-done | bytes 196640 | tf_op jit(solution)/shard_map/ppermute | solution.py:25
  116.8 0.0 copy-start.6
  116.8 13.5 %all-to-all-done.3 = bf16[64,8,512]{2,1,0:T(8,128)(2,1)S(1)} async-done(((bf16[64,8,512]{2,1,0:T(8,128)(2,1)}), bf16[64,8,512]{2,1,0:T(8,128)(2,1)S(1)}, u32[]{:S(2)}, u32[]{:S(2)}) %all-to-all-start.3) | async-done | bytes 524320 | tf_op jit(solution)/shard_map/all_to_all | solution.py:20
  130.3 0.4 fusion.4
  130.8 0.2 fusion
  131.0 0.1 fusion.2
  131.1 2.8 %collective-permute-start.8 = (bf16[128,1024]{1,0:T(8,128)(2,1)S(1)}, bf16[128,1024]{1,0:T(8,128)(2,1)S(1)}, u32[]{:S(2)}, u32[]{:S(2)}) collective-permute-start(bf16[128,1024]{1,0:T(8,128)(2,1)S(1)} %fusion.2), channel_id=1, source_target_pairs={{0,6},{1,7},{2,0},{3,1},{4,2},{5,3},{6,4},{7,5},{8,14},{9,15},{10,... | collective-permute-start | bytes 786440 | tf_op jit(solution)/shard_map/ppermute | solution.py:25
  133.9 2.5 %collective-permute-start.7 = (bf16[128,1024]{1,0:T(8,128)(2,1)S(1)}, bf16[128,1024]{1,0:T(8,128)(2,1)S(1)}, u32[]{:S(2)}, u32[]{:S(2)}) collective-permute-start(bf16[128,1024]{1,0:T(8,128)(2,1)S(1)} %fusion.2), channel_id=1, source_target_pairs={{0,2},{1,3},{2,4},{3,5},{4,6},{5,7},{6,0},{7,1},{8,10},{9,11},{10,... | collective-permute-start | bytes 786440 | tf_op jit(solution)/shard_map/ppermute | solution.py:25
  136.4 2.6 %collective-permute-start.6 = (bf16[128,1024]{1,0:T(8,128)(2,1)S(1)}, bf16[128,1024]{1,0:T(8,128)(2,1)S(1)}, u32[]{:S(2)}, u32[]{:S(2)}) collective-permute-start(bf16[128,1024]{1,0:T(8,128)(2,1)S(1)} %fusion.2), channel_id=1, source_target_pairs={{0,4},{1,5},{2,6},{3,7},{4,0},{5,1},{6,2},{7,3},{8,12},{9,13},{10,... | collective-permute-start | bytes 786440 | tf_op jit(solution)/shard_map/ppermute | solution.py:25
  139.1 3.2 %collective-permute-done.7 = bf16[128,1024]{1,0:T(8,128)(2,1)S(1)} collective-permute-done((bf16[128,1024]{1,0:T(8,128)(2,1)S(1)}, bf16[128,1024]{1,0:T(8,128)(2,1)S(1)}, u32[]{:S(2)}, u32[]{:S(2)}) %collective-permute-start.7) | collective-permute-done | bytes 262176 | tf_op jit(solution)/shard_map/ppermute | solution.py:25
  142.3 5.9 %collective-permute-done.6 = bf16[128,1024]{1,0:T(8,128)(2,1)S(1)} collective-permute-done((bf16[128,1024]{1,0:T(8,128)(2,1)S(1)}, bf16[128,1024]{1,0:T(8,128)(2,1)S(1)}, u32[]{:S(2)}, u32[]{:S(2)}) %collective-permute-start.6) | collective-permute-done | bytes 262176 | tf_op jit(solution)/shard_map/ppermute | solution.py:25
  148.1 0.1 pad_maximum_fusion
  148.2 5.8 %collective-permute-start.12 = (bf16[512,1024]{1,0:T(8,128)(2,1)S(1)}, bf16[512,1024]{1,0:T(8,128)(2,1)S(1)}, u32[]{:S(2)}, u32[]{:S(2)}) collective-permute-start(bf16[512,1024]{1,0:T(8,128)(2,1)S(1)} %pad_maximum_fusion), channel_id=1, source_target_pairs={{0,1},{1,0},{2,3},{3,2},{4,5},{5,4},{6,7},{7,6},{8,9},{9,8},{10,11... | collective-permute-start | bytes 3145736 | tf_op jit(solution)/shard_map/ppermute | solution.py:25
  154.1 0.1 constant_dynamic-slice_fusion
  154.2 0.7 convolution_convert_fusion.1.near
  154.9 1.3 collective-permute-done.12
  156.3 0.7 convolution_convert_fusion.far
  157.0 3.7 %attention.1 = bf16[8,128,128]{2,1,0:T(8,128)(2,1)S(1)} custom-call(s32[8]{0:T(128)S(1)} %pad_add_fusion.1.ids, s32[1]{0:T(128)S(6)} %copy.83.train, bf16[512,384]{1,0:T(8,128)(2,1)S(1)} %convolution_convert_fusion.1.near, bf16[512,384]{1,0:T(8,128)(2,1)S(1)} %convolution_convert_fusion.far), custom_call_target="tpu_custom_call" | custom-call | tf_op jit(solution)/shard_map/attention/pallas_call | solution.py:207
  160.7 9.2 %all_to_all.25.pieces = bf16[8,128,128]{2,1,0:T(8,128)(2,1)S(1)} all-to-all(bf16[8,128,128]{2,1,0:T(8,128)(2,1)S(1)} %attention.1), channel_id=1, replica_groups=mesh['exp'=64,'ctx'=8] {'ctx'}, dimensions={0} | all-to-all | bytes 524288 | tf_op jit(solution)/shard_map/all_to_all | solution.py:20
  170.0 0.8 shard_map.134
  (55 shorter events, 0.6 us)
Async XLA Ops:
  0.6 21.8 %copy-start = (bf16[16,1024]{1,0:T(8,128)(2,1)S(1)}, bf16[16,1024]{1,0:T(8,128)(2,1)}, u32[]{:S(2)}) copy-start(bf16[16,1024]{1,0:T(8,128)(2,1)} %param.19) | copy-start | bytes 98308
  0.6 43.4 %copy-start.5 = (s32[128,16]{0,1:T(8,128)S(1)}, s32[128,16]{0,1:T(8,128)}, u32[]{:S(2)}) copy-start(s32[128,16]{0,1:T(8,128)} %param.13) | copy-start | bytes 24580
  3.0 54.7 %copy-start.7 = (f32[2,16]{1,0:T(2,128)S(1)}, f32[2,16]{1,0:T(2,128)}, u32[]{:S(2)}) copy-start(f32[2,16]{1,0:T(2,128)} %param.14) | copy-start | bytes 388
  3.0 48.7 %all-to-all-start = ((bf16[64,8,512]{2,1,0:T(8,128)(2,1)}), bf16[64,8,512]{2,1,0:T(8,128)(2,1)S(1)}, u32[]{:S(2)}, u32[]{:S(2)}) async-start(bf16[64,8,512]{2,1,0:T(8,128)(2,1)} %bitcast.3), calls=%async_computation | async-start | bytes 1048576 | tf_op jit(solution)/shard_map/all_to_all | solution.py:20
  23.2 29.7 %collective-permute-start = (bf16[16,384]{1,0:T(8,128)(2,1)S(1)}, bf16[16,384]{1,0:T(8,128)(2,1)S(1)}, u32[]{:S(2)}, u32[]{:S(2)}) collective-permute-start(bf16[16,384]{1,0:T(8,128)(2,1)S(1)} %pad_maximum_fusion.1), channel_id=1, source_target_pairs={{0,32},{8,40},{16,48},{24,56},{32,64},{40,72},{48,80},{56,88},{64,... | collective-permute-start | bytes 36872 | tf_op jit(solution)/shard_map/ppermute | solution.py:25
  30.0 25.2 %collective-permute-start.1 = (bf16[16,384]{1,0:T(8,128)(2,1)S(1)}, bf16[16,384]{1,0:T(8,128)(2,1)S(1)}, u32[]{:S(2)}, u32[]{:S(2)}) collective-permute-start(bf16[16,384]{1,0:T(8,128)(2,1)S(1)} %pad_maximum_fusion.1), channel_id=1, source_target_pairs={{0,64},{8,72},{16,80},{24,88},{32,96},{40,104},{48,112},{56,120},{... | collective-permute-start | bytes 36872 | tf_op jit(solution)/shard_map/ppermute | solution.py:25
  37.0 18.2 %collective-permute-start.2 = (bf16[16,384]{1,0:T(8,128)(2,1)S(1)}, bf16[16,384]{1,0:T(8,128)(2,1)S(1)}, u32[]{:S(2)}, u32[]{:S(2)}) collective-permute-start(bf16[16,384]{1,0:T(8,128)(2,1)S(1)} %pad_maximum_fusion.1), channel_id=1, source_target_pairs={{0,96},{8,104},{16,112},{24,120},{32,0},{40,8},{48,16},{56,24},{64... | collective-permute-start | bytes 36872 | tf_op jit(solution)/shard_map/ppermute | solution.py:25
  51.7 23.3 %copy-start.1 = (bf16[2,1024,256]{2,1,0:T(8,128)(2,1)S(1)}, bf16[2,1024,256]{2,1,0:T(8,128)(2,1)}, u32[]{:S(2)}) copy-start(bf16[2,1024,256]{2,1,0:T(8,128)(2,1)} %gate.1) | copy-start | bytes 3145732
  51.7 23.3 %copy-start.2 = (bf16[2,1024,256]{2,1,0:T(8,128)(2,1)S(1)}, bf16[2,1024,256]{2,1,0:T(8,128)(2,1)}, u32[]{:S(2)}) copy-start(bf16[2,1024,256]{2,1,0:T(8,128)(2,1)} %up.1) | copy-start | bytes 3145732
  55.3 15.2 %collective-permute-start.3 = (bf16[4,16,384]{2,1,0:T(8,128)(2,1)S(1)}, bf16[4,16,384]{2,1,0:T(8,128)(2,1)S(1)}, u32[]{:S(2)}, u32[]{:S(2)}) collective-permute-start(bf16[4,16,384]{2,1,0:T(8,128)(2,1)S(1)} %constant_dynamic-slice_fusion.1), channel_id=1, source_target_pairs={{0,24},{8,0},{16,8},{24,16},{32,56},{40,32},{48,40},{56,48},{64,88... | collective-permute-start | bytes 147464 | tf_op jit(solution)/shard_map/ppermute | solution.py:25
  57.8 17.2 %all-to-all-start.1 = ((bf16[8,32,1024]{2,1,0:T(8,128)(2,1)}), bf16[8,32,1024]{2,1,0:T(8,128)(2,1)S(1)}, u32[]{:S(2)}, u32[]{:S(2)}) async-start(bf16[8,32,1024]{2,1,0:T(8,128)(2,1)} %shard_map.132), calls=%async_computation.1 | async-start | bytes 1048576 | tf_op jit(solution)/shard_map/all_to_all | solution.py:20
  65.7 7.3 %collective-permute-start.4 = (bf16[4,16,384]{2,1,0:T(8,128)(2,1)S(1)}, bf16[4,16,384]{2,1,0:T(8,128)(2,1)S(1)}, u32[]{:S(2)}, u32[]{:S(2)}) collective-permute-start(bf16[4,16,384]{2,1,0:T(8,128)(2,1)S(1)} %constant_dynamic-slice_fusion.1), channel_id=1, source_target_pairs={{0,16},{8,24},{16,0},{24,8},{32,48},{40,56},{48,32},{56,40},{64,80... | collective-permute-start | bytes 147464 | tf_op jit(solution)/shard_map/ppermute | solution.py:25
  68.0 6.9 %collective-permute-start.5 = (bf16[4,16,384]{2,1,0:T(8,128)(2,1)S(1)}, bf16[4,16,384]{2,1,0:T(8,128)(2,1)S(1)}, u32[]{:S(2)}, u32[]{:S(2)}) collective-permute-start(bf16[4,16,384]{2,1,0:T(8,128)(2,1)S(1)} %constant_dynamic-slice_fusion.1), channel_id=1, source_target_pairs={{0,8},{8,16},{16,24},{24,0},{32,40},{40,48},{48,56},{56,32},{64,72... | collective-permute-start | bytes 147464 | tf_op jit(solution)/shard_map/ppermute | solution.py:25
  77.7 15.3 %all-to-all-start.2 = ((bf16[8,32,1024]{2,1,0:T(8,128)(2,1)}), bf16[8,32,1024]{2,1,0:T(8,128)(2,1)S(1)}, u32[]{:S(2)}, u32[]{:S(2)}) async-start(bf16[8,32,1024]{2,1,0:T(8,128)(2,1)} %experts.1), calls=%async_computation.2 | async-start | bytes 1048576 | tf_op jit(solution)/shard_map/all_to_all | solution.py:20
  83.7 18.1 %copy-start.8 = (s32[4]{0:T(128)S(1)}, s32[4]{0:T(128)}, u32[]{:S(2)}) copy-start(s32[4]{0:T(128)} %constant.120.clone) | copy-start | bytes 52
  94.3 36.0 %all-to-all-start.3 = ((bf16[64,8,512]{2,1,0:T(8,128)(2,1)}), bf16[64,8,512]{2,1,0:T(8,128)(2,1)S(1)}, u32[]{:S(2)}, u32[]{:S(2)}) async-start(bf16[64,8,512]{2,1,0:T(8,128)(2,1)} %bitcast.18), calls=%async_computation.3 | async-start | bytes 1048576 | tf_op jit(solution)/shard_map/all_to_all | solution.py:20
  101.9 10.2 %collective-permute-start.9 = (bf16[4,4,16,384]{3,2,1,0:T(8,128)(2,1)S(1)}, bf16[4,4,16,384]{3,2,1,0:T(8,128)(2,1)S(1)}, u32[]{:S(2)}, u32[]{:S(2)}) collective-permute-start(bf16[4,4,16,384]{3,2,1,0:T(8,128)(2,1)S(1)} %dynamic-slice_bitcast_fusion), channel_id=1, source_target_pairs={{0,384},{8,392},{16,400},{24,408},{32,416},{40,424},{48,432},{56,4... | collective-permute-start | bytes 589832 | tf_op jit(solution)/shard_map/ppermute | solution.py:25
  107.1 23.7 %copy-start.4 = (bf16[128,1024]{1,0:T(8,128)(2,1)S(1)}, bf16[128,1024]{1,0:T(8,128)(2,1)}, u32[]{:S(2)}) copy-start(bf16[128,1024]{1,0:T(8,128)(2,1)} %inputs.1) | copy-start | bytes 786436
  107.1 9.7 %collective-permute-start.10 = (bf16[4,4,16,384]{3,2,1,0:T(8,128)(2,1)S(1)}, bf16[4,4,16,384]{3,2,1,0:T(8,128)(2,1)S(1)}, u32[]{:S(2)}, u32[]{:S(2)}) collective-permute-start(bf16[4,4,16,384]{3,2,1,0:T(8,128)(2,1)S(1)} %dynamic-slice_bitcast_fusion), channel_id=1, source_target_pairs={{0,256},{8,264},{16,272},{24,280},{32,288},{40,296},{48,304},{56,3... | collective-permute-start | bytes 589832 | tf_op jit(solution)/shard_map/ppermute | solution.py:25
  109.5 29.5 %collective-permute-start.11 = (bf16[4,4,16,384]{3,2,1,0:T(8,128)(2,1)S(1)}, bf16[4,4,16,384]{3,2,1,0:T(8,128)(2,1)S(1)}, u32[]{:S(2)}, u32[]{:S(2)}) collective-permute-start(bf16[4,4,16,384]{3,2,1,0:T(8,128)(2,1)S(1)} %dynamic-slice_bitcast_fusion), channel_id=1, source_target_pairs={{0,128},{8,136},{16,144},{24,152},{32,160},{40,168},{48,176},{56,1... | collective-permute-start | bytes 589832 | tf_op jit(solution)/shard_map/ppermute | solution.py:25
  116.8 14.2 %copy-start.6 = (f32[1024]{0:T(1024)S(1)}, f32[1024]{0:T(1024)}, u32[]{:S(2)}) copy-start(f32[1024]{0:T(1024)} %param.18) | copy-start | bytes 12292
  131.0 17.3 %copy-start.3 = (bf16[128,1024]{1,0:T(8,128)(2,1)}, bf16[128,1024]{1,0:T(8,128)(2,1)S(1)}, u32[]{:S(2)}) copy-start(bf16[128,1024]{1,0:T(8,128)(2,1)S(1)} %get-tuple-element.15) | copy-start | bytes 786436
  131.1 8.0 %collective-permute-start.8 = (bf16[128,1024]{1,0:T(8,128)(2,1)S(1)}, bf16[128,1024]{1,0:T(8,128)(2,1)S(1)}, u32[]{:S(2)}, u32[]{:S(2)}) collective-permute-start(bf16[128,1024]{1,0:T(8,128)(2,1)S(1)} %fusion.2), channel_id=1, source_target_pairs={{0,6},{1,7},{2,0},{3,1},{4,2},{5,3},{6,4},{7,5},{8,14},{9,15},{10,... | collective-permute-start | bytes 786440 | tf_op jit(solution)/shard_map/ppermute | solution.py:25
  133.9 8.3 %collective-permute-start.7 = (bf16[128,1024]{1,0:T(8,128)(2,1)S(1)}, bf16[128,1024]{1,0:T(8,128)(2,1)S(1)}, u32[]{:S(2)}, u32[]{:S(2)}) collective-permute-start(bf16[128,1024]{1,0:T(8,128)(2,1)S(1)} %fusion.2), channel_id=1, source_target_pairs={{0,2},{1,3},{2,4},{3,5},{4,6},{5,7},{6,0},{7,1},{8,10},{9,11},{10,... | collective-permute-start | bytes 786440 | tf_op jit(solution)/shard_map/ppermute | solution.py:25
  136.4 11.7 %collective-permute-start.6 = (bf16[128,1024]{1,0:T(8,128)(2,1)S(1)}, bf16[128,1024]{1,0:T(8,128)(2,1)S(1)}, u32[]{:S(2)}, u32[]{:S(2)}) collective-permute-start(bf16[128,1024]{1,0:T(8,128)(2,1)S(1)} %fusion.2), channel_id=1, source_target_pairs={{0,4},{1,5},{2,6},{3,7},{4,0},{5,1},{6,2},{7,3},{8,12},{9,13},{10,... | collective-permute-start | bytes 786440 | tf_op jit(solution)/shard_map/ppermute | solution.py:25
  148.2 8.0 %collective-permute-start.12 = (bf16[512,1024]{1,0:T(8,128)(2,1)S(1)}, bf16[512,1024]{1,0:T(8,128)(2,1)S(1)}, u32[]{:S(2)}, u32[]{:S(2)}) collective-permute-start(bf16[512,1024]{1,0:T(8,128)(2,1)S(1)} %pad_maximum_fusion), channel_id=1, source_target_pairs={{0,1},{1,0},{2,3},{3,2},{4,5},{5,4},{6,7},{7,6},{8,9},{9,8},{10,11... | collective-permute-start | bytes 3145736 | tf_op jit(solution)/shard_map/ppermute | solution.py:25
